TPU v7x, 512 devices: a whole 4x8x8 slice. The times are simulated.
512 devices in a mesh: gx: 32 (over y, x), gy: 16 (over z, core).
Axes of the slice: x: 4, y: 8, z: 8, core: 2. Of those that a mesh axis runs over, the one named last changes fastest.
Arguments:
- terminal: float32 [512, 8192], P('gx', 'gy'), may hold values from -15 to 15
- initial_density: float32 [512, 8192], P('gx', 'gy'), may hold values from 0.1 to 1
- density_guess: float32 [2, 512, 8192], P(None, 'gx', 'gy'), may hold values from 0.1 to 1
- diagonal: float32 [512, 8192], P('gx', 'gy'), may hold values from 0.1 to 2
Outputs:
- value_field: float32 [512, 8192], P('gx', 'gy')
- density_field: float32 [512, 8192], P('gx', 'gy')
All inputs are finite; a program needn't handle non-finite values.
Results may differ from a plain program's by a relative error of at most 0.00011.
Values sent between devices are 32-bit elements; how exact they have to be, the bound alone decides.
No kernel may reach another device: no remote copies, remote signals or barrier semaphores. Data moves between devices by JAX's collectives and lax.ppermute only.
A program may use at most 64 MiB of HBM per device.

v0:
```python
import jax
import jax.numpy as jnp
from jax import lax
from jax.sharding import Mesh
from jax.sharding import PartitionSpec as P

LEVELS = 2
STEPS = 3
GX = ("gx_0", "gx_1")
GY = ("gy_0", "gy_1")


inv_step = 0.5
coupling = 0.5


def padded_2(shard, sides, width):
    edges = {}
    for axis, dim in sides:
        peers, length = (lax.axis_size(axis), shard.shape[dim])
        up = [(i, (i + 1) % peers) for i in range(peers - 1)]
        last = lax.slice_in_dim(shard, length - width, length, axis=dim)
        leading = lax.slice_in_dim(shard, 0, width, axis=dim)
        edges[dim] = (
            lax.ppermute(last, axis, up),
            lax.ppermute(leading, axis, [(b, a) for a, b in up]),
        )
    done = []
    for _, dim in sides:
        low, high = edges[dim]
        around = [(width, width) if d in done else (0, 0) for d in range(shard.ndim)]
        shard = jnp.concatenate([jnp.pad(low, around), shard, jnp.pad(high, around)], axis=dim)
        done.append(dim)
    return shard


def copy_for_each(shard, axis):
    copies = jnp.broadcast_to(shard, (lax.axis_size(axis), *shard.shape))
    return lax.all_to_all(copies, axis, split_axis=0, concat_axis=0, tiled=True)


def taken_together(shard, axis):
    return copy_for_each(shard, axis).sum(axis=0)


def by_axis(shard, axes):
    far, near = axes
    nearer = taken_together(shard, near)
    return taken_together(nearer, far)


def together(arrays, axis):
    ends = [0]
    for a in arrays:
        ends.append(ends[-1] + a.size)
    total = by_axis(jnp.concatenate([a.ravel() for a in arrays]), axis)
    return tuple((total[b:e].reshape(a.shape) for a, b, e in zip(arrays, ends, ends[1:])))


def apply_padded(padded, center, diagonal):
    beside = padded[2:, 1:-1] + padded[:-2, 1:-1] + padded[1:-1, 2:] + padded[1:-1, :-2]
    return (inv_step + diagonal) * center + (4.0 * center - beside)


def hamiltonian(padded):
    center = padded[1:-1, 1:-1]
    back_x = center - padded[:-2, 1:-1]
    ahead_x = padded[2:, 1:-1] - center
    back_y = center - padded[1:-1, :-2]
    ahead_y = padded[1:-1, 2:] - center
    return 0.5 * (
        jnp.maximum(back_x, 0.0) ** 2
        + jnp.minimum(ahead_x, 0.0) ** 2
        + jnp.maximum(back_y, 0.0) ** 2
        + jnp.minimum(ahead_y, 0.0) ** 2
    )


def divergence(pad_m, pad_u):
    m_mid = pad_m[1:-1, 1:-1]
    u_mid = pad_u[1:-1, 1:-1]
    speed_ahead = -(pad_u[2:, 1:-1] - u_mid)
    speed_back = -(u_mid - pad_u[:-2, 1:-1])
    flux_ahead = (
        jnp.maximum(speed_ahead, 0.0) * m_mid + jnp.minimum(speed_ahead, 0.0) * pad_m[2:, 1:-1]
    )
    flux_back = (
        jnp.maximum(speed_back, 0.0) * pad_m[:-2, 1:-1] + jnp.minimum(speed_back, 0.0) * m_mid
    )
    total = flux_ahead - flux_back
    speed_ahead = -(pad_u[1:-1, 2:] - u_mid)
    speed_back = -(u_mid - pad_u[1:-1, :-2])
    flux_ahead = (
        jnp.maximum(speed_ahead, 0.0) * m_mid + jnp.minimum(speed_ahead, 0.0) * pad_m[1:-1, 2:]
    )
    flux_back = (
        jnp.maximum(speed_back, 0.0) * pad_m[1:-1, :-2] + jnp.minimum(speed_back, 0.0) * m_mid
    )
    return total + flux_ahead - flux_back


def stencil(field, diagonal):
    padded = padded_2(field, ((GX, 0), (GY, 1)), 1)
    return apply_padded(padded, field, diagonal)


def paired(resid, image):
    return together(
        (jnp.sum(resid * resid), jnp.sum(resid * image)), ("gx_0", ("gx_1", "gy_0", "gy_1"))
    )


def solve(rhs, diagonal):
    answer = jnp.zeros_like(rhs)
    resid = rhs
    image = stencil(resid, diagonal)
    norm_now, product = paired(resid, image)
    alpha = norm_now / product
    direction = resid
    along = image
    for step in range(STEPS):
        answer = answer + alpha * direction
        if step + 1 < STEPS:
            resid = resid - alpha * along
            image = stencil(resid, diagonal)
            norm_next, product = paired(resid, image)
            ratio = norm_next / norm_now
            alpha = norm_next / (product - ratio * norm_next / alpha)
            direction = resid + ratio * direction
            along = image + ratio * along
            norm_now = norm_next
    return answer


def shards(terminal, initial_density, density_guess, diagonal):
    levels = [None] * LEVELS
    kept = [None] * (LEVELS + 1)
    later = terminal
    for level in reversed(range(LEVELS)):
        padded = padded_2(later, ((GX, 0), (GY, 1)), 1)
        kept[level + 1] = padded
        rhs = inv_step * later - hamiltonian(padded) + coupling * density_guess[level]
        later = solve(rhs, diagonal)
        levels[level] = later
    density = initial_density
    for level in range(LEVELS):
        if level == 0:
            both = padded_2(jnp.stack([density, levels[level]]), ((GX, 1), (GY, 2)), 1)
            pad_m = both[0]
            pad_u = both[1]
        else:
            pad_m = padded_2(density, ((GX, 0), (GY, 1)), 1)
            pad_u = kept[level]
        rhs = inv_step * density - divergence(pad_m, pad_u)
        density = solve(rhs, diagonal)
    return (levels[0], density)


def solution(mesh):
    torus = Mesh(mesh.devices.reshape(8, 4, 8, 2), ("gx_0", "gx_1", "gy_0", "gy_1"))
    in_specs = (P(GX, GY), P(GX, GY), P(None, GX, GY), P(GX, GY))
    out_specs = (P(GX, GY), P(GX, GY))
    return jax.shard_map(
        shards, mesh=torus, in_specs=in_specs, out_specs=out_specs, check_vma=False
    )
```

profile of v0, /device:TPU:1, one launch (start us, length us, event | category | flops | bytes accessed | tf_op | source)
XLA Modules:
  0.0 636.1 jit_solution(2204022311446060917)
XLA Ops:
  32.3 28.8 %all_to_all.144 = f32[64,1,2]{2,1,0:T(1,128)S(1)} all-to-all(f32[64,1,2]{2,1,0:T(1,128)S(1)} %broadcast_in_dim.72), channel_id=1, replica_groups=mesh['gx_0'=8,'gx_1'=4,'gy_0'=8,'gy_1'=2] {'gx_1','gy_0','gy_1'}, dimensions={0} | all-to-all | bytes 1024 | tf_op jit(solution)/shard_map/all_to_all | solution.py:39
  61.2 15.8 %all_to_all.145 = f32[8,1,2]{2,1,0:T(1,128)S(1)} all-to-all(f32[8,1,2]{2,1,0:T(1,128)S(1)} %broadcast_in_dim.73), channel_id=1, replica_groups=mesh['gx_0'=8,'gx_1'=4,'gy_0'=8,'gy_1'=2] {'gx_0'}, dimensions={0} | all-to-all | bytes 128 | tf_op jit(solution)/shard_map/all_to_all | solution.py:39
  92.0 17.9 %all_to_all.146 = f32[64,1,2]{2,1,0:T(1,128)S(1)} all-to-all(f32[64,1,2]{2,1,0:T(1,128)S(1)} %broadcast_in_dim.74), channel_id=1, replica_groups=mesh['gx_0'=8,'gx_1'=4,'gy_0'=8,'gy_1'=2] {'gx_1','gy_0','gy_1'}, dimensions={0} | all-to-all | bytes 1024 | tf_op jit(solution)/shard_map/all_to_all | solution.py:39
  110.0 10.3 %all_to_all.147 = f32[8,1,2]{2,1,0:T(1,128)S(1)} all-to-all(f32[8,1,2]{2,1,0:T(1,128)S(1)} %broadcast_in_dim.75), channel_id=1, replica_groups=mesh['gx_0'=8,'gx_1'=4,'gy_0'=8,'gy_1'=2] {'gx_0'}, dimensions={0} | all-to-all | bytes 128 | tf_op jit(solution)/shard_map/all_to_all | solution.py:39
  138.6 17.9 %all_to_all.148 = f32[64,1,2]{2,1,0:T(1,128)S(1)} all-to-all(f32[64,1,2]{2,1,0:T(1,128)S(1)} %broadcast_in_dim.76), channel_id=1, replica_groups=mesh['gx_0'=8,'gx_1'=4,'gy_0'=8,'gy_1'=2] {'gx_1','gy_0','gy_1'}, dimensions={0} | all-to-all | bytes 1024 | tf_op jit(solution)/shard_map/all_to_all | solution.py:39
  156.6 10.3 %all_to_all.149 = f32[8,1,2]{2,1,0:T(1,128)S(1)} all-to-all(f32[8,1,2]{2,1,0:T(1,128)S(1)} %broadcast_in_dim.77), channel_id=1, replica_groups=mesh['gx_0'=8,'gx_1'=4,'gy_0'=8,'gy_1'=2] {'gx_0'}, dimensions={0} | all-to-all | bytes 128 | tf_op jit(solution)/shard_map/all_to_all | solution.py:39
  198.7 21.7 %all_to_all.150 = f32[64,1,2]{2,1,0:T(1,128)S(1)} all-to-all(f32[64,1,2]{2,1,0:T(1,128)S(1)} %broadcast_in_dim.78), channel_id=1, replica_groups=mesh['gx_0'=8,'gx_1'=4,'gy_0'=8,'gy_1'=2] {'gx_1','gy_0','gy_1'}, dimensions={0} | all-to-all | bytes 1024 | tf_op jit(solution)/shard_map/all_to_all | solution.py:39
  220.5 10.1 %all_to_all.151 = f32[8,1,2]{2,1,0:T(1,128)S(1)} all-to-all(f32[8,1,2]{2,1,0:T(1,128)S(1)} %broadcast_in_dim.79), channel_id=1, replica_groups=mesh['gx_0'=8,'gx_1'=4,'gy_0'=8,'gy_1'=2] {'gx_0'}, dimensions={0} | all-to-all | bytes 128 | tf_op jit(solution)/shard_map/all_to_all | solution.py:39
  245.7 17.9 %all_to_all.152 = f32[64,1,2]{2,1,0:T(1,128)S(1)} all-to-all(f32[64,1,2]{2,1,0:T(1,128)S(1)} %broadcast_in_dim.80), channel_id=1, replica_groups=mesh['gx_0'=8,'gx_1'=4,'gy_0'=8,'gy_1'=2] {'gx_1','gy_0','gy_1'}, dimensions={0} | all-to-all | bytes 1024 | tf_op jit(solution)/shard_map/all_to_all | solution.py:39
  263.6 10.3 %all_to_all.153 = f32[8,1,2]{2,1,0:T(1,128)S(1)} all-to-all(f32[8,1,2]{2,1,0:T(1,128)S(1)} %broadcast_in_dim.81), channel_id=1, replica_groups=mesh['gx_0'=8,'gx_1'=4,'gy_0'=8,'gy_1'=2] {'gx_0'}, dimensions={0} | all-to-all | bytes 128 | tf_op jit(solution)/shard_map/all_to_all | solution.py:39
  292.3 17.9 %all_to_all.154 = f32[64,1,2]{2,1,0:T(1,128)S(1)} all-to-all(f32[64,1,2]{2,1,0:T(1,128)S(1)} %broadcast_in_dim.82), channel_id=1, replica_groups=mesh['gx_0'=8,'gx_1'=4,'gy_0'=8,'gy_1'=2] {'gx_1','gy_0','gy_1'}, dimensions={0} | all-to-all | bytes 1024 | tf_op jit(solution)/shard_map/all_to_all | solution.py:39
  310.2 10.3 %all_to_all.155 = f32[8,1,2]{2,1,0:T(1,128)S(1)} all-to-all(f32[8,1,2]{2,1,0:T(1,128)S(1)} %broadcast_in_dim.83), channel_id=1, replica_groups=mesh['gx_0'=8,'gx_1'=4,'gy_0'=8,'gy_1'=2] {'gx_0'}, dimensions={0} | all-to-all | bytes 128 | tf_op jit(solution)/shard_map/all_to_all | solution.py:39
  353.5 22.2 %all_to_all.156 = f32[64,1,2]{2,1,0:T(1,128)S(1)} all-to-all(f32[64,1,2]{2,1,0:T(1,128)S(1)} %broadcast_in_dim.84), channel_id=1, replica_groups=mesh['gx_0'=8,'gx_1'=4,'gy_0'=8,'gy_1'=2] {'gx_1','gy_0','gy_1'}, dimensions={0} | all-to-all | bytes 1024 | tf_op jit(solution)/shard_map/all_to_all | solution.py:39
  375.8 11.5 %all_to_all.157 = f32[8,1,2]{2,1,0:T(1,128)S(1)} all-to-all(f32[8,1,2]{2,1,0:T(1,128)S(1)} %broadcast_in_dim.85), channel_id=1, replica_groups=mesh['gx_0'=8,'gx_1'=4,'gy_0'=8,'gy_1'=2] {'gx_0'}, dimensions={0} | all-to-all | bytes 128 | tf_op jit(solution)/shard_map/all_to_all | solution.py:39
  402.4 17.9 %all_to_all.158 = f32[64,1,2]{2,1,0:T(1,128)S(1)} all-to-all(f32[64,1,2]{2,1,0:T(1,128)S(1)} %broadcast_in_dim.86), channel_id=1, replica_groups=mesh['gx_0'=8,'gx_1'=4,'gy_0'=8,'gy_1'=2] {'gx_1','gy_0','gy_1'}, dimensions={0} | all-to-all | bytes 1024 | tf_op jit(solution)/shard_map/all_to_all | solution.py:39
  420.3 10.3 %all_to_all.159 = f32[8,1,2]{2,1,0:T(1,128)S(1)} all-to-all(f32[8,1,2]{2,1,0:T(1,128)S(1)} %broadcast_in_dim.87), channel_id=1, replica_groups=mesh['gx_0'=8,'gx_1'=4,'gy_0'=8,'gy_1'=2] {'gx_0'}, dimensions={0} | all-to-all | bytes 128 | tf_op jit(solution)/shard_map/all_to_all | solution.py:39
  449.0 17.9 %all_to_all.160 = f32[64,1,2]{2,1,0:T(1,128)S(1)} all-to-all(f32[64,1,2]{2,1,0:T(1,128)S(1)} %broadcast_in_dim.88), channel_id=1, replica_groups=mesh['gx_0'=8,'gx_1'=4,'gy_0'=8,'gy_1'=2] {'gx_1','gy_0','gy_1'}, dimensions={0} | all-to-all | bytes 1024 | tf_op jit(solution)/shard_map/all_to_all | solution.py:39
  467.0 10.3 %all_to_all.161 = f32[8,1,2]{2,1,0:T(1,128)S(1)} all-to-all(f32[8,1,2]{2,1,0:T(1,128)S(1)} %broadcast_in_dim.89), channel_id=1, replica_groups=mesh['gx_0'=8,'gx_1'=4,'gy_0'=8,'gy_1'=2] {'gx_0'}, dimensions={0} | all-to-all | bytes 128 | tf_op jit(solution)/shard_map/all_to_all | solution.py:39
  508.0 21.0 %all_to_all.162 = f32[64,1,2]{2,1,0:T(1,128)S(1)} all-to-all(f32[64,1,2]{2,1,0:T(1,128)S(1)} %broadcast_in_dim.90), channel_id=1, replica_groups=mesh['gx_0'=8,'gx_1'=4,'gy_0'=8,'gy_1'=2] {'gx_1','gy_0','gy_1'}, dimensions={0} | all-to-all | bytes 1024 | tf_op jit(solution)/shard_map/all_to_all | solution.py:39
  529.1 11.8 %all_to_all.163 = f32[8,1,2]{2,1,0:T(1,128)S(1)} all-to-all(f32[8,1,2]{2,1,0:T(1,128)S(1)} %broadcast_in_dim.91), channel_id=1, replica_groups=mesh['gx_0'=8,'gx_1'=4,'gy_0'=8,'gy_1'=2] {'gx_0'}, dimensions={0} | all-to-all | bytes 128 | tf_op jit(solution)/shard_map/all_to_all | solution.py:39
  556.0 17.9 %all_to_all.164 = f32[64,1,2]{2,1,0:T(1,128)S(1)} all-to-all(f32[64,1,2]{2,1,0:T(1,128)S(1)} %broadcast_in_dim.92), channel_id=1, replica_groups=mesh['gx_0'=8,'gx_1'=4,'gy_0'=8,'gy_1'=2] {'gx_1','gy_0','gy_1'}, dimensions={0} | all-to-all | bytes 1024 | tf_op jit(solution)/shard_map/all_to_all | solution.py:39
  573.9 10.3 %all_to_all.165 = f32[8,1,2]{2,1,0:T(1,128)S(1)} all-to-all(f32[8,1,2]{2,1,0:T(1,128)S(1)} %broadcast_in_dim.93), channel_id=1, replica_groups=mesh['gx_0'=8,'gx_1'=4,'gy_0'=8,'gy_1'=2] {'gx_0'}, dimensions={0} | all-to-all | bytes 128 | tf_op jit(solution)/shard_map/all_to_all | solution.py:39
  602.6 17.9 %all_to_all.166 = f32[64,1,2]{2,1,0:T(1,128)S(1)} all-to-all(f32[64,1,2]{2,1,0:T(1,128)S(1)} %broadcast_in_dim.94), channel_id=1, replica_groups=mesh['gx_0'=8,'gx_1'=4,'gy_0'=8,'gy_1'=2] {'gx_1','gy_0','gy_1'}, dimensions={0} | all-to-all | bytes 1024 | tf_op jit(solution)/shard_map/all_to_all | solution.py:39
  620.6 10.3 %all_to_all.167 = f32[8,1,2]{2,1,0:T(1,128)S(1)} all-to-all(f32[8,1,2]{2,1,0:T(1,128)S(1)} %broadcast_in_dim.95), channel_id=1, replica_groups=mesh['gx_0'=8,'gx_1'=4,'gy_0'=8,'gy_1'=2] {'gx_0'}, dimensions={0} | all-to-all | bytes 128 | tf_op jit(solution)/shard_map/all_to_all | solution.py:39
  (272 shorter events, 227.8 us)
Async XLA Ops:
  1.4 15.8 %collective-permute-start = (f32[1,512]{1,0:T(1,128)S(1)}, f32[1,512]{1,0:T(1,128)S(1)}, u32[]{:S(2)}, u32[]{:S(2)}) collective-permute-start(f32[1,512]{1,0:T(1,128)S(1)} %get-tuple-element.94), channel_id=1, source_target_pairs={{0,16},{16,32},{32,48},{48,64},{64,80},{80,96},{96,112},{112,128},... | collective-permute-start | bytes 6152 | tf_op jit(solution)/shard_map/ppermute | solution.py:25
  5.4 11.9 %collective-permute-start.1 = (f32[1,512]{1,0:T(1,128)S(1)}, f32[1,512]{1,0:T(1,128)S(1)}, u32[]{:S(2)}, u32[]{:S(2)}) collective-permute-start(f32[1,512]{1,0:T(1,128)S(1)} %get-tuple-element.95), channel_id=1, source_target_pairs={{16,0},{32,16},{48,32},{64,48},{80,64},{96,80},{112,96},{128,112},... | collective-permute-start | bytes 6152 | tf_op jit(solution)/shard_map/ppermute | solution.py:26
  18.2 12.0 %collective-permute-start.5 = (f32[1,512]{1,0:T(1,128)S(1)}, f32[1,512]{1,0:T(1,128)S(1)}, u32[]{:S(2)}, u32[]{:S(2)}) collective-permute-start(f32[1,512]{1,0:T(1,128)S(1)} %get-tuple-element.90), channel_id=1, source_target_pairs={{0,16},{16,32},{32,48},{48,64},{64,80},{80,96},{96,112},{112,128},... | collective-permute-start | bytes 6152 | tf_op jit(solution)/shard_map/ppermute | solution.py:25
  78.9 11.0 %collective-permute-start.9 = (f32[1,512]{1,0:T(1,128)S(1)}, f32[1,512]{1,0:T(1,128)S(1)}, u32[]{:S(2)}, u32[]{:S(2)}) collective-permute-start(f32[1,512]{1,0:T(1,128)S(1)} %get-tuple-element.86), channel_id=1, source_target_pairs={{0,16},{16,32},{32,48},{48,64},{64,80},{80,96},{96,112},{112,128},... | collective-permute-start | bytes 6152 | tf_op jit(solution)/shard_map/ppermute | solution.py:25
  125.5 11.0 %collective-permute-start.13 = (f32[1,512]{1,0:T(1,128)S(1)}, f32[1,512]{1,0:T(1,128)S(1)}, u32[]{:S(2)}, u32[]{:S(2)}) collective-permute-start(f32[1,512]{1,0:T(1,128)S(1)} %get-tuple-element.82), channel_id=1, source_target_pairs={{0,16},{16,32},{32,48},{48,64},{64,80},{80,96},{96,112},{112,128},... | collective-permute-start | bytes 6152 | tf_op jit(solution)/shard_map/ppermute | solution.py:25
  127.8 8.7 %collective-permute-start.12 = (f32[1,512]{1,0:T(1,128)S(1)}, f32[1,512]{1,0:T(1,128)S(1)}, u32[]{:S(2)}, u32[]{:S(2)}) collective-permute-start(f32[1,512]{1,0:T(1,128)S(1)} %get-tuple-element.83), channel_id=1, source_target_pairs={{16,0},{32,16},{48,32},{64,48},{80,64},{96,80},{112,96},{128,112},... | collective-permute-start | bytes 6152 | tf_op jit(solution)/shard_map/ppermute | solution.py:26
  171.3 15.1 %collective-permute-start.17 = (f32[1,512]{1,0:T(1,128)S(1)}, f32[1,512]{1,0:T(1,128)S(1)}, u32[]{:S(2)}, u32[]{:S(2)}) collective-permute-start(f32[1,512]{1,0:T(1,128)S(1)} %get-tuple-element.78), channel_id=1, source_target_pairs={{16,0},{32,16},{48,32},{64,48},{80,64},{96,80},{112,96},{128,112},... | collective-permute-start | bytes 6152 | tf_op jit(solution)/shard_map/ppermute | solution.py:26
  172.6 13.8 %collective-permute-start.16 = (f32[1,512]{1,0:T(1,128)S(1)}, f32[1,512]{1,0:T(1,128)S(1)}, u32[]{:S(2)}, u32[]{:S(2)}) collective-permute-start(f32[1,512]{1,0:T(1,128)S(1)} %get-tuple-element.79), channel_id=1, source_target_pairs={{0,16},{16,32},{32,48},{48,64},{64,80},{80,96},{96,112},{112,128},... | collective-permute-start | bytes 6152 | tf_op jit(solution)/shard_map/ppermute | solution.py:25
  186.6 10.0 %collective-permute-start.21 = (f32[1,512]{1,0:T(1,128)S(1)}, f32[1,512]{1,0:T(1,128)S(1)}, u32[]{:S(2)}, u32[]{:S(2)}) collective-permute-start(f32[1,512]{1,0:T(1,128)S(1)} %get-tuple-element.74), channel_id=1, source_target_pairs={{0,16},{16,32},{32,48},{48,64},{64,80},{80,96},{96,112},{112,128},... | collective-permute-start | bytes 6152 | tf_op jit(solution)/shard_map/ppermute | solution.py:25
  232.6 11.0 %collective-permute-start.25 = (f32[1,512]{1,0:T(1,128)S(1)}, f32[1,512]{1,0:T(1,128)S(1)}, u32[]{:S(2)}, u32[]{:S(2)}) collective-permute-start(f32[1,512]{1,0:T(1,128)S(1)} %get-tuple-element.70), channel_id=1, source_target_pairs={{0,16},{16,32},{32,48},{48,64},{64,80},{80,96},{96,112},{112,128},... | collective-permute-start | bytes 6152 | tf_op jit(solution)/shard_map/ppermute | solution.py:25
  279.1 11.0 %collective-permute-start.29 = (f32[1,512]{1,0:T(1,128)S(1)}, f32[1,512]{1,0:T(1,128)S(1)}, u32[]{:S(2)}, u32[]{:S(2)}) collective-permute-start(f32[1,512]{1,0:T(1,128)S(1)} %get-tuple-element.66), channel_id=1, source_target_pairs={{0,16},{16,32},{32,48},{48,64},{64,80},{80,96},{96,112},{112,128},... | collective-permute-start | bytes 6152 | tf_op jit(solution)/shard_map/ppermute | solution.py:25
  281.4 8.7 %collective-permute-start.28 = (f32[1,512]{1,0:T(1,128)S(1)}, f32[1,512]{1,0:T(1,128)S(1)}, u32[]{:S(2)}, u32[]{:S(2)}) collective-permute-start(f32[1,512]{1,0:T(1,128)S(1)} %get-tuple-element.67), channel_id=1, source_target_pairs={{16,0},{32,16},{48,32},{64,48},{80,64},{96,80},{112,96},{128,112},... | collective-permute-start | bytes 6152 | tf_op jit(solution)/shard_map/ppermute | solution.py:26
  325.7 13.3 %collective-permute-start.33 = (f32[2,1,512]{2,1,0:T(1,128)S(1)}, f32[2,1,512]{2,1,0:T(1,128)S(1)}, u32[]{:S(2)}, u32[]{:S(2)}) collective-permute-start(f32[2,1,512]{2,1,0:T(1,128)S(1)} %get-tuple-element.32), channel_id=1, source_target_pairs={{0,16},{16,32},{32,48},{48,64},{64,80},{80,96},{96,112},{112,128},... | collective-permute-start | bytes 12296 | tf_op jit(solution)/shard_map/ppermute | solution.py:25
  328.0 11.0 %collective-permute-start.34 = (f32[2,1,512]{2,1,0:T(1,128)S(1)}, f32[2,1,512]{2,1,0:T(1,128)S(1)}, u32[]{:S(2)}, u32[]{:S(2)}) collective-permute-start(f32[2,1,512]{2,1,0:T(1,128)S(1)} %get-tuple-element.33), channel_id=1, source_target_pairs={{16,0},{32,16},{48,32},{64,48},{80,64},{96,80},{112,96},{128,112},... | collective-permute-start | bytes 12296 | tf_op jit(solution)/shard_map/ppermute | solution.py:26
  339.3 12.0 %collective-permute-start.37 = (f32[1,512]{1,0:T(1,128)S(1)}, f32[1,512]{1,0:T(1,128)S(1)}, u32[]{:S(2)}, u32[]{:S(2)}) collective-permute-start(f32[1,512]{1,0:T(1,128)S(1)} %get-tuple-element.62), channel_id=1, source_target_pairs={{0,16},{16,32},{32,48},{48,64},{64,80},{80,96},{96,112},{112,128},... | collective-permute-start | bytes 6152 | tf_op jit(solution)/shard_map/ppermute | solution.py:25
  389.3 11.0 %collective-permute-start.41 = (f32[1,512]{1,0:T(1,128)S(1)}, f32[1,512]{1,0:T(1,128)S(1)}, u32[]{:S(2)}, u32[]{:S(2)}) collective-permute-start(f32[1,512]{1,0:T(1,128)S(1)} %get-tuple-element.58), channel_id=1, source_target_pairs={{0,16},{16,32},{32,48},{48,64},{64,80},{80,96},{96,112},{112,128},... | collective-permute-start | bytes 6152 | tf_op jit(solution)/shard_map/ppermute | solution.py:25
  435.8 11.0 %collective-permute-start.45 = (f32[1,512]{1,0:T(1,128)S(1)}, f32[1,512]{1,0:T(1,128)S(1)}, u32[]{:S(2)}, u32[]{:S(2)}) collective-permute-start(f32[1,512]{1,0:T(1,128)S(1)} %get-tuple-element.54), channel_id=1, source_target_pairs={{0,16},{16,32},{32,48},{48,64},{64,80},{80,96},{96,112},{112,128},... | collective-permute-start | bytes 6152 | tf_op jit(solution)/shard_map/ppermute | solution.py:25
  438.1 8.7 %collective-permute-start.44 = (f32[1,512]{1,0:T(1,128)S(1)}, f32[1,512]{1,0:T(1,128)S(1)}, u32[]{:S(2)}, u32[]{:S(2)}) collective-permute-start(f32[1,512]{1,0:T(1,128)S(1)} %get-tuple-element.55), channel_id=1, source_target_pairs={{16,0},{32,16},{48,32},{64,48},{80,64},{96,80},{112,96},{128,112},... | collective-permute-start | bytes 6152 | tf_op jit(solution)/shard_map/ppermute | solution.py:26
  481.9 11.0 %collective-permute-start.49 = (f32[1,512]{1,0:T(1,128)S(1)}, f32[1,512]{1,0:T(1,128)S(1)}, u32[]{:S(2)}, u32[]{:S(2)}) collective-permute-start(f32[1,512]{1,0:T(1,128)S(1)} %get-tuple-element.50), channel_id=1, source_target_pairs={{0,16},{16,32},{32,48},{48,64},{64,80},{80,96},{96,112},{112,128},... | collective-permute-start | bytes 6152 | tf_op jit(solution)/shard_map/ppermute | solution.py:25
  484.2 8.7 %collective-permute-start.48 = (f32[1,512]{1,0:T(1,128)S(1)}, f32[1,512]{1,0:T(1,128)S(1)}, u32[]{:S(2)}, u32[]{:S(2)}) collective-permute-start(f32[1,512]{1,0:T(1,128)S(1)} %get-tuple-element.51), channel_id=1, source_target_pairs={{16,0},{32,16},{48,32},{64,48},{80,64},{96,80},{112,96},{128,112},... | collective-permute-start | bytes 6152 | tf_op jit(solution)/shard_map/ppermute | solution.py:26
  493.1 12.7 %collective-permute-start.53 = (f32[1,512]{1,0:T(1,128)S(1)}, f32[1,512]{1,0:T(1,128)S(1)}, u32[]{:S(2)}, u32[]{:S(2)}) collective-permute-start(f32[1,512]{1,0:T(1,128)S(1)} %get-tuple-element.46), channel_id=1, source_target_pairs={{0,16},{16,32},{32,48},{48,64},{64,80},{80,96},{96,112},{112,128},... | collective-permute-start | bytes 6152 | tf_op jit(solution)/shard_map/ppermute | solution.py:25
  542.9 11.0 %collective-permute-start.57 = (f32[1,512]{1,0:T(1,128)S(1)}, f32[1,512]{1,0:T(1,128)S(1)}, u32[]{:S(2)}, u32[]{:S(2)}) collective-permute-start(f32[1,512]{1,0:T(1,128)S(1)} %get-tuple-element.42), channel_id=1, source_target_pairs={{0,16},{16,32},{32,48},{48,64},{64,80},{80,96},{96,112},{112,128},... | collective-permute-start | bytes 6152 | tf_op jit(solution)/shard_map/ppermute | solution.py:25
  589.4 11.0 %collective-permute-start.61 = (f32[1,512]{1,0:T(1,128)S(1)}, f32[1,512]{1,0:T(1,128)S(1)}, u32[]{:S(2)}, u32[]{:S(2)}) collective-permute-start(f32[1,512]{1,0:T(1,128)S(1)} %get-tuple-element.38), channel_id=1, source_target_pairs={{0,16},{16,32},{32,48},{48,64},{64,80},{80,96},{96,112},{112,128},... | collective-permute-start | bytes 6152 | tf_op jit(solution)/shard_map/ppermute | solution.py:25
  591.7 8.7 %collective-permute-start.60 = (f32[1,512]{1,0:T(1,128)S(1)}, f32[1,512]{1,0:T(1,128)S(1)}, u32[]{:S(2)}, u32[]{:S(2)}) collective-permute-start(f32[1,512]{1,0:T(1,128)S(1)} %get-tuple-element.39), channel_id=1, source_target_pairs={{16,0},{32,16},{48,32},{64,48},{80,64},{96,80},{112,96},{128,112},... | collective-permute-start | bytes 6152 | tf_op jit(solution)/shard_map/ppermute | solution.py:26
  (45 other events, 287.2 us)
where the time goes:
time: 640 us; the launch traced here: 636 us
  blocking collectives  368 us (58%)
  starting transfers between devices  168 us (26%)
  between operations  40.2 us (6%)
  other arithmetic  29 us (5%)
  waiting for transfers between devices  19.8 us (3%)
  local copies, waits for them, and re-layouts  11.1 us (2%)
    all_to_all x24, blocking collectives, copy_for_each(): return lax.all_to_all(copies, axis, split_axis=0, concat_axis=0, tiled=True)  368 us
    ppermute x32, starting transfers between devices, padded_2(): lax.ppermute(last, axis, up)  94.3 us
    ppermute x32, starting transfers between devices, padded_2(): lax.ppermute(leading, axis, [(b, a) for a, b in up])  73.6 us
    concatenate x12, other arithmetic, together(): total = by_axis(jnp.concatenate([a.ravel() for a in arrays]), axis)  16.3 us
  transfers between devices with their start and end apart: 64, of which 16 were waited for; matrix products, arithmetic and copies ran while one was open for 0% of the time, Pallas kernels for 0%

commit v1 on v0

v1 whole, which is shorter than its diff:
```python
import functools

import jax
import jax.numpy as jnp
from jax import lax
from jax.experimental import pallas as pl
from jax.experimental.pallas import tpu as pltpu
from jax.sharding import Mesh
from jax.sharding import PartitionSpec as P

GX = ("gx_0", "gx_1")
GY = ("gy_0", "gy_1")
FIRST = ("gx_1", "gy_1")
SECOND = ("gx_0", "gy_0")

inv_step = 0.5
coupling = 0.5

LOW = 0.6
HIGH = 10.5
S1 = 2.0
S2 = 6.0
S3 = 4.0
PAIRS = ((0, 0), (0, 1), (0, 2), (1, 1), (1, 2), (2, 2), (2, 3))
MIXED = ((0, 0), (1, 1), (2, 2), (0, 1), (0, 2), (1, 2))

HALF = 64
EDGE = 128


def before(v, dim):
    return pltpu.roll(v, 1, dim)


def after(v, dim):
    return pltpu.roll(v, v.shape[dim] - 1, dim)


def inside(rows, wide, first_row, own, grid):
    nx, ny, local_x, local_y = grid
    row = lax.broadcasted_iota(jnp.int32, (rows, wide), 0) + (lax.axis_index(GX) * local_x + first_row)
    lane = lax.broadcasted_iota(jnp.int32, (rows, wide), 1)
    column = jnp.where(lane < own + HALF, lane, lane - wide) + lax.axis_index(GY) * local_y
    return (row >= 0) & (row < nx) & (column >= 0) & (column < ny)


def shifted(v, center, shift, keep):
    beside = (before(v, 0) + after(v, 0)) + (before(v, 1) + after(v, 1))
    return jnp.where(keep, (center - shift) * v - beside, 0.0)


def basis(v0, center, keep):
    v1 = shifted(v0, center, S1, keep)
    v2 = shifted(v1, center, S2, keep)
    return [v0, v1, v2, shifted(v2, center, S3, keep)]


def hamiltonian(u):
    ahead_x = after(u, 0) - u
    back_x = u - before(u, 0)
    ahead_y = after(u, 1) - u
    back_y = u - before(u, 1)
    return 0.5 * (
        jnp.maximum(back_x, 0.0) ** 2
        + jnp.minimum(ahead_x, 0.0) ** 2
        + jnp.maximum(back_y, 0.0) ** 2
        + jnp.minimum(ahead_y, 0.0) ** 2
    )


def drift(u):
    speed_x = u - after(u, 0)
    speed_y = u - after(u, 1)
    return (
        jnp.maximum(speed_x, 0.0),
        jnp.minimum(speed_x, 0.0),
        jnp.maximum(speed_y, 0.0),
        jnp.minimum(speed_y, 0.0),
    )


def density_rhs(m, speeds, keep):
    out_x, in_x, out_y, in_y = speeds
    flux_x = out_x * m + in_x * after(m, 0)
    flux_y = out_y * m + in_y * after(m, 1)
    div = (flux_x - before(flux_x, 0)) + (flux_y - before(flux_y, 1))
    return jnp.where(keep, inv_step * m - div, 0.0)


def dot(a, b):
    return jnp.sum(jnp.sum(a * b, axis=0, keepdims=True), axis=1, keepdims=True)


def row_of(values):
    lane = lax.broadcasted_iota(jnp.int32, (1, 128), 1)
    row = jnp.zeros((1, 128), jnp.float32)
    for place, value in values:
        row = jnp.where(lane == place, value, row)
    return row


def entry(row, place):
    lane = lax.broadcasted_iota(jnp.int32, row.shape, 1)
    return jnp.sum(jnp.where(lane == place, row, 0.0), axis=1, keepdims=True)


def form(matrix, vector):
    total = None
    for i, a in enumerate(vector):
        for j, b in enumerate(vector[: i + 1]):
            term = a * b * matrix[j][i]
            term = term if i == j else 2.0 * term
            total = term if total is None else total + term
    return total


def alpha_of(squared, energy):
    return jnp.clip(squared / jnp.maximum(energy, 1e-36), 0.999 / HIGH, 1.001 / LOW)


def beta_of(new, old):
    return jnp.clip(new / jnp.maximum(old, 1e-36), 0.0, 1.001 * HIGH / LOW)


def coefficients(products):
    g = dict(zip(PAIRS, products))
    gram = [[g[0, 0], g[0, 1], g[0, 2]], [None, g[1, 1], g[1, 2]], [None, None, g[2, 2]]]
    energy = [
        [g[0, 1] + S1 * g[0, 0], g[1, 1] + S1 * g[0, 1], g[1, 2] + S1 * g[0, 2]],
        [None, g[1, 2] + S2 * g[1, 1], g[2, 2] + S2 * g[1, 2]],
        [None, None, g[2, 3] + S3 * g[2, 2]],
    ]
    norm0 = g[0, 0]
    alpha0 = alpha_of(norm0, energy[0][0])
    resid1 = (1.0 - alpha0 * S1, -alpha0)
    norm1 = jnp.maximum(form(gram, resid1), 0.0)
    beta0 = beta_of(norm1, norm0)
    direct1 = (resid1[0] + beta0, resid1[1])
    alpha1 = alpha_of(norm1, form(energy, direct1))
    resid2 = (
        resid1[0] - alpha1 * (S1 * direct1[0]),
        resid1[1] - alpha1 * (direct1[0] + S2 * direct1[1]),
        -alpha1 * direct1[1],
    )
    norm2 = jnp.maximum(form(gram, resid2), 0.0)
    beta1 = beta_of(norm2, norm1)
    direct2 = (resid2[0] + beta1 * direct1[0], resid2[1] + beta1 * direct1[1], resid2[2])
    alpha2 = alpha_of(norm2, form(energy, direct2))
    return (
        alpha0 + alpha1 * direct1[0] + alpha2 * direct2[0],
        alpha1 * direct1[1] + alpha2 * direct2[1],
        alpha2 * direct2[2],
    )


def combined(coefs, vectors):
    total = coefs[0] * vectors[0]
    for c, v in zip(coefs[1:], vectors[1:]):
        total = total + c * v
    return total


def middle(v, x, own):
    return v[(v.shape[0] - x) // 2 : (v.shape[0] + x) // 2, :own]


def gathered_products(parts_ref):
    parts = parts_ref[...]
    return jnp.sum(parts.reshape(parts.shape[0], 128), axis=0, keepdims=True)


def first_kernel(grid, own_ref, above_ref, below_ref, left_ref, right_ref, basis_ref, fields_ref, sums_ref):
    x, own = own_ref.shape[1:]
    wide = own + EDGE
    keep = inside(3 * x, wide, -x, own, grid)
    half = lax.broadcasted_iota(jnp.int32, (3 * x, EDGE), 1) < HALF

    def extended(k):
        middle_part = jnp.concatenate([above_ref[k], own_ref[k], below_ref[k]], axis=0)
        edge = jnp.where(half, right_ref[k], left_ref[k])
        return jnp.concatenate([middle_part, edge], axis=1)

    later = extended(0)
    center = extended(1) + (inv_step + 4.0)
    rhs = inv_step * later - hamiltonian(later) + coupling * extended(2)
    vs = basis(jnp.where(keep, rhs, 0.0), center, keep)
    for k in range(3):
        basis_ref[k] = vs[k]
    fields_ref[0] = center
    fields_ref[1] = extended(3)
    fields_ref[2] = extended(4)
    mine = [middle(v, x, own) for v in vs]
    sums_ref[...] = row_of([(k, dot(mine[i], mine[j])) for k, (i, j) in enumerate(PAIRS)])


def second_kernel(grid, parts_ref, last_ref, fields_ref, later_ref, basis_ref, sums_ref):
    _, _, x, own = grid
    rows, wide = last_ref.shape[1:]
    keep = inside(rows, wide, -x, own, grid)
    row = gathered_products(parts_ref)
    coefs = coefficients([entry(row, k) for k in range(len(PAIRS))])
    later = combined(coefs, [last_ref[k] for k in range(3)])
    later_ref[...] = later
    rhs = inv_step * later - hamiltonian(later) + coupling * fields_ref[1]
    vs = basis(jnp.where(keep, rhs, 0.0), fields_ref[0], keep)
    for k in range(3):
        basis_ref[k] = vs[k]
    mine = [middle(v, x, own) for v in vs]
    sums_ref[...] = row_of([(k, dot(mine[i], mine[j])) for k, (i, j) in enumerate(PAIRS)])


def third_kernel(grid, parts_ref, last_ref, fields_ref, later_ref, value_ref, images_ref, sums_ref):
    _, _, x, own = grid
    rows, wide = last_ref.shape[1:]
    cut = x // 2
    some = pl.ds(cut, rows - 2 * cut)
    keep = inside(rows - 2 * cut, wide, cut - x, own, grid)
    row = gathered_products(parts_ref)
    coefs = coefficients([entry(row, k) for k in range(len(PAIRS))])
    value = combined(coefs, [last_ref[k, some, :] for k in range(3)])
    value_ref[...] = middle(value, x, own)
    center = fields_ref[0, some, :]
    firsts = basis(density_rhs(fields_ref[2, some, :], drift(value), keep), center, keep)
    mine = [middle(v, x, own) for v in firsts]
    values = [(6 * 8 + k, dot(mine[i], mine[j])) for k, (i, j) in enumerate(PAIRS)]
    speeds = drift(later_ref[some, :])
    images = []
    for v in firsts[:3]:
        chain = basis(density_rhs(v, speeds, keep), center, keep)
        images.append([middle(w, x, own) for w in chain])
    for i in range(3):
        for k in range(3):
            images_ref[3 * i + k] = images[i][k]
    for place, (a, b) in enumerate(MIXED):
        for k, (i, j) in enumerate(PAIRS):
            values.append((8 * place + k, dot(images[a][i], images[b][j])))
    sums_ref[...] = row_of(values)


def fourth_kernel(parts_ref, images_ref, density_ref):
    row = gathered_products(parts_ref)
    first = coefficients([entry(row, 6 * 8 + k) for k in range(len(PAIRS))])
    products = []
    for k in range(len(PAIRS)):
        total = None
        for place, (a, b) in enumerate(MIXED):
            term = first[a] * first[b] * entry(row, 8 * place + k)
            term = term if a == b else 2.0 * term
            total = term if total is None else total + term
        products.append(total)
    second = coefficients(products)
    total = None
    for i in range(3):
        for k in range(3):
            term = (first[i] * second[k]) * images_ref[3 * i + k]
            total = term if total is None else total + term
    density_ref[...] = total


def spread(row, axes):
    size = lax.axis_size(axes)
    copies = jnp.broadcast_to(row, (size, 1, 128))
    return lax.all_to_all(copies, axes, split_axis=0, concat_axis=0, tiled=True)


def everywhere(row):
    nearer = spread(row, FIRST).sum(axis=0)
    return spread(nearer, SECOND)


def neighbours(shard, axis):
    peers = lax.axis_size(axis)
    up = [(i, i + 1) for i in range(peers - 1)]
    return up, [(b, a) for a, b in up]


def call(kernel, out_shape, *args):
    vmem = pl.BlockSpec(memory_space=pltpu.VMEM)
    return pl.pallas_call(
        kernel,
        out_shape=[jax.ShapeDtypeStruct(s, jnp.float32) for s in out_shape],
        in_specs=[vmem] * len(args),
        out_specs=[vmem] * len(out_shape),
    )(*args)


def shards(terminal, initial_density, density_guess, diagonal):
    x, own = terminal.shape
    grid = (x * lax.axis_size(GX), own * lax.axis_size(GY), x, own)
    fields = jnp.stack([terminal, diagonal, density_guess[1], density_guess[0], initial_density])
    up, down = neighbours(fields, GX)
    above = lax.ppermute(fields, GX, up)
    below = lax.ppermute(fields, GX, down)
    tall = [above, fields, below]
    up, down = neighbours(fields, GY)
    left = lax.ppermute(jnp.concatenate([f[:, :, own - EDGE :] for f in tall], axis=1), GY, up)
    right = lax.ppermute(jnp.concatenate([f[:, :, :EDGE] for f in tall], axis=1), GY, down)
    full = (3 * x, own + EDGE)
    basis1, kept, sums = call(
        functools.partial(first_kernel, grid),
        [(3, *full), (3, *full), (1, 128)],
        fields, above, below, left, right,
    )
    later, basis0, sums = call(
        functools.partial(second_kernel, grid),
        [full, (3, *full), (1, 128)],
        everywhere(sums), basis1, kept,
    )
    value, images, sums = call(
        functools.partial(third_kernel, grid),
        [(x, own), (9, x, own), (1, 128)],
        everywhere(sums), basis0, kept, later,
    )
    (density,) = call(fourth_kernel, [(x, own)], everywhere(sums), images)
    return value, density


def solution(mesh):
    torus = Mesh(mesh.devices.reshape(8, 4, 8, 2), ("gx_0", "gx_1", "gy_0", "gy_1"))
    in_specs = (P(GX, GY), P(GX, GY), P(None, GX, GY), P(GX, GY))
    out_specs = (P(GX, GY), P(GX, GY))
    return jax.shard_map(
        shards, mesh=torus, in_specs=in_specs, out_specs=out_specs, check_vma=False
    )
```

time: 640 us -> 125 us (0.20)
  blocking collectives: 368 us -> 88 us
  starting transfers between devices: 168 us -> 16.4 us
  between operations: 40.2 us -> 0.78 us
  other arithmetic: 29 us -> 0.07 us
  waiting for transfers between devices: 19.8 us -> 4.06 us
  Pallas kernels: 0 us -> 9.97 us
    all_to_all x24 -> x6, blocking collectives: 368 us -> 88 us  [spread(): return lax.all_to_all(copies, axes, split_axis=0, concat_axis=0, tiled=True)]
    ppermute x64 -> x4, starting transfers between devices: 168 us -> 16.4 us  [the longest x1 6.27 us: shards(): lax.ppermute(jnp.concatenate([f[:, :, own - EDGE:] for f in tall], axis=1...]
    concatenate x13 -> x2, other arithmetic: 16.4 us -> 0.02 us  [the longest x1 0.01 us: shards(): jnp.concatenate([f[:, :, own - EDGE:] for f in tall], axis=1)]
    ppermute x64 -> x4, waiting for transfers between devices: 19.8 us -> 4.06 us  [the longest x1 1.85 us: shards(): lax.ppermute(jnp.concatenate([f[:, :, :EDGE] for f in tall], axis=1), GY,...]
    reduce_sum x36 -> x3, other arithmetic: 10.2 us -> 0.05 us  [everywhere(): nearer = spread(row, FIRST).sum(axis=0)]
    pallas_call x0 -> x4, Pallas kernels: none -> 9.97 us  [call(): pl.pallas_call(kernel, out_shape=[jax.ShapeDtypeStruct(s, jnp.float32) fo...]
    slice x42 -> x3, local copies, waits for them, and re-layouts: 9.97 us -> 0.02 us  [shards(): f[:, :, :EDGE]]
  transfers between devices with their start and end apart: 64 -> 4, of which waited for: 16 -> 3; matrix products, arithmetic and copies ran while one was open for 0% -> 0% of each run, Pallas kernels for 0% -> 0%
where the time goes in v1:
time: 125 us; the launch traced here: 124 us
  blocking collectives  88 us (70%)
  starting transfers between devices  16.4 us (13%)
  Pallas kernels  9.97 us (8%)
  local copies, waits for them, and re-layouts  4.93 us (4%)
  waiting for transfers between devices  4.06 us (3%)
    all_to_all x6, blocking collectives, spread(): return lax.all_to_all(copies, axes, split_axis=0, concat_axis=0, tiled=True)  88 us
    pallas_call x4, Pallas kernels, call(): pl.pallas_call(kernel, out_shape=[jax.ShapeDtypeStruct(s, jnp.float32) fo...  9.97 us
    ppermute x1, starting transfers between devices, shards(): lax.ppermute(jnp.concatenate([f[:, :, own - EDGE:] for f in tall], axis=1...  6.27 us
    unnamed x26, local copies, waits for them, and re-layouts  4.83 us
    ppermute x1, starting transfers between devices, shards(): above = lax.ppermute(fields, GX, up)  4.57 us
    ppermute x1, starting transfers between devices, shards(): lax.ppermute(jnp.concatenate([f[:, :, :EDGE] for f in tall], axis=1), GY,...  4.32 us
  transfers between devices with their start and end apart: 4, of which 3 were waited for; matrix products, arithmetic and copies ran while one was open for 0% of the time, Pallas kernels for 0%

profile of v1, /device:TPU:1, one launch (start us, length us, event | category | flops | bytes accessed | tf_op | source)
XLA Modules:
  0.0 124.3 jit_solution(7920012312207823879)
XLA Ops:
  0.6 0.8 bitcast_dynamic-update-slice_fusion.2
  1.5 0.7 copy-done.7
  2.3 1.3 %collective-permute-start.1 = (f32[5,16,512]{2,1,0:T(8,128)S(1)}, f32[5,16,512]{2,1,0:T(8,128)S(1)}, u32[]{:S(2)}, u32[]{:S(2)}) collective-permute-start(f32[5,16,512]{2,1,0:T(8,128)S(1)} %bitcast_dynamic-update-slice_fusion.own_ref), channel_id=1, source_target_pairs={{16,0},{32,16},{48,32},{64,48},{80,64},{96,80},{112,96},{128,112},... | collective-permute-start | bytes 491528 | tf_op jit(solution)/shard_map/ppermute | solution.py:293
  3.5 4.6 %collective-permute-start = (f32[5,16,512]{2,1,0:T(8,128)S(1)}, f32[5,16,512]{2,1,0:T(8,128)S(1)}, u32[]{:S(2)}, u32[]{:S(2)}) collective-permute-start(f32[5,16,512]{2,1,0:T(8,128)S(1)} %bitcast_dynamic-update-slice_fusion.own_ref), channel_id=1, source_target_pairs={{0,16},{16,32},{32,48},{48,64},{64,80},{80,96},{96,112},{112,128},... | collective-permute-start | bytes 491528 | tf_op jit(solution)/shard_map/ppermute | solution.py:292
  8.1 0.7 collective-permute-done.1.below_ref
  8.9 1.5 %collective-permute-done.above_ref = f32[5,16,512]{2,1,0:T(8,128)S(1)} collective-permute-done((f32[5,16,512]{2,1,0:T(8,128)S(1)}, f32[5,16,512]{2,1,0:T(8,128)S(1)}, u32[]{:S(2)}, u32[]{:S(2)}) %collective-permute-start) | collective-permute-done | bytes 163872 | tf_op jit(solution)/shard_map/ppermute | solution.py:292
  10.4 0.6 copy-done.2
  11.0 6.3 %collective-permute-start.2 = (f32[5,48,128]{2,1,0:T(8,128)S(1)}, f32[5,48,128]{2,1,0:T(8,128)S(1)}, u32[]{:S(2)}, u32[]{:S(2)}) collective-permute-start(f32[5,48,128]{2,1,0:T(8,128)S(1)} %pad_maximum_fusion), channel_id=1, source_target_pairs={{0,1},{1,2},{2,3},{3,4},{4,5},{5,6},{6,7},{7,8},{8,9},{9,10},{10,1... | collective-permute-start | bytes 368648 | tf_op jit(solution)/shard_map/ppermute | solution.py:296
  17.3 4.3 %collective-permute-start.3 = (f32[5,48,128]{2,1,0:T(8,128)S(1)}, f32[5,48,128]{2,1,0:T(8,128)S(1)}, u32[]{:S(2)}, u32[]{:S(2)}) collective-permute-start(f32[5,48,128]{2,1,0:T(8,128)S(1)} %pad_maximum_fusion.1), channel_id=1, source_target_pairs={{1,0},{2,1},{3,2},{4,3},{5,4},{6,5},{7,6},{8,7},{9,8},{10,9},{11,1... | collective-permute-start | bytes 368648 | tf_op jit(solution)/shard_map/ppermute | solution.py:297
  21.7 1.8 %collective-permute-done.3.right_ref = f32[5,48,128]{2,1,0:T(8,128)S(1)} collective-permute-done((f32[5,48,128]{2,1,0:T(8,128)S(1)}, f32[5,48,128]{2,1,0:T(8,128)S(1)}, u32[]{:S(2)}, u32[]{:S(2)}) %collective-permute-start.3) | collective-permute-done | bytes 122912 | tf_op jit(solution)/shard_map/ppermute | solution.py:297
  23.5 0.6 copy-done.4
  24.2 2.6 %shard_map.59 = (f32[3,48,640]{2,1,0:T(8,128)}, f32[3,48,640]{2,1,0:T(8,128)}, f32[1,128]{1,0:T(1,128)}) custom-call(f32[5,16,512]{2,1,0:T(8,128)} %copy-done, f32[5,16,512]{2,1,0:T(8,128)} %copy-done.2, f32[5,16,512]{2,1,0:T(8,128)} %copy-done.1, f32[5,48,128]{2,1,0:T(8,128)} %copy-done.3, f32[5,48,128]{2,1,0:T(8,128)} %copy-done.4), custom_call_target="tpu_custom_call" | custom-call | tf_op jit(solution)/shard_map/pallas_call | solution.py:279
  26.7 0.7 copy-done.8
  27.4 10.6 %all_to_all.30 = f32[8,1,128]{2,1,0:T(1,128)S(1)} all-to-all(f32[8,1,128]{2,1,0:T(1,128)S(1)} %broadcast_in_dim.18), channel_id=1, replica_groups=mesh['gx_0'=8,'gx_1'=4,'gy_0'=8,'gy_1'=2] {'gx_1','gy_1'}, dimensions={0} | all-to-all | bytes 8192 | tf_op jit(solution)/shard_map/all_to_all | solution.py:263
  38.1 28.8 %all_to_all.31.parts_ref = f32[64,1,128]{2,1,0:T(1,128)} all-to-all(f32[64,1,128]{2,1,0:T(1,128)S(1)} %broadcast_in_dim.19), channel_id=1, replica_groups=mesh['gx_0'=8,'gx_1'=4,'gy_0'=8,'gy_1'=2] {'gx_0','gy_0'}, dimensions={0} | all-to-all | bytes 65536 | tf_op jit(solution)/shard_map/all_to_all | solution.py:263
  66.9 2.5 %shard_map.60 = (f32[48,640]{1,0:T(8,128)}, f32[3,48,640]{2,1,0:T(8,128)}, f32[1,128]{1,0:T(1,128)}) custom-call(f32[64,1,128]{2,1,0:T(1,128)} %all_to_all.31.parts_ref, f32[3,48,640]{2,1,0:T(8,128)} %get-tuple-element.12.last_ref, f32[3,48,640]{2,1,0:T(8,128)} %get-tuple-element.13.fields_ref), custom_call_target="tpu_custom_call" | custom-call | tf_op jit(solution)/shard_map/pallas_call | solution.py:279
  69.4 0.7 copy-done.10
  70.1 9.2 %all_to_all.32 = f32[8,1,128]{2,1,0:T(1,128)S(1)} all-to-all(f32[8,1,128]{2,1,0:T(1,128)S(1)} %broadcast_in_dim.20), channel_id=1, replica_groups=mesh['gx_0'=8,'gx_1'=4,'gy_0'=8,'gy_1'=2] {'gx_1','gy_1'}, dimensions={0} | all-to-all | bytes 8192 | tf_op jit(solution)/shard_map/all_to_all | solution.py:263
  79.3 15.3 %all_to_all.33.parts_ref = f32[64,1,128]{2,1,0:T(1,128)} all-to-all(f32[64,1,128]{2,1,0:T(1,128)S(1)} %broadcast_in_dim.21), channel_id=1, replica_groups=mesh['gx_0'=8,'gx_1'=4,'gy_0'=8,'gy_1'=2] {'gx_0','gy_0'}, dimensions={0} | all-to-all | bytes 65536 | tf_op jit(solution)/shard_map/all_to_all | solution.py:263
  94.7 3.0 %shard_map.61 = (f32[16,512]{1,0:T(8,128)}, f32[9,16,512]{2,1,0:T(8,128)}, f32[1,128]{1,0:T(1,128)}) custom-call(f32[64,1,128]{2,1,0:T(1,128)} %all_to_all.33.parts_ref, f32[3,48,640]{2,1,0:T(8,128)} %get-tuple-element.15.last_ref, f32[3,48,640]{2,1,0:T(8,128)} %get-tuple-element.13.fields_ref, f32[48,640]{1,0:T(8,128)} %get-tuple-element.16.later_ref), custom_call_target="tpu_custom_call" | custom-call | tf_op jit(solution)/shard_map/pallas_call | solution.py:279
  97.7 0.7 copy-done.9
  98.3 8.6 %all_to_all.34 = f32[8,1,128]{2,1,0:T(1,128)S(1)} all-to-all(f32[8,1,128]{2,1,0:T(1,128)S(1)} %broadcast_in_dim.22), channel_id=1, replica_groups=mesh['gx_0'=8,'gx_1'=4,'gy_0'=8,'gy_1'=2] {'gx_1','gy_1'}, dimensions={0} | all-to-all | bytes 8192 | tf_op jit(solution)/shard_map/all_to_all | solution.py:263
  107.0 15.4 %all_to_all.35.parts_ref = f32[64,1,128]{2,1,0:T(1,128)} all-to-all(f32[64,1,128]{2,1,0:T(1,128)S(1)} %broadcast_in_dim.23), channel_id=1, replica_groups=mesh['gx_0'=8,'gx_1'=4,'gy_0'=8,'gy_1'=2] {'gx_0','gy_0'}, dimensions={0} | all-to-all | bytes 65536 | tf_op jit(solution)/shard_map/all_to_all | solution.py:263
  122.4 1.9 %shard_map.62 = f32[16,512]{1,0:T(8,128)} custom-call(f32[64,1,128]{2,1,0:T(1,128)} %all_to_all.35.parts_ref, f32[9,16,512]{2,1,0:T(8,128)} %get-tuple-element.19.images_ref), custom_call_target="tpu_custom_call" | custom-call | tf_op jit(solution)/shard_map/pallas_call | solution.py:279
  (35 shorter events, 0.2 us)
Async XLA Ops:
  0.6 0.8 copy-start.6
  0.6 0.8 copy-start.5
  1.5 0.8 copy-start.7
  2.3 8.1 %copy-start = (f32[5,16,512]{2,1,0:T(8,128)}, f32[5,16,512]{2,1,0:T(8,128)S(1)}, u32[]{:S(2)}) copy-start(f32[5,16,512]{2,1,0:T(8,128)S(1)} %bitcast_dynamic-update-slice_fusion.own_ref) | copy-start | bytes 491524
  2.3 6.6 %collective-permute-start.1 = (f32[5,16,512]{2,1,0:T(8,128)S(1)}, f32[5,16,512]{2,1,0:T(8,128)S(1)}, u32[]{:S(2)}, u32[]{:S(2)}) collective-permute-start(f32[5,16,512]{2,1,0:T(8,128)S(1)} %bitcast_dynamic-update-slice_fusion.own_ref), channel_id=1, source_target_pairs={{16,0},{32,16},{48,32},{64,48},{80,64},{96,80},{112,96},{128,112},... | collective-permute-start | bytes 491528 | tf_op jit(solution)/shard_map/ppermute | solution.py:293
  3.5 6.8 %collective-permute-start = (f32[5,16,512]{2,1,0:T(8,128)S(1)}, f32[5,16,512]{2,1,0:T(8,128)S(1)}, u32[]{:S(2)}, u32[]{:S(2)}) collective-permute-start(f32[5,16,512]{2,1,0:T(8,128)S(1)} %bitcast_dynamic-update-slice_fusion.own_ref), channel_id=1, source_target_pairs={{0,16},{16,32},{32,48},{48,64},{64,80},{80,96},{96,112},{112,128},... | collective-permute-start | bytes 491528 | tf_op jit(solution)/shard_map/ppermute | solution.py:292
  8.9 1.5 %copy-start.1 = (f32[5,16,512]{2,1,0:T(8,128)}, f32[5,16,512]{2,1,0:T(8,128)S(1)}, u32[]{:S(2)}) copy-start(f32[5,16,512]{2,1,0:T(8,128)S(1)} %collective-permute-done.1.below_ref) | copy-start | bytes 491524
  10.4 0.7 copy-start.2
  11.0 10.6 %collective-permute-start.2 = (f32[5,48,128]{2,1,0:T(8,128)S(1)}, f32[5,48,128]{2,1,0:T(8,128)S(1)}, u32[]{:S(2)}, u32[]{:S(2)}) collective-permute-start(f32[5,48,128]{2,1,0:T(8,128)S(1)} %pad_maximum_fusion), channel_id=1, source_target_pairs={{0,1},{1,2},{2,3},{3,4},{4,5},{5,6},{6,7},{7,8},{8,9},{9,10},{10,1... | collective-permute-start | bytes 368648 | tf_op jit(solution)/shard_map/ppermute | solution.py:296
  17.3 6.2 %collective-permute-start.3 = (f32[5,48,128]{2,1,0:T(8,128)S(1)}, f32[5,48,128]{2,1,0:T(8,128)S(1)}, u32[]{:S(2)}, u32[]{:S(2)}) collective-permute-start(f32[5,48,128]{2,1,0:T(8,128)S(1)} %pad_maximum_fusion.1), channel_id=1, source_target_pairs={{1,0},{2,1},{3,2},{4,3},{5,4},{6,5},{7,6},{8,7},{9,8},{10,9},{11,1... | collective-permute-start | bytes 368648 | tf_op jit(solution)/shard_map/ppermute | solution.py:297
  21.7 1.9 %copy-start.3 = (f32[5,48,128]{2,1,0:T(8,128)}, f32[5,48,128]{2,1,0:T(8,128)S(1)}, u32[]{:S(2)}) copy-start(f32[5,48,128]{2,1,0:T(8,128)S(1)} %collective-permute-done.2.left_ref) | copy-start | bytes 368644
  23.5 0.6 copy-start.4
  26.7 0.7 copy-start.8
  69.4 0.7 copy-start.10
  97.7 0.7 copy-start.9

commit v2 on v1

--- a/solution.py
+++ b/solution.py
@@ -10,8 +10,8 @@
 
 GX = ("gx_0", "gx_1")
 GY = ("gy_0", "gy_1")
-FIRST = ("gx_1", "gy_1")
-SECOND = ("gx_0", "gy_0")
+FIRST = ("gx_0", "gy_1")
+SECOND = ("gx_1", "gy_0")
 
 inv_step = 0.5
 coupling = 0.5
@@ -26,6 +26,7 @@
 
 HALF = 64
 EDGE = 128
+TERMINAL, DIAGONAL, GUESS, INITIAL = 0, 1, 2, 4
 
 
 def before(v, dim):
@@ -169,26 +170,37 @@
     return jnp.sum(parts.reshape(parts.shape[0], 128), axis=0, keepdims=True)
 
 
-def first_kernel(grid, own_ref, above_ref, below_ref, left_ref, right_ref, basis_ref, fields_ref, sums_ref):
+def stack_kernel(terminal, diagonal, guess, initial, fields_ref, sems):
+    copies = [
+        pltpu.make_async_copy(terminal, fields_ref.at[TERMINAL], sems.at[0]),
+        pltpu.make_async_copy(diagonal, fields_ref.at[DIAGONAL], sems.at[1]),
+        pltpu.make_async_copy(guess, fields_ref.at[pl.ds(GUESS, 2)], sems.at[2]),
+        pltpu.make_async_copy(initial, fields_ref.at[INITIAL], sems.at[3]),
+    ]
+    for copy in copies:
+        copy.start()
+    for copy in copies:
+        copy.wait()
+
+
+def first_kernel(grid, own_ref, above_ref, below_ref, own_edge, above_edge, below_edge, basis_ref, fields_ref, sums_ref):
     x, own = own_ref.shape[1:]
     wide = own + EDGE
     keep = inside(3 * x, wide, -x, own, grid)
-    half = lax.broadcasted_iota(jnp.int32, (3 * x, EDGE), 1) < HALF
 
     def extended(k):
-        middle_part = jnp.concatenate([above_ref[k], own_ref[k], below_ref[k]], axis=0)
-        edge = jnp.where(half, right_ref[k], left_ref[k])
-        return jnp.concatenate([middle_part, edge], axis=1)
-
-    later = extended(0)
-    center = extended(1) + (inv_step + 4.0)
-    rhs = inv_step * later - hamiltonian(later) + coupling * extended(2)
+        rows = [(above_ref, above_edge), (own_ref, own_edge), (below_ref, below_edge)]
+        return jnp.concatenate([jnp.concatenate([r[k], e[k]], axis=1) for r, e in rows], axis=0)
+
+    later = extended(TERMINAL)
+    center = extended(DIAGONAL) + (inv_step + 4.0)
+    rhs = inv_step * later - hamiltonian(later) + coupling * extended(GUESS + 1)
     vs = basis(jnp.where(keep, rhs, 0.0), center, keep)
     for k in range(3):
         basis_ref[k] = vs[k]
     fields_ref[0] = center
-    fields_ref[1] = extended(3)
-    fields_ref[2] = extended(4)
+    fields_ref[1] = extended(GUESS)
+    fields_ref[2] = extended(INITIAL)
     mine = [middle(v, x, own) for v in vs]
     sums_ref[...] = row_of([(k, dot(mine[i], mine[j])) for k, (i, j) in enumerate(PAIRS)])
 
@@ -278,28 +290,37 @@
     vmem = pl.BlockSpec(memory_space=pltpu.VMEM)
     return pl.pallas_call(
         kernel,
-        out_shape=[jax.ShapeDtypeStruct(s, jnp.float32) for s in out_shape],
+        out_shape=[pltpu.VMEM(s, jnp.float32) for s in out_shape],
         in_specs=[vmem] * len(args),
         out_specs=[vmem] * len(out_shape),
-    )(*args)
+    )(*[pltpu.with_memory_space_constraint(a, pltpu.VMEM) for a in args])
 
 
 def shards(terminal, initial_density, density_guess, diagonal):
     x, own = terminal.shape
     grid = (x * lax.axis_size(GX), own * lax.axis_size(GY), x, own)
-    fields = jnp.stack([terminal, diagonal, density_guess[1], density_guess[0], initial_density])
-    up, down = neighbours(fields, GX)
-    above = lax.ppermute(fields, GX, up)
-    below = lax.ppermute(fields, GX, down)
-    tall = [above, fields, below]
-    up, down = neighbours(fields, GY)
-    left = lax.ppermute(jnp.concatenate([f[:, :, own - EDGE :] for f in tall], axis=1), GY, up)
-    right = lax.ppermute(jnp.concatenate([f[:, :, :EDGE] for f in tall], axis=1), GY, down)
+    fields = pl.pallas_call(
+        stack_kernel,
+        out_shape=pltpu.VMEM((5, x, own), jnp.float32),
+        in_specs=[pl.BlockSpec(memory_space=pltpu.HBM)] * 4,
+        out_specs=pl.BlockSpec(memory_space=pltpu.VMEM),
+        scratch_shapes=[pltpu.SemaphoreType.DMA((4,))],
+    )(terminal, diagonal, density_guess, initial_density)
+    down, up = neighbours(fields, GX)
+    above = lax.ppermute(fields, GX, down)
+    below = lax.ppermute(fields, GX, up)
+    ahead, back = neighbours(fields, GY)
+    left = lax.ppermute(fields[:, :, own - EDGE :], GY, ahead)
+    right = lax.ppermute(fields[:, :, :EDGE], GY, back)
+    lane = lax.broadcasted_iota(jnp.int32, left.shape, 2)
+    edge = jnp.where(lane < HALF, right, left)
+    above_edge = lax.ppermute(edge, GX, down)
+    below_edge = lax.ppermute(edge, GX, up)
     full = (3 * x, own + EDGE)
     basis1, kept, sums = call(
         functools.partial(first_kernel, grid),
         [(3, *full), (3, *full), (1, 128)],
-        fields, above, below, left, right,
+        fields, above, below, edge, above_edge, below_edge,
     )
     later, basis0, sums = call(
         functools.partial(second_kernel, grid),

time: 125 us -> 119 us (0.952)
  blocking collectives: 88 us -> 77 us
  starting transfers between devices: 16.4 us -> 25 us
  Pallas kernels: 9.97 us -> 3.75 us
  waiting for transfers between devices: 4.06 us -> 9.88 us
  local copies, waits for them, and re-layouts: 4.93 us -> 1.91 us
    all_to_all x6 -> x5, blocking collectives: 88 us -> 77 us  [spread(): return lax.all_to_all(copies, axes, split_axis=0, concat_axis=0, tiled=True)]
    all_to_all x0 -> x1, waiting for transfers between devices: none -> 7.97 us  [spread(): return lax.all_to_all(copies, axes, split_axis=0, concat_axis=0, tiled=True)]
    pallas_call x4 -> x5, Pallas kernels: 9.97 us -> 3.75 us  [the longest x4 2.84 us: call(): pl.pallas_call(kernel, out_shape=[pltpu.VMEM(s, jnp.float32) for s in out...]
    ppermute x4 -> x6, starting transfers between devices: 16.4 us -> 21.2 us  [the longest x1 5.36 us: shards(): left = lax.ppermute(fields[:, :, own - EDGE:], GY, ahead)]
    all_to_all x0 -> x1, starting transfers between devices: none -> 3.83 us  [spread(): return lax.all_to_all(copies, axes, split_axis=0, concat_axis=0, tiled=True)]
    unnamed x26 -> x2, local copies, waits for them, and re-layouts: 4.83 us -> 1.23 us
    ppermute x4 -> x6, waiting for transfers between devices: 4.06 us -> 1.91 us  [the longest x1 1.07 us: shards(): above_edge = lax.ppermute(edge, GX, down)]
  transfers between devices with their start and end apart: 4 -> 7, of which waited for: 3 -> 3; matrix products, arithmetic and copies ran while one was open for 0% -> 1% of each run, Pallas kernels for 0% -> 0%
where the time goes in v2:
time: 119 us; the launch traced here: 118 us
  blocking collectives  77 us (65%)
  starting transfers between devices  25 us (21%)
  waiting for transfers between devices  9.88 us (8%)
  Pallas kernels  3.75 us (3%)
  local copies, waits for them, and re-layouts  1.91 us (2%)
    all_to_all x5, blocking collectives, spread(): return lax.all_to_all(copies, axes, split_axis=0, concat_axis=0, tiled=True)  77 us
    all_to_all x1, waiting for transfers between devices, spread(): return lax.all_to_all(copies, axes, split_axis=0, concat_axis=0, tiled=True)  7.97 us
    ppermute x1, starting transfers between devices, shards(): left = lax.ppermute(fields[:, :, own - EDGE:], GY, ahead)  5.36 us
    ppermute x1, starting transfers between devices, shards(): right = lax.ppermute(fields[:, :, :EDGE], GY, back)  4.66 us
    ppermute x1, starting transfers between devices, shards(): above = lax.ppermute(fields, GX, down)  4.57 us
    ppermute x1, starting transfers between devices, shards(): above_edge = lax.ppermute(edge, GX, down)  3.99 us
    all_to_all x1, starting transfers between devices, spread(): return lax.all_to_all(copies, axes, split_axis=0, concat_axis=0, tiled=True)  3.83 us
    pallas_call x4, Pallas kernels, call(): pl.pallas_call(kernel, out_shape=[pltpu.VMEM(s, jnp.float32) for s in out...  2.84 us
  transfers between devices with their start and end apart: 7, of which 3 were waited for; matrix products, arithmetic and copies ran while one was open for 1% of the time, Pallas kernels for 0%

profile of v2, /device:TPU:1, one launch (start us, length us, event | category | flops | bytes accessed | tf_op | source)
XLA Modules:
  0.0 118.4 jit_solution(13017695478805251182)
XLA Ops:
  0.6 0.9 shard_map.59.own_ref
  1.6 1.3 %collective-permute-start.1 = (f32[5,16,512]{2,1,0:T(8,128)S(1)}, f32[5,16,512]{2,1,0:T(8,128)S(1)}, u32[]{:S(2)}, u32[]{:S(2)}) collective-permute-start(f32[5,16,512]{2,1,0:T(8,128)S(1)} %shard_map.59.own_ref), channel_id=1, source_target_pairs={{16,0},{32,16},{48,32},{64,48},{80,64},{96,80},{112,96},{128,112},... | collective-permute-start | bytes 491528 | tf_op jit(solution)/shard_map/ppermute | solution.py:311
  2.9 4.6 %collective-permute-start = (f32[5,16,512]{2,1,0:T(8,128)S(1)}, f32[5,16,512]{2,1,0:T(8,128)S(1)}, u32[]{:S(2)}, u32[]{:S(2)}) collective-permute-start(f32[5,16,512]{2,1,0:T(8,128)S(1)} %shard_map.59.own_ref), channel_id=1, source_target_pairs={{0,16},{16,32},{32,48},{48,64},{64,80},{80,96},{96,112},{112,128},... | collective-permute-start | bytes 491528 | tf_op jit(solution)/shard_map/ppermute | solution.py:310
  7.4 5.4 %collective-permute-start.3 = (f32[5,16,128]{2,1,0:T(8,128)S(1)}, f32[5,16,128]{2,1,0:T(8,128)S(1)}, u32[]{:S(2)}, u32[]{:S(2)}) collective-permute-start(f32[5,16,128]{2,1,0:T(8,128)S(1)} %get-tuple-element.20), channel_id=1, source_target_pairs={{0,1},{1,2},{2,3},{3,4},{4,5},{5,6},{6,7},{7,8},{8,9},{9,10},{10,1... | collective-permute-start | bytes 122888 | tf_op jit(solution)/shard_map/ppermute | solution.py:313
  12.8 4.7 %collective-permute-start.2 = (f32[5,16,128]{2,1,0:T(8,128)S(1)}, f32[5,16,128]{2,1,0:T(8,128)S(1)}, u32[]{:S(2)}, u32[]{:S(2)}) collective-permute-start(f32[5,16,128]{2,1,0:T(8,128)S(1)} %get-tuple-element.21), channel_id=1, source_target_pairs={{1,0},{2,1},{3,2},{4,3},{5,4},{6,5},{7,6},{8,7},{9,8},{10,9},{11,1... | collective-permute-start | bytes 122888 | tf_op jit(solution)/shard_map/ppermute | solution.py:314
  17.5 0.0 collective-permute-done.3
  17.5 0.8 collective-permute-done.2
  18.3 1.3 %collective-permute-start.5 = (f32[5,16,128]{2,1,0:T(8,128)S(1)}, f32[5,16,128]{2,1,0:T(8,128)S(1)}, u32[]{:S(2)}, u32[]{:S(2)}) collective-permute-start(f32[5,16,128]{2,1,0:T(8,128)S(1)} %broadcast_select_fusion.own_edge), channel_id=1, source_target_pairs={{16,0},{32,16},{48,32},{64,48},{80,64},{96,80},{112,96},{128,112},... | collective-permute-start | bytes 122888 | tf_op jit(solution)/shard_map/ppermute | solution.py:318
  19.6 4.0 %collective-permute-start.4 = (f32[5,16,128]{2,1,0:T(8,128)S(1)}, f32[5,16,128]{2,1,0:T(8,128)S(1)}, u32[]{:S(2)}, u32[]{:S(2)}) collective-permute-start(f32[5,16,128]{2,1,0:T(8,128)S(1)} %broadcast_select_fusion.own_edge), channel_id=1, source_target_pairs={{0,16},{16,32},{32,48},{48,64},{64,80},{80,96},{96,112},{112,128},... | collective-permute-start | bytes 122888 | tf_op jit(solution)/shard_map/ppermute | solution.py:317
  23.6 1.1 collective-permute-done.4.above_edge
  24.7 0.5 shard_map.60
  25.3 23.1 %all_to_all.30 = f32[16,1,128]{2,1,0:T(1,128)S(1)} all-to-all(f32[16,1,128]{2,1,0:T(1,128)S(1)} %broadcast_in_dim.18), channel_id=1, replica_groups=mesh['gx_0'=8,'gx_1'=4,'gy_0'=8,'gy_1'=2] {'gx_0','gy_1'}, dimensions={0} | all-to-all | bytes 16384 | tf_op jit(solution)/shard_map/all_to_all | solution.py:275
  48.5 19.4 %all_to_all.31.parts_ref = f32[32,1,128]{2,1,0:T(1,128)S(1)} all-to-all(f32[32,1,128]{2,1,0:T(1,128)S(1)} %broadcast_in_dim.19), channel_id=1, replica_groups=mesh['gx_0'=8,'gx_1'=4,'gy_0'=8,'gy_1'=2] {'gx_1','gy_0'}, dimensions={0} | all-to-all | bytes 32768 | tf_op jit(solution)/shard_map/all_to_all | solution.py:275
  67.9 0.7 shard_map.61
  68.5 11.6 %all_to_all.32 = f32[16,1,128]{2,1,0:T(1,128)S(1)} all-to-all(f32[16,1,128]{2,1,0:T(1,128)S(1)} %broadcast_in_dim.20), channel_id=1, replica_groups=mesh['gx_0'=8,'gx_1'=4,'gy_0'=8,'gy_1'=2] {'gx_0','gy_1'}, dimensions={0} | all-to-all | bytes 16384 | tf_op jit(solution)/shard_map/all_to_all | solution.py:275
  80.1 11.6 %all_to_all.33.parts_ref = f32[32,1,128]{2,1,0:T(1,128)S(1)} all-to-all(f32[32,1,128]{2,1,0:T(1,128)S(1)} %broadcast_in_dim.21), channel_id=1, replica_groups=mesh['gx_0'=8,'gx_1'=4,'gy_0'=8,'gy_1'=2] {'gx_1','gy_0'}, dimensions={0} | all-to-all | bytes 32768 | tf_op jit(solution)/shard_map/all_to_all | solution.py:275
  91.8 1.3 %shard_map.62 = (f32[16,512]{1,0:T(8,128)S(1)}, f32[9,16,512]{2,1,0:T(8,128)S(1)}, f32[1,128]{1,0:T(1,128)S(1)}) custom-call(f32[32,1,128]{2,1,0:T(1,128)S(1)} %all_to_all.33.parts_ref, f32[3,48,640]{2,1,0:T(8,128)S(1)} %get-tuple-element.15.last_ref, f32[3,48,640]{2,1,0:T(8,128)S(1)} %get-tuple-element.13.fields_ref, f32[48,640]{1,0:T(8,128)S(1)} %get-tuple-element.16.later_ref), custom_call_target="tpu_custom_call" | custom-call | tf_op jit(solution)/shard_map/pallas_call | solution.py:291
  93.1 11.3 %all_to_all.34 = f32[16,1,128]{2,1,0:T(1,128)S(1)} all-to-all(f32[16,1,128]{2,1,0:T(1,128)S(1)} %broadcast_in_dim.22), channel_id=1, replica_groups=mesh['gx_0'=8,'gx_1'=4,'gy_0'=8,'gy_1'=2] {'gx_0','gy_1'}, dimensions={0} | all-to-all | bytes 16384 | tf_op jit(solution)/shard_map/all_to_all | solution.py:275
  104.4 0.6 broadcast_in_dim.23
  105.0 3.8 %all-to-all-start.5 = ((f32[32,1,128]{2,1,0:T(1,128)}), f32[32,1,128]{2,1,0:T(1,128)S(1)}, u32[]{:S(2)}, u32[]{:S(2)}) async-start(f32[32,1,128]{2,1,0:T(1,128)} %broadcast_in_dim.23), calls=%async_computation.5 | async-start | bytes 32768 | tf_op jit(solution)/shard_map/all_to_all | solution.py:275
  108.9 0.6 copy.9
  109.5 8.0 %all-to-all-done.5.parts_ref = f32[32,1,128]{2,1,0:T(1,128)S(1)} async-done(((f32[32,1,128]{2,1,0:T(1,128)}), f32[32,1,128]{2,1,0:T(1,128)S(1)}, u32[]{:S(2)}, u32[]{:S(2)}) %all-to-all-start.5) | async-done | bytes 16416 | tf_op jit(solution)/shard_map/all_to_all | solution.py:275
  117.5 0.3 shard_map.63
  117.8 0.6 copy.10
  (14 shorter events, 0.1 us)
Async XLA Ops:
  1.6 23.2 %collective-permute-start.1 = (f32[5,16,512]{2,1,0:T(8,128)S(1)}, f32[5,16,512]{2,1,0:T(8,128)S(1)}, u32[]{:S(2)}, u32[]{:S(2)}) collective-permute-start(f32[5,16,512]{2,1,0:T(8,128)S(1)} %shard_map.59.own_ref), channel_id=1, source_target_pairs={{16,0},{32,16},{48,32},{64,48},{80,64},{96,80},{112,96},{128,112},... | collective-permute-start | bytes 491528 | tf_op jit(solution)/shard_map/ppermute | solution.py:311
  2.9 21.9 %collective-permute-start = (f32[5,16,512]{2,1,0:T(8,128)S(1)}, f32[5,16,512]{2,1,0:T(8,128)S(1)}, u32[]{:S(2)}, u32[]{:S(2)}) collective-permute-start(f32[5,16,512]{2,1,0:T(8,128)S(1)} %shard_map.59.own_ref), channel_id=1, source_target_pairs={{0,16},{16,32},{32,48},{48,64},{64,80},{80,96},{96,112},{112,128},... | collective-permute-start | bytes 491528 | tf_op jit(solution)/shard_map/ppermute | solution.py:310
  7.4 10.1 %collective-permute-start.3 = (f32[5,16,128]{2,1,0:T(8,128)S(1)}, f32[5,16,128]{2,1,0:T(8,128)S(1)}, u32[]{:S(2)}, u32[]{:S(2)}) collective-permute-start(f32[5,16,128]{2,1,0:T(8,128)S(1)} %get-tuple-element.20), channel_id=1, source_target_pairs={{0,1},{1,2},{2,3},{3,4},{4,5},{5,6},{6,7},{7,8},{8,9},{9,10},{10,1... | collective-permute-start | bytes 122888 | tf_op jit(solution)/shard_map/ppermute | solution.py:313
  12.8 5.5 %collective-permute-start.2 = (f32[5,16,128]{2,1,0:T(8,128)S(1)}, f32[5,16,128]{2,1,0:T(8,128)S(1)}, u32[]{:S(2)}, u32[]{:S(2)}) collective-permute-start(f32[5,16,128]{2,1,0:T(8,128)S(1)} %get-tuple-element.21), channel_id=1, source_target_pairs={{1,0},{2,1},{3,2},{4,3},{5,4},{6,5},{7,6},{8,7},{9,8},{10,9},{11,1... | collective-permute-start | bytes 122888 | tf_op jit(solution)/shard_map/ppermute | solution.py:314
  18.3 5.3 %collective-permute-start.5 = (f32[5,16,128]{2,1,0:T(8,128)S(1)}, f32[5,16,128]{2,1,0:T(8,128)S(1)}, u32[]{:S(2)}, u32[]{:S(2)}) collective-permute-start(f32[5,16,128]{2,1,0:T(8,128)S(1)} %broadcast_select_fusion.own_edge), channel_id=1, source_target_pairs={{16,0},{32,16},{48,32},{64,48},{80,64},{96,80},{112,96},{128,112},... | collective-permute-start | bytes 122888 | tf_op jit(solution)/shard_map/ppermute | solution.py:318
  19.6 5.1 %collective-permute-start.4 = (f32[5,16,128]{2,1,0:T(8,128)S(1)}, f32[5,16,128]{2,1,0:T(8,128)S(1)}, u32[]{:S(2)}, u32[]{:S(2)}) collective-permute-start(f32[5,16,128]{2,1,0:T(8,128)S(1)} %broadcast_select_fusion.own_edge), channel_id=1, source_target_pairs={{0,16},{16,32},{32,48},{48,64},{64,80},{80,96},{96,112},{112,128},... | collective-permute-start | bytes 122888 | tf_op jit(solution)/shard_map/ppermute | solution.py:317
  105.0 12.4 %all-to-all-start.5 = ((f32[32,1,128]{2,1,0:T(1,128)}), f32[32,1,128]{2,1,0:T(1,128)S(1)}, u32[]{:S(2)}, u32[]{:S(2)}) async-start(f32[32,1,128]{2,1,0:T(1,128)} %broadcast_in_dim.23), calls=%async_computation.5 | async-start | bytes 32768 | tf_op jit(solution)/shard_map/all_to_all | solution.py:275

commit v3 on v2

--- a/solution.py
+++ b/solution.py
@@ -27,6 +27,8 @@
 HALF = 64
 EDGE = 128
 TERMINAL, DIAGONAL, GUESS, INITIAL = 0, 1, 2, 4
+FIELDS = 5
+STRIP = 16
 
 
 def before(v, dim):
@@ -170,7 +172,12 @@
     return jnp.sum(parts.reshape(parts.shape[0], 128), axis=0, keepdims=True)
 
 
-def stack_kernel(terminal, diagonal, guess, initial, fields_ref, sems):
+def odd_index(axis, shape):
+    place = lax.rem(lax.axis_index(axis), 2)
+    return (lax.broadcasted_iota(jnp.int32, shape, 0) * 0 + place) == 1
+
+
+def stack_kernel(terminal, diagonal, guess, initial, fields_ref, far_ref, near_ref, sems):
     copies = [
         pltpu.make_async_copy(terminal, fields_ref.at[TERMINAL], sems.at[0]),
         pltpu.make_async_copy(diagonal, fields_ref.at[DIAGONAL], sems.at[1]),
@@ -181,16 +188,75 @@
         copy.start()
     for copy in copies:
         copy.wait()
-
-
-def first_kernel(grid, own_ref, above_ref, below_ref, own_edge, above_edge, below_edge, basis_ref, fields_ref, sums_ref):
+    fields = fields_ref[...]
+    shape = (8, fields.shape[2])
+    row = lax.broadcasted_iota(jnp.int32, shape, 0)
+    first, second = fields[:, :8], fields[:, 8:]
+    top = [first[k] for k in range(FIELDS)] + [
+        jnp.where(row < 5, second[TERMINAL], pltpu.roll(second[DIAGONAL], 5, 0)),
+        jnp.where(row < 4, second[GUESS + 1], pltpu.roll(second[GUESS], 4, 0)),
+    ]
+    bottom = [second[k] for k in range(FIELDS)] + [
+        jnp.where(row >= 3, first[TERMINAL], pltpu.roll(first[DIAGONAL], 3, 0)),
+        jnp.where(row >= 4, first[GUESS + 1], pltpu.roll(first[GUESS], 4, 0)),
+    ]
+    odd = odd_index(GX, shape)
+    for k, (t, b) in enumerate(zip(top, bottom)):
+        far_ref[8 * k : 8 * k + 8, :] = jnp.where(odd, b, t)
+        near_ref[8 * k : 8 * k + 8, :] = jnp.where(odd, t, b)
+
+
+def column_kernel(own_ref, far_ref, near_ref, tall_ref, far_edge, near_edge):
     x, own = own_ref.shape[1:]
+    odd = odd_index(GX, (8, own))
+
+    def tile(k, odd_from, even_from):
+        here = pl.ds(8 * k, 8)
+        return jnp.where(odd, odd_from[here, :], even_from[here, :])
+
+    above = [tile(k, near_ref, far_ref) for k in range(FIELDS + 2)]
+    below = [tile(k, far_ref, near_ref) for k in range(FIELDS + 2)]
+    rest_above = {
+        TERMINAL: above[FIELDS],
+        DIAGONAL: pltpu.roll(above[FIELDS], 5, 0),
+        GUESS + 1: above[FIELDS + 1],
+        GUESS: pltpu.roll(above[FIELDS + 1], 4, 0),
+    }
+    rest_below = {
+        TERMINAL: below[FIELDS],
+        DIAGONAL: pltpu.roll(below[FIELDS], 3, 0),
+        GUESS + 1: below[FIELDS + 1],
+        GUESS: pltpu.roll(below[FIELDS + 1], 4, 0),
+    }
+    nothing = jnp.zeros((8, own), jnp.float32)
+    shape = (3 * x, 128)
+    strip = lax.broadcasted_iota(jnp.int32, shape, 1) // STRIP
+    firsts = lasts = jnp.zeros(shape, jnp.float32)
+    for k in range(FIELDS):
+        parts = [rest_above.get(k, nothing), above[k], own_ref[k], below[k], rest_below.get(k, nothing)]
+        whole = jnp.concatenate(parts, axis=0)
+        tall_ref[k] = whole
+        first, last = whole[:, :128], whole[:, own - 128 :]
+        firsts = jnp.where(strip == k, pltpu.roll(first, STRIP * k, 1) if k else first, firsts)
+        lasts = jnp.where(strip == k, pltpu.roll(last, STRIP * (k + 1), 1), lasts)
+    odd = odd_index(GY, shape)
+    far_edge[...] = jnp.where(odd, lasts, firsts)
+    near_edge[...] = jnp.where(odd, firsts, lasts)
+
+
+def first_kernel(grid, tall_ref, far_edge, near_edge, basis_ref, fields_ref, sums_ref):
+    _, _, x, own = grid
     wide = own + EDGE
     keep = inside(3 * x, wide, -x, own, grid)
+    odd = odd_index(GY, (3 * x, EDGE))
+    left = jnp.where(odd, near_edge[...], far_edge[...])
+    right = jnp.where(odd, far_edge[...], near_edge[...])
+    half = lax.broadcasted_iota(jnp.int32, (3 * x, EDGE), 1) < HALF
 
     def extended(k):
-        rows = [(above_ref, above_edge), (own_ref, own_edge), (below_ref, below_edge)]
-        return jnp.concatenate([jnp.concatenate([r[k], e[k]], axis=1) for r, e in rows], axis=0)
+        from_right = pltpu.roll(right, 128 - STRIP * k, 1) if k else right
+        from_left = pltpu.roll(left, 128 - STRIP * (k + 1), 1)
+        return jnp.concatenate([tall_ref[k], jnp.where(half, from_right, from_left)], axis=1)
 
     later = extended(TERMINAL)
     center = extended(DIAGONAL) + (inv_step + 4.0)
@@ -249,7 +315,8 @@
     sums_ref[...] = row_of(values)
 
 
-def fourth_kernel(parts_ref, images_ref, density_ref):
+def fourth_kernel(parts_ref, images_ref, value_ref, value_out, density_ref):
+    value_out[...] = value_ref[...]
     row = gathered_products(parts_ref)
     first = coefficients([entry(row, 6 * 8 + k) for k in range(len(PAIRS))])
     products = []
@@ -280,17 +347,21 @@
     return spread(nearer, SECOND)
 
 
-def neighbours(shard, axis):
+def swapped(far, near, axis):
     peers = lax.axis_size(axis)
-    up = [(i, i + 1) for i in range(peers - 1)]
-    return up, [(b, a) for a, b in up]
-
-
-def call(kernel, out_shape, *args):
+
+    def swap(array, start):
+        pairs = [(i, i + 1) for i in range(start, peers - 1, 2)]
+        return lax.ppermute(array, axis, pairs + [(b, a) for a, b in pairs])
+
+    return swap(far, 1), swap(near, 0)
+
+
+def call(kernel, out_shape, *args, results=pltpu.VMEM):
     vmem = pl.BlockSpec(memory_space=pltpu.VMEM)
     return pl.pallas_call(
         kernel,
-        out_shape=[pltpu.VMEM(s, jnp.float32) for s in out_shape],
+        out_shape=[results(s, jnp.float32) for s in out_shape],
         in_specs=[vmem] * len(args),
         out_specs=[vmem] * len(out_shape),
     )(*[pltpu.with_memory_space_constraint(a, pltpu.VMEM) for a in args])
@@ -299,28 +370,23 @@
 def shards(terminal, initial_density, density_guess, diagonal):
     x, own = terminal.shape
     grid = (x * lax.axis_size(GX), own * lax.axis_size(GY), x, own)
-    fields = pl.pallas_call(
+    packed = (8 * (FIELDS + 2), own)
+    fields, far, near = pl.pallas_call(
         stack_kernel,
-        out_shape=pltpu.VMEM((5, x, own), jnp.float32),
+        out_shape=[pltpu.VMEM(s, jnp.float32) for s in [(FIELDS, x, own), packed, packed]],
         in_specs=[pl.BlockSpec(memory_space=pltpu.HBM)] * 4,
-        out_specs=pl.BlockSpec(memory_space=pltpu.VMEM),
+        out_specs=[pl.BlockSpec(memory_space=pltpu.VMEM)] * 3,
         scratch_shapes=[pltpu.SemaphoreType.DMA((4,))],
     )(terminal, diagonal, density_guess, initial_density)
-    down, up = neighbours(fields, GX)
-    above = lax.ppermute(fields, GX, down)
-    below = lax.ppermute(fields, GX, up)
-    ahead, back = neighbours(fields, GY)
-    left = lax.ppermute(fields[:, :, own - EDGE :], GY, ahead)
-    right = lax.ppermute(fields[:, :, :EDGE], GY, back)
-    lane = lax.broadcasted_iota(jnp.int32, left.shape, 2)
-    edge = jnp.where(lane < HALF, right, left)
-    above_edge = lax.ppermute(edge, GX, down)
-    below_edge = lax.ppermute(edge, GX, up)
+    strips = (3 * x, 128)
+    tall, far, near = call(
+        column_kernel, [(FIELDS, 3 * x, own), strips, strips], fields, *swapped(far, near, GX)
+    )
     full = (3 * x, own + EDGE)
     basis1, kept, sums = call(
         functools.partial(first_kernel, grid),
         [(3, *full), (3, *full), (1, 128)],
-        fields, above, below, edge, above_edge, below_edge,
+        tall, *swapped(far, near, GY),
     )
     later, basis0, sums = call(
         functools.partial(second_kernel, grid),
@@ -332,8 +398,12 @@
         [(x, own), (9, x, own), (1, 128)],
         everywhere(sums), basis0, kept, later,
     )
-    (density,) = call(fourth_kernel, [(x, own)], everywhere(sums), images)
-    return value, density
+    return tuple(
+        call(
+            fourth_kernel, [(x, own)] * 2, everywhere(sums), images, value,
+            results=jax.ShapeDtypeStruct,
+        )
+    )
 
 
 def solution(mesh):

time: 119 us -> 104 us (0.87)
  starting transfers between devices: 25 us -> 14.8 us
  waiting for transfers between devices: 9.88 us -> 3.31 us
  blocking collectives: 77 us -> 80.2 us
  local copies, waits for them, and re-layouts: 1.91 us -> 0.06 us
    all_to_all x1 -> x0, waiting for transfers between devices: 7.97 us -> none  [spread(): return lax.all_to_all(copies, axes, split_axis=0, concat_axis=0, tiled=True)]
    ppermute x6 -> x4, starting transfers between devices: 21.2 us -> 14.8 us  [swap(): return lax.ppermute(array, axis, pairs + [(b, a) for a, b in pairs])]
    all_to_all x1 -> x0, starting transfers between devices: 3.83 us -> none  [spread(): return lax.all_to_all(copies, axes, split_axis=0, concat_axis=0, tiled=True)]
    all_to_all x5 -> x6, blocking collectives: 77 us -> 80.2 us  [spread(): return lax.all_to_all(copies, axes, split_axis=0, concat_axis=0, tiled=True)]
    ppermute x6 -> x4, waiting for transfers between devices: 1.91 us -> 3.31 us  [swap(): return lax.ppermute(array, axis, pairs + [(b, a) for a, b in pairs])]
    unnamed x2 -> x0, local copies, waits for them, and re-layouts: 1.23 us -> none
    pallas_call x5 -> x6, Pallas kernels: 3.75 us -> 4.52 us  [the longest x5 3.58 us: call(): pl.pallas_call(kernel, out_shape=[results(s, jnp.float32) for s in out_sh...]
  transfers between devices with their start and end apart: 7 -> 4, of which waited for: 3 -> 2; matrix products, arithmetic and copies ran while one was open for 1% -> 0% of each run, Pallas kernels for 0% -> 0%
where the time goes in v3:
time: 104 us
  blocking collectives  80.2 us (77%)
  starting transfers between devices  14.8 us (14%)
  Pallas kernels  4.52 us (4%)
  waiting for transfers between devices  3.31 us (3%)
    all_to_all x6, blocking collectives, spread(): return lax.all_to_all(copies, axes, split_axis=0, concat_axis=0, tiled=True)  80.2 us
    ppermute x4, starting transfers between devices, swap(): return lax.ppermute(array, axis, pairs + [(b, a) for a, b in pairs])  14.8 us
    pallas_call x5, Pallas kernels, call(): pl.pallas_call(kernel, out_shape=[results(s, jnp.float32) for s in out_sh...  3.58 us
    ppermute x4, waiting for transfers between devices, swap(): return lax.ppermute(array, axis, pairs + [(b, a) for a, b in pairs])  3.31 us
  transfers between devices with their start and end apart: 4, of which 2 were waited for; matrix products, arithmetic and copies ran while one was open for 0% of the time, Pallas kernels for 0%

profile of v3, /device:TPU:1, one launch (start us, length us, event | category | flops | bytes accessed | tf_op | source)
XLA Modules:
  0.0 103.7 jit_solution(15399158773579530357)
XLA Ops:
  0.6 0.9 shard_map.59
  1.6 0.7 collective-permute-start
  2.3 6.4 %collective-permute-start.1 = (f32[56,512]{1,0:T(8,128)S(1)}, f32[56,512]{1,0:T(8,128)S(1)}, u32[]{:S(2)}, u32[]{:S(2)}) collective-permute-start(f32[56,512]{1,0:T(8,128)S(1)} %get-tuple-element.19), channel_id=1, source_target_pairs={{0,16},{32,48},{64,80},{96,112},{128,144},{160,176},{192,208},{224... | collective-permute-start | bytes 344072 | tf_op jit(solution)/shard_map/ppermute | solution.py:355
  8.7 0.0 collective-permute-done.far_ref
  8.7 2.2 %collective-permute-done.1.near_ref = f32[56,512]{1,0:T(8,128)S(1)} collective-permute-done((f32[56,512]{1,0:T(8,128)S(1)}, f32[56,512]{1,0:T(8,128)S(1)}, u32[]{:S(2)}, u32[]{:S(2)}) %collective-permute-start.1) | collective-permute-done | bytes 114720 | tf_op jit(solution)/shard_map/ppermute | solution.py:355
  10.8 0.1 shard_map.60
  11.0 5.8 %collective-permute-start.2 = (f32[48,128]{1,0:T(8,128)S(1)}, f32[48,128]{1,0:T(8,128)S(1)}, u32[]{:S(2)}, u32[]{:S(2)}) collective-permute-start(f32[48,128]{1,0:T(8,128)S(1)} %get-tuple-element.21), channel_id=1, source_target_pairs={{1,2},{3,4},{5,6},{7,8},{9,10},{11,12},{13,14},{2,1},{4,3},{6,5},{... | collective-permute-start | bytes 73736 | tf_op jit(solution)/shard_map/ppermute | solution.py:355
  16.8 1.9 %collective-permute-start.3 = (f32[48,128]{1,0:T(8,128)S(1)}, f32[48,128]{1,0:T(8,128)S(1)}, u32[]{:S(2)}, u32[]{:S(2)}) collective-permute-start(f32[48,128]{1,0:T(8,128)S(1)} %get-tuple-element.22), channel_id=1, source_target_pairs={{0,1},{2,3},{4,5},{6,7},{8,9},{10,11},{12,13},{14,15},{1,0},{3,2},... | collective-permute-start | bytes 73736 | tf_op jit(solution)/shard_map/ppermute | solution.py:355
  18.7 0.0 collective-permute-done.2.far_edge
  18.7 1.2 %collective-permute-done.3.near_edge = f32[48,128]{1,0:T(8,128)S(1)} collective-permute-done((f32[48,128]{1,0:T(8,128)S(1)}, f32[48,128]{1,0:T(8,128)S(1)}, u32[]{:S(2)}, u32[]{:S(2)}) %collective-permute-start.3) | collective-permute-done | bytes 24608 | tf_op jit(solution)/shard_map/ppermute | solution.py:355
  19.9 0.6 shard_map.61
  20.4 15.8 %all_to_all.30 = f32[16,1,128]{2,1,0:T(1,128)S(1)} all-to-all(f32[16,1,128]{2,1,0:T(1,128)S(1)} %broadcast_in_dim.18), channel_id=1, replica_groups=mesh['gx_0'=8,'gx_1'=4,'gy_0'=8,'gy_1'=2] {'gx_0','gy_1'}, dimensions={0} | all-to-all | bytes 16384 | tf_op jit(solution)/shard_map/all_to_all | solution.py:342
  36.3 18.3 %all_to_all.31.parts_ref = f32[32,1,128]{2,1,0:T(1,128)S(1)} all-to-all(f32[32,1,128]{2,1,0:T(1,128)S(1)} %broadcast_in_dim.19), channel_id=1, replica_groups=mesh['gx_0'=8,'gx_1'=4,'gy_0'=8,'gy_1'=2] {'gx_1','gy_0'}, dimensions={0} | all-to-all | bytes 32768 | tf_op jit(solution)/shard_map/all_to_all | solution.py:342
  54.6 0.7 shard_map.62
  55.3 11.6 %all_to_all.32 = f32[16,1,128]{2,1,0:T(1,128)S(1)} all-to-all(f32[16,1,128]{2,1,0:T(1,128)S(1)} %broadcast_in_dim.20), channel_id=1, replica_groups=mesh['gx_0'=8,'gx_1'=4,'gy_0'=8,'gy_1'=2] {'gx_0','gy_1'}, dimensions={0} | all-to-all | bytes 16384 | tf_op jit(solution)/shard_map/all_to_all | solution.py:342
  66.8 11.6 %all_to_all.33.parts_ref = f32[32,1,128]{2,1,0:T(1,128)S(1)} all-to-all(f32[32,1,128]{2,1,0:T(1,128)S(1)} %broadcast_in_dim.21), channel_id=1, replica_groups=mesh['gx_0'=8,'gx_1'=4,'gy_0'=8,'gy_1'=2] {'gx_1','gy_0'}, dimensions={0} | all-to-all | bytes 32768 | tf_op jit(solution)/shard_map/all_to_all | solution.py:342
  78.5 1.3 %shard_map.63 = (f32[16,512]{1,0:T(8,128)S(1)}, f32[9,16,512]{2,1,0:T(8,128)S(1)}, f32[1,128]{1,0:T(1,128)S(1)}) custom-call(f32[32,1,128]{2,1,0:T(1,128)S(1)} %all_to_all.33.parts_ref, f32[3,48,640]{2,1,0:T(8,128)S(1)} %get-tuple-element.27.last_ref, f32[3,48,640]{2,1,0:T(8,128)S(1)} %get-tuple-element.25.fields_ref, f32[48,640]{1,0:T(8,128)S(1)} %get-tuple-element.28.later_ref), custom_call_target="tpu_custom_call" | custom-call | tf_op jit(solution)/shard_map/pallas_call | solution.py:362
  79.8 11.3 %all_to_all.34 = f32[16,1,128]{2,1,0:T(1,128)S(1)} all-to-all(f32[16,1,128]{2,1,0:T(1,128)S(1)} %broadcast_in_dim.22), channel_id=1, replica_groups=mesh['gx_0'=8,'gx_1'=4,'gy_0'=8,'gy_1'=2] {'gx_0','gy_1'}, dimensions={0} | all-to-all | bytes 16384 | tf_op jit(solution)/shard_map/all_to_all | solution.py:342
  91.1 11.6 %all_to_all.35.parts_ref = f32[32,1,128]{2,1,0:T(1,128)S(1)} all-to-all(f32[32,1,128]{2,1,0:T(1,128)S(1)} %broadcast_in_dim.23), channel_id=1, replica_groups=mesh['gx_0'=8,'gx_1'=4,'gy_0'=8,'gy_1'=2] {'gx_1','gy_0'}, dimensions={0} | all-to-all | bytes 32768 | tf_op jit(solution)/shard_map/all_to_all | solution.py:342
  102.8 0.9 shard_map.64
  (9 shorter events, 0.1 us)
Async XLA Ops:
  1.6 7.1 %collective-permute-start = (f32[56,512]{1,0:T(8,128)S(1)}, f32[56,512]{1,0:T(8,128)S(1)}, u32[]{:S(2)}, u32[]{:S(2)}) collective-permute-start(f32[56,512]{1,0:T(8,128)S(1)} %get-tuple-element.18), channel_id=1, source_target_pairs={{16,32},{48,64},{80,96},{112,128},{144,160},{176,192},{208,224},{2... | collective-permute-start | bytes 344072 | tf_op jit(solution)/shard_map/ppermute | solution.py:355
  2.3 8.6 %collective-permute-start.1 = (f32[56,512]{1,0:T(8,128)S(1)}, f32[56,512]{1,0:T(8,128)S(1)}, u32[]{:S(2)}, u32[]{:S(2)}) collective-permute-start(f32[56,512]{1,0:T(8,128)S(1)} %get-tuple-element.19), channel_id=1, source_target_pairs={{0,16},{32,48},{64,80},{96,112},{128,144},{160,176},{192,208},{224... | collective-permute-start | bytes 344072 | tf_op jit(solution)/shard_map/ppermute | solution.py:355
  11.0 7.7 %collective-permute-start.2 = (f32[48,128]{1,0:T(8,128)S(1)}, f32[48,128]{1,0:T(8,128)S(1)}, u32[]{:S(2)}, u32[]{:S(2)}) collective-permute-start(f32[48,128]{1,0:T(8,128)S(1)} %get-tuple-element.21), channel_id=1, source_target_pairs={{1,2},{3,4},{5,6},{7,8},{9,10},{11,12},{13,14},{2,1},{4,3},{6,5},{... | collective-permute-start | bytes 73736 | tf_op jit(solution)/shard_map/ppermute | solution.py:355
  16.8 3.1 %collective-permute-start.3 = (f32[48,128]{1,0:T(8,128)S(1)}, f32[48,128]{1,0:T(8,128)S(1)}, u32[]{:S(2)}, u32[]{:S(2)}) collective-permute-start(f32[48,128]{1,0:T(8,128)S(1)} %get-tuple-element.22), channel_id=1, source_target_pairs={{0,1},{2,3},{4,5},{6,7},{8,9},{10,11},{12,13},{14,15},{1,0},{3,2},... | collective-permute-start | bytes 73736 | tf_op jit(solution)/shard_map/ppermute | solution.py:355

commit v4 on v3

--- a/solution.py
+++ b/solution.py
@@ -8,10 +8,10 @@
 from jax.sharding import Mesh
 from jax.sharding import PartitionSpec as P
 
-GX = ("gx_0", "gx_1")
+GX = ("gx_0", "gx_1", "gx_2")
 GY = ("gy_0", "gy_1")
 FIRST = ("gx_0", "gy_1")
-SECOND = ("gx_1", "gy_0")
+SECOND = ("gx_1", "gx_2", "gy_0")
 
 inv_step = 0.5
 coupling = 0.5
@@ -210,12 +210,14 @@
     x, own = own_ref.shape[1:]
     odd = odd_index(GX, (8, own))
 
-    def tile(k, odd_from, even_from):
-        here = pl.ds(8 * k, 8)
-        return jnp.where(odd, odd_from[here, :], even_from[here, :])
-
-    above = [tile(k, near_ref, far_ref) for k in range(FIELDS + 2)]
-    below = [tile(k, far_ref, near_ref) for k in range(FIELDS + 2)]
+    sent = FIELDS + 2
+
+    def tile(k, odd_from, odd_start, even_from, even_start):
+        odd_tile = odd_from[8 * (odd_start + k) : 8 * (odd_start + k) + 8, :]
+        return jnp.where(odd, odd_tile, even_from[8 * (even_start + k) : 8 * (even_start + k) + 8, :])
+
+    above = [tile(k, near_ref, 0, far_ref, 0) for k in range(sent)]
+    below = [tile(k, far_ref, 0, near_ref, sent) for k in range(sent)]
     rest_above = {
         TERMINAL: above[FIELDS],
         DIAGONAL: pltpu.roll(above[FIELDS], 5, 0),
@@ -249,8 +251,8 @@
     wide = own + EDGE
     keep = inside(3 * x, wide, -x, own, grid)
     odd = odd_index(GY, (3 * x, EDGE))
-    left = jnp.where(odd, near_edge[...], far_edge[...])
-    right = jnp.where(odd, far_edge[...], near_edge[...])
+    left = jnp.where(odd, near_edge[: 3 * x, :], far_edge[...])
+    right = jnp.where(odd, far_edge[...], near_edge[3 * x :, :])
     half = lax.broadcasted_iota(jnp.int32, (3 * x, EDGE), 1) < HALF
 
     def extended(k):
@@ -349,12 +351,11 @@
 
 def swapped(far, near, axis):
     peers = lax.axis_size(axis)
-
-    def swap(array, start):
-        pairs = [(i, i + 1) for i in range(start, peers - 1, 2)]
-        return lax.ppermute(array, axis, pairs + [(b, a) for a, b in pairs])
-
-    return swap(far, 1), swap(near, 0)
+    pairs = [(i, i + 1) for i in range(1, peers - 1, 2)]
+    return (
+        lax.ppermute(far, axis, pairs + [(b, a) for a, b in pairs]),
+        lax.all_gather(near, axis[-1], tiled=True),
+    )
 
 
 def call(kernel, out_shape, *args, results=pltpu.VMEM):
@@ -407,7 +408,7 @@
 
 
 def solution(mesh):
-    torus = Mesh(mesh.devices.reshape(8, 4, 8, 2), ("gx_0", "gx_1", "gy_0", "gy_1"))
+    torus = Mesh(mesh.devices.reshape(8, 2, 2, 8, 2), GX + GY)
     in_specs = (P(GX, GY), P(GX, GY), P(None, GX, GY), P(GX, GY))
     out_specs = (P(GX, GY), P(GX, GY))
     return jax.shard_map(

time: 104 us -> 104 us (level)
  blocking collectives: 80.2 us -> 91.4 us
  starting transfers between devices: 14.8 us -> 6.47 us
  waiting for transfers between devices: 3.31 us -> 0.01 us
    all_gather x0 -> x2, blocking collectives: none -> 9.16 us  [swapped(): lax.all_gather(near, axis[-1], tiled=True)]
    ppermute x4 -> x2, starting transfers between devices: 14.8 us -> 6.47 us  [swapped(): lax.ppermute(far, axis, pairs + [(b, a) for a, b in pairs])]
    ppermute x4 -> x2, waiting for transfers between devices: 3.31 us -> 0.01 us  [swapped(): lax.ppermute(far, axis, pairs + [(b, a) for a, b in pairs])]
    all_to_all x6, blocking collectives: 80.2 us -> 82.2 us  [spread(): return lax.all_to_all(copies, axes, split_axis=0, concat_axis=0, tiled=True)]
  transfers between devices with their start and end apart: 4 -> 2, of which waited for: 2 -> 0; matrix products, arithmetic and copies ran while one was open for 0% -> 0% of each run, Pallas kernels for 0% -> 0%
where the time goes in v4:
time: 104 us; the launch traced here: 103 us
  blocking collectives  91.4 us (88%)
  starting transfers between devices  6.47 us (6%)
  Pallas kernels  4.53 us (4%)
    all_to_all x6, blocking collectives, spread(): return lax.all_to_all(copies, axes, split_axis=0, concat_axis=0, tiled=True)  82.2 us
    all_gather x2, blocking collectives, swapped(): lax.all_gather(near, axis[-1], tiled=True)  9.16 us
    ppermute x2, starting transfers between devices, swapped(): lax.ppermute(far, axis, pairs + [(b, a) for a, b in pairs])  6.47 us
    pallas_call x5, Pallas kernels, call(): pl.pallas_call(kernel, out_shape=[results(s, jnp.float32) for s in out_sh...  3.59 us
  transfers between devices with their start and end apart: 2, of which 0 were waited for; matrix products, arithmetic and copies ran while one was open for 0% of the time, Pallas kernels for 0%

profile of v4, /device:TPU:1, one launch (start us, length us, event | category | flops | bytes accessed | tf_op | source)
XLA Modules:
  0.0 103.2 jit_solution(9967167330556463334)
XLA Ops:
  0.6 0.9 shard_map.59
  1.6 0.7 collective-permute-start
  2.3 7.3 %all_gather.6.near_ref = f32[112,512]{1,0:T(8,128)S(1)} all-gather(f32[56,512]{1,0:T(8,128)S(1)} %get-tuple-element.19), channel_id=1, replica_groups=mesh['gx_0'=8,'gx_1'=2,'gx_2'=2,'gy_0'=8,'gy_1'=2] {'gx_2'}, dimensions={0}, use_global_device_ids=true | all-gather | bytes 344064 | tf_op jit(solution)/shard_map/all_gather | solution.py:357
  9.6 0.0 collective-permute-done.far_ref
  9.6 0.1 shard_map.60
  9.7 5.8 %collective-permute-start.1 = (f32[48,128]{1,0:T(8,128)S(1)}, f32[48,128]{1,0:T(8,128)S(1)}, u32[]{:S(2)}, u32[]{:S(2)}) collective-permute-start(f32[48,128]{1,0:T(8,128)S(1)} %get-tuple-element.21), channel_id=1, source_target_pairs={{1,2},{3,4},{5,6},{7,8},{9,10},{11,12},{13,14},{2,1},{4,3},{6,5},{... | collective-permute-start | bytes 73736 | tf_op jit(solution)/shard_map/ppermute | solution.py:356
  15.5 1.8 %all_gather.7.near_edge = f32[96,128]{1,0:T(8,128)S(1)} all-gather(f32[48,128]{1,0:T(8,128)S(1)} %get-tuple-element.22), channel_id=1, replica_groups=mesh['gx_0'=8,'gx_1'=2,'gx_2'=2,'gy_0'=8,'gy_1'=2] {'gy_1'}, dimensions={0}, use_global_device_ids=true | all-gather | bytes 73728 | tf_op jit(solution)/shard_map/all_gather | solution.py:357
  17.4 0.0 collective-permute-done.1.far_edge
  17.4 0.6 shard_map.61
  17.9 15.8 %all_to_all.30 = f32[16,1,128]{2,1,0:T(1,128)S(1)} all-to-all(f32[16,1,128]{2,1,0:T(1,128)S(1)} %broadcast_in_dim.18), channel_id=1, replica_groups=mesh['gx_0'=8,'gx_1'=2,'gx_2'=2,'gy_0'=8,'gy_1'=2] {'gx_0','gy_1'}, dimensions={0} | all-to-all | bytes 16384 | tf_op jit(solution)/shard_map/all_to_all | solution.py:344
  33.8 20.3 %all_to_all.31.parts_ref = f32[32,1,128]{2,1,0:T(1,128)S(1)} all-to-all(f32[32,1,128]{2,1,0:T(1,128)S(1)} %broadcast_in_dim.19), channel_id=1, replica_groups=mesh['gx_0'=8,'gx_1'=2,'gx_2'=2,'gy_0'=8,'gy_1'=2] {'gx_1','gx_2','gy_0'}, dimensions={0} | all-to-all | bytes 32768 | tf_op jit(solution)/shard_map/all_to_all | solution.py:344
  54.1 0.7 shard_map.62
  54.7 11.6 %all_to_all.32 = f32[16,1,128]{2,1,0:T(1,128)S(1)} all-to-all(f32[16,1,128]{2,1,0:T(1,128)S(1)} %broadcast_in_dim.20), channel_id=1, replica_groups=mesh['gx_0'=8,'gx_1'=2,'gx_2'=2,'gy_0'=8,'gy_1'=2] {'gx_0','gy_1'}, dimensions={0} | all-to-all | bytes 16384 | tf_op jit(solution)/shard_map/all_to_all | solution.py:344
  66.3 11.6 %all_to_all.33.parts_ref = f32[32,1,128]{2,1,0:T(1,128)S(1)} all-to-all(f32[32,1,128]{2,1,0:T(1,128)S(1)} %broadcast_in_dim.21), channel_id=1, replica_groups=mesh['gx_0'=8,'gx_1'=2,'gx_2'=2,'gy_0'=8,'gy_1'=2] {'gx_1','gx_2','gy_0'}, dimensions={0} | all-to-all | bytes 32768 | tf_op jit(solution)/shard_map/all_to_all | solution.py:344
  78.0 1.3 %shard_map.63 = (f32[16,512]{1,0:T(8,128)S(1)}, f32[9,16,512]{2,1,0:T(8,128)S(1)}, f32[1,128]{1,0:T(1,128)S(1)}) custom-call(f32[32,1,128]{2,1,0:T(1,128)S(1)} %all_to_all.33.parts_ref, f32[3,48,640]{2,1,0:T(8,128)S(1)} %get-tuple-element.27.last_ref, f32[3,48,640]{2,1,0:T(8,128)S(1)} %get-tuple-element.25.fields_ref, f32[48,640]{1,0:T(8,128)S(1)} %get-tuple-element.28.later_ref), custom_call_target="tpu_custom_call" | custom-call | tf_op jit(solution)/shard_map/pallas_call | solution.py:363
  79.3 11.3 %all_to_all.34 = f32[16,1,128]{2,1,0:T(1,128)S(1)} all-to-all(f32[16,1,128]{2,1,0:T(1,128)S(1)} %broadcast_in_dim.22), channel_id=1, replica_groups=mesh['gx_0'=8,'gx_1'=2,'gx_2'=2,'gy_0'=8,'gy_1'=2] {'gx_0','gy_1'}, dimensions={0} | all-to-all | bytes 16384 | tf_op jit(solution)/shard_map/all_to_all | solution.py:344
  90.6 11.6 %all_to_all.35.parts_ref = f32[32,1,128]{2,1,0:T(1,128)S(1)} all-to-all(f32[32,1,128]{2,1,0:T(1,128)S(1)} %broadcast_in_dim.23), channel_id=1, replica_groups=mesh['gx_0'=8,'gx_1'=2,'gx_2'=2,'gy_0'=8,'gy_1'=2] {'gx_1','gx_2','gy_0'}, dimensions={0} | all-to-all | bytes 32768 | tf_op jit(solution)/shard_map/all_to_all | solution.py:344
  102.3 0.9 shard_map.64
  (9 shorter events, 0.1 us)
Async XLA Ops:
  1.6 8.0 %collective-permute-start = (f32[56,512]{1,0:T(8,128)S(1)}, f32[56,512]{1,0:T(8,128)S(1)}, u32[]{:S(2)}, u32[]{:S(2)}) collective-permute-start(f32[56,512]{1,0:T(8,128)S(1)} %get-tuple-element.18), channel_id=1, source_target_pairs={{16,32},{48,64},{80,96},{112,128},{144,160},{176,192},{208,224},{2... | collective-permute-start | bytes 344072 | tf_op jit(solution)/shard_map/ppermute | solution.py:356
  9.7 7.7 %collective-permute-start.1 = (f32[48,128]{1,0:T(8,128)S(1)}, f32[48,128]{1,0:T(8,128)S(1)}, u32[]{:S(2)}, u32[]{:S(2)}) collective-permute-start(f32[48,128]{1,0:T(8,128)S(1)} %get-tuple-element.21), channel_id=1, source_target_pairs={{1,2},{3,4},{5,6},{7,8},{9,10},{11,12},{13,14},{2,1},{4,3},{6,5},{... | collective-permute-start | bytes 73736 | tf_op jit(solution)/shard_map/ppermute | solution.py:356

commit v5 on v4

--- a/solution.py
+++ b/solution.py
@@ -8,10 +8,10 @@
 from jax.sharding import Mesh
 from jax.sharding import PartitionSpec as P
 
-GX = ("gx_0", "gx_1", "gx_2")
+BAND = ("band_0", "band_1")
+PART = "part"
+GX = (*BAND, PART)
 GY = ("gy_0", "gy_1")
-FIRST = ("gx_0", "gy_1")
-SECOND = ("gx_1", "gx_2", "gy_0")
 
 inv_step = 0.5
 coupling = 0.5
@@ -28,7 +28,10 @@
 EDGE = 128
 TERMINAL, DIAGONAL, GUESS, INITIAL = 0, 1, 2, 4
 FIELDS = 5
+VMEM_LIMIT = 24 * 2**20
 STRIP = 16
+HALO = 16
+INNER = 8
 
 
 def before(v, dim):
@@ -41,7 +44,7 @@
 
 def inside(rows, wide, first_row, own, grid):
     nx, ny, local_x, local_y = grid
-    row = lax.broadcasted_iota(jnp.int32, (rows, wide), 0) + (lax.axis_index(GX) * local_x + first_row)
+    row = lax.broadcasted_iota(jnp.int32, (rows, wide), 0) + (lax.axis_index(BAND) * local_x + first_row)
     lane = lax.broadcasted_iota(jnp.int32, (rows, wide), 1)
     column = jnp.where(lane < own + HALF, lane, lane - wide) + lax.axis_index(GY) * local_y
     return (row >= 0) & (row < nx) & (column >= 0) & (column < ny)
@@ -167,9 +170,12 @@
     return v[(v.shape[0] - x) // 2 : (v.shape[0] + x) // 2, :own]
 
 
+def inner(v):
+    return v[HALO - INNER : v.shape[0] - (HALO - INNER)]
+
+
 def gathered_products(parts_ref):
-    parts = parts_ref[...]
-    return jnp.sum(parts.reshape(parts.shape[0], 128), axis=0, keepdims=True)
+    return jnp.sum(parts_ref[...], axis=0, keepdims=True)
 
 
 def odd_index(axis, shape):
@@ -177,7 +183,7 @@
     return (lax.broadcasted_iota(jnp.int32, shape, 0) * 0 + place) == 1
 
 
-def stack_kernel(terminal, diagonal, guess, initial, fields_ref, far_ref, near_ref, sems):
+def stack_kernel(terminal, diagonal, guess, initial, fields_ref, sems):
     copies = [
         pltpu.make_async_copy(terminal, fields_ref.at[TERMINAL], sems.at[0]),
         pltpu.make_async_copy(diagonal, fields_ref.at[DIAGONAL], sems.at[1]),
@@ -188,27 +194,31 @@
         copy.start()
     for copy in copies:
         copy.wait()
-    fields = fields_ref[...]
-    shape = (8, fields.shape[2])
+
+
+def row_kernel(band_ref, far_ref, near_ref):
+    parts, _, _, own = band_ref.shape
+    shape = (8, own)
     row = lax.broadcasted_iota(jnp.int32, shape, 0)
-    first, second = fields[:, :8], fields[:, 8:]
-    top = [first[k] for k in range(FIELDS)] + [
+    first, second = ([band_ref[0, k, half] for k in range(FIELDS)] for half in (pl.ds(0, 8), pl.ds(8, 8)))
+    top = first + [
         jnp.where(row < 5, second[TERMINAL], pltpu.roll(second[DIAGONAL], 5, 0)),
         jnp.where(row < 4, second[GUESS + 1], pltpu.roll(second[GUESS], 4, 0)),
     ]
-    bottom = [second[k] for k in range(FIELDS)] + [
+    first, second = ([band_ref[parts - 1, k, half] for k in range(FIELDS)] for half in (pl.ds(0, 8), pl.ds(8, 8)))
+    bottom = second + [
         jnp.where(row >= 3, first[TERMINAL], pltpu.roll(first[DIAGONAL], 3, 0)),
         jnp.where(row >= 4, first[GUESS + 1], pltpu.roll(first[GUESS], 4, 0)),
     ]
-    odd = odd_index(GX, shape)
+    odd = odd_index(BAND, shape)
     for k, (t, b) in enumerate(zip(top, bottom)):
         far_ref[8 * k : 8 * k + 8, :] = jnp.where(odd, b, t)
         near_ref[8 * k : 8 * k + 8, :] = jnp.where(odd, t, b)
 
 
-def column_kernel(own_ref, far_ref, near_ref, tall_ref, far_edge, near_edge):
-    x, own = own_ref.shape[1:]
-    odd = odd_index(GX, (8, own))
+def column_kernel(band_ref, far_ref, near_ref, tall_ref, far_edge, near_edge):
+    parts, _, x, own = band_ref.shape
+    odd = odd_index(BAND, (8, own))
 
     sent = FIELDS + 2
 
@@ -231,12 +241,14 @@
         GUESS: pltpu.roll(below[FIELDS + 1], 4, 0),
     }
     nothing = jnp.zeros((8, own), jnp.float32)
-    shape = (3 * x, 128)
+    shape = (parts * x + 2 * HALO, 128)
     strip = lax.broadcasted_iota(jnp.int32, shape, 1) // STRIP
     firsts = lasts = jnp.zeros(shape, jnp.float32)
     for k in range(FIELDS):
-        parts = [rest_above.get(k, nothing), above[k], own_ref[k], below[k], rest_below.get(k, nothing)]
-        whole = jnp.concatenate(parts, axis=0)
+        blocks = [band_ref[part, k] for part in range(parts)]
+        whole = jnp.concatenate(
+            [rest_above.get(k, nothing), above[k], *blocks, below[k], rest_below.get(k, nothing)], axis=0
+        )
         tall_ref[k] = whole
         first, last = whole[:, :128], whole[:, own - 128 :]
         firsts = jnp.where(strip == k, pltpu.roll(first, STRIP * k, 1) if k else first, firsts)
@@ -246,14 +258,15 @@
     near_edge[...] = jnp.where(odd, firsts, lasts)
 
 
-def first_kernel(grid, tall_ref, far_edge, near_edge, basis_ref, fields_ref, sums_ref):
+def first_kernel(grid, tall_ref, far_edge, near_edge, basis_ref, center_ref, guess_ref, initial_ref, sums_ref):
     _, _, x, own = grid
     wide = own + EDGE
-    keep = inside(3 * x, wide, -x, own, grid)
-    odd = odd_index(GY, (3 * x, EDGE))
-    left = jnp.where(odd, near_edge[: 3 * x, :], far_edge[...])
-    right = jnp.where(odd, far_edge[...], near_edge[3 * x :, :])
-    half = lax.broadcasted_iota(jnp.int32, (3 * x, EDGE), 1) < HALF
+    rows = tall_ref.shape[1]
+    keep = inside(rows, wide, -HALO, own, grid)
+    odd = odd_index(GY, (rows, EDGE))
+    left = jnp.where(odd, near_edge[:rows, :], far_edge[...])
+    right = jnp.where(odd, far_edge[...], near_edge[rows:, :])
+    half = lax.broadcasted_iota(jnp.int32, (rows, EDGE), 1) < HALF
 
     def extended(k):
         from_right = pltpu.roll(right, 128 - STRIP * k, 1) if k else right
@@ -266,44 +279,44 @@
     vs = basis(jnp.where(keep, rhs, 0.0), center, keep)
     for k in range(3):
         basis_ref[k] = vs[k]
-    fields_ref[0] = center
-    fields_ref[1] = extended(GUESS)
-    fields_ref[2] = extended(INITIAL)
+    center_ref[...] = center
+    guess_ref[...] = extended(GUESS)
+    initial_ref[...] = inner(extended(INITIAL))
     mine = [middle(v, x, own) for v in vs]
     sums_ref[...] = row_of([(k, dot(mine[i], mine[j])) for k, (i, j) in enumerate(PAIRS)])
 
 
-def second_kernel(grid, parts_ref, last_ref, fields_ref, later_ref, basis_ref, sums_ref):
+def second_kernel(grid, parts_ref, last_ref, center_ref, guess_ref, later_ref, basis_ref, inner_center, sums_ref):
     _, _, x, own = grid
     rows, wide = last_ref.shape[1:]
-    keep = inside(rows, wide, -x, own, grid)
+    keep = inside(rows, wide, -HALO, own, grid)
     row = gathered_products(parts_ref)
     coefs = coefficients([entry(row, k) for k in range(len(PAIRS))])
     later = combined(coefs, [last_ref[k] for k in range(3)])
-    later_ref[...] = later
-    rhs = inv_step * later - hamiltonian(later) + coupling * fields_ref[1]
-    vs = basis(jnp.where(keep, rhs, 0.0), fields_ref[0], keep)
+    later_ref[...] = inner(later)
+    center = center_ref[...]
+    inner_center[...] = inner(center)
+    rhs = inv_step * later - hamiltonian(later) + coupling * guess_ref[...]
+    vs = basis(jnp.where(keep, rhs, 0.0), center, keep)
     for k in range(3):
-        basis_ref[k] = vs[k]
+        basis_ref[k] = inner(vs[k])
     mine = [middle(v, x, own) for v in vs]
     sums_ref[...] = row_of([(k, dot(mine[i], mine[j])) for k, (i, j) in enumerate(PAIRS)])
 
 
-def third_kernel(grid, parts_ref, last_ref, fields_ref, later_ref, value_ref, images_ref, sums_ref):
+def third_kernel(grid, parts_ref, last_ref, center_ref, initial_ref, later_ref, value_ref, images_ref, sums_ref):
     _, _, x, own = grid
     rows, wide = last_ref.shape[1:]
-    cut = x // 2
-    some = pl.ds(cut, rows - 2 * cut)
-    keep = inside(rows - 2 * cut, wide, cut - x, own, grid)
+    keep = inside(rows, wide, -INNER, own, grid)
     row = gathered_products(parts_ref)
     coefs = coefficients([entry(row, k) for k in range(len(PAIRS))])
-    value = combined(coefs, [last_ref[k, some, :] for k in range(3)])
+    value = combined(coefs, [last_ref[k] for k in range(3)])
     value_ref[...] = middle(value, x, own)
-    center = fields_ref[0, some, :]
-    firsts = basis(density_rhs(fields_ref[2, some, :], drift(value), keep), center, keep)
+    center = center_ref[...]
+    firsts = basis(density_rhs(initial_ref[...], drift(value), keep), center, keep)
     mine = [middle(v, x, own) for v in firsts]
     values = [(6 * 8 + k, dot(mine[i], mine[j])) for k, (i, j) in enumerate(PAIRS)]
-    speeds = drift(later_ref[some, :])
+    speeds = drift(later_ref[...])
     images = []
     for v in firsts[:3]:
         chain = basis(density_rhs(v, speeds, keep), center, keep)
@@ -318,7 +331,9 @@
 
 
 def fourth_kernel(parts_ref, images_ref, value_ref, value_out, density_ref):
-    value_out[...] = value_ref[...]
+    x = value_out.shape[0]
+    mine = pl.ds(pl.multiple_of(lax.axis_index(PART) * x, x), x)
+    value_out[...] = value_ref[mine, :]
     row = gathered_products(parts_ref)
     first = coefficients([entry(row, 6 * 8 + k) for k in range(len(PAIRS))])
     products = []
@@ -333,20 +348,16 @@
     total = None
     for i in range(3):
         for k in range(3):
-            term = (first[i] * second[k]) * images_ref[3 * i + k]
+            term = (first[i] * second[k]) * images_ref[3 * i + k, mine, :]
             total = term if total is None else total + term
     density_ref[...] = total
 
 
-def spread(row, axes):
+def everywhere(row):
+    axes = (*BAND, *GY)
     size = lax.axis_size(axes)
     copies = jnp.broadcast_to(row, (size, 1, 128))
-    return lax.all_to_all(copies, axes, split_axis=0, concat_axis=0, tiled=True)
-
-
-def everywhere(row):
-    nearer = spread(row, FIRST).sum(axis=0)
-    return spread(nearer, SECOND)
+    return lax.all_to_all(copies, axes, split_axis=0, concat_axis=0, tiled=True).reshape(size, 128)
 
 
 def swapped(far, near, axis):
@@ -365,39 +376,46 @@
         out_shape=[results(s, jnp.float32) for s in out_shape],
         in_specs=[vmem] * len(args),
         out_specs=[vmem] * len(out_shape),
+        compiler_params=pltpu.CompilerParams(vmem_limit_bytes=VMEM_LIMIT),
     )(*[pltpu.with_memory_space_constraint(a, pltpu.VMEM) for a in args])
 
 
 def shards(terminal, initial_density, density_guess, diagonal):
     x, own = terminal.shape
-    grid = (x * lax.axis_size(GX), own * lax.axis_size(GY), x, own)
-    packed = (8 * (FIELDS + 2), own)
-    fields, far, near = pl.pallas_call(
+    band = x * lax.axis_size(PART)
+    grid = (x * lax.axis_size(GX), own * lax.axis_size(GY), band, own)
+    fields = pl.pallas_call(
         stack_kernel,
-        out_shape=[pltpu.VMEM(s, jnp.float32) for s in [(FIELDS, x, own), packed, packed]],
+        out_shape=pltpu.VMEM((FIELDS, x, own), jnp.float32),
         in_specs=[pl.BlockSpec(memory_space=pltpu.HBM)] * 4,
-        out_specs=[pl.BlockSpec(memory_space=pltpu.VMEM)] * 3,
+        out_specs=pl.BlockSpec(memory_space=pltpu.VMEM),
         scratch_shapes=[pltpu.SemaphoreType.DMA((4,))],
     )(terminal, diagonal, density_guess, initial_density)
-    strips = (3 * x, 128)
+    whole = lax.all_gather(fields, PART)
+    packed = (8 * (FIELDS + 2), own)
+    far, near = call(row_kernel, [packed, packed], whole)
+    rows = band + 2 * HALO
     tall, far, near = call(
-        column_kernel, [(FIELDS, 3 * x, own), strips, strips], fields, *swapped(far, near, GX)
-    )
-    full = (3 * x, own + EDGE)
-    basis1, kept, sums = call(
+        column_kernel,
+        [(FIELDS, rows, own), (rows, 128), (rows, 128)],
+        whole, *swapped(far, near, BAND),
+    )
+    wide = own + EDGE
+    full, fewer = (rows, wide), (band + 2 * INNER, wide)
+    basis1, center, guess, initial, sums = call(
         functools.partial(first_kernel, grid),
-        [(3, *full), (3, *full), (1, 128)],
+        [(3, *full), full, full, fewer, (1, 128)],
         tall, *swapped(far, near, GY),
     )
-    later, basis0, sums = call(
+    later, basis0, center, sums = call(
         functools.partial(second_kernel, grid),
-        [full, (3, *full), (1, 128)],
-        everywhere(sums), basis1, kept,
+        [fewer, (3, *fewer), fewer, (1, 128)],
+        everywhere(sums), basis1, center, guess,
     )
     value, images, sums = call(
         functools.partial(third_kernel, grid),
-        [(x, own), (9, x, own), (1, 128)],
-        everywhere(sums), basis0, kept, later,
+        [(band, own), (9, band, own), (1, 128)],
+        everywhere(sums), basis0, center, initial, later,
     )
     return tuple(
         call(
@@ -408,7 +426,7 @@
 
 
 def solution(mesh):
-    torus = Mesh(mesh.devices.reshape(8, 2, 2, 8, 2), GX + GY)
+    torus = Mesh(mesh.devices.reshape(4, 2, 4, 8, 2), GX + GY)
     in_specs = (P(GX, GY), P(GX, GY), P(None, GX, GY), P(GX, GY))
     out_specs = (P(GX, GY), P(GX, GY))
     return jax.shard_map(

time: 104 us -> 99.8 us (0.960)
  blocking collectives: 91.4 us -> 83.2 us
  Pallas kernels: 4.53 us -> 7.46 us
  starting transfers between devices: 6.47 us -> 8.03 us
    all_to_all x6 -> x3, blocking collectives: 82.2 us -> 62.1 us  [everywhere(): lax.all_to_all(copies, axes, split_axis=0, concat_axis=0, tiled=True)]
    all_gather x0 -> x1, blocking collectives: none -> 11.3 us  [shards(): whole = lax.all_gather(fields, PART)]
    pallas_call x5 -> x6, Pallas kernels: 3.59 us -> 6.54 us  [call(): pl.pallas_call(kernel, out_shape=[results(s, jnp.float32) for s in out_sh...]
    ppermute x2, starting transfers between devices: 6.47 us -> 8.03 us  [swapped(): lax.ppermute(far, axis, pairs + [(b, a) for a, b in pairs])]
where the time goes in v5:
time: 99.8 us; the launch traced here: 99.5 us
  blocking collectives  83.2 us (83%)
  starting transfers between devices  8.03 us (8%)
  Pallas kernels  7.46 us (7%)
    all_to_all x3, blocking collectives, everywhere(): lax.all_to_all(copies, axes, split_axis=0, concat_axis=0, tiled=True)  62.1 us
    all_gather x1, blocking collectives, shards(): whole = lax.all_gather(fields, PART)  11.3 us
    all_gather x2, blocking collectives, swapped(): lax.all_gather(near, axis[-1], tiled=True)  9.79 us
    ppermute x2, starting transfers between devices, swapped(): lax.ppermute(far, axis, pairs + [(b, a) for a, b in pairs])  8.03 us
    pallas_call x6, Pallas kernels, call(): pl.pallas_call(kernel, out_shape=[results(s, jnp.float32) for s in out_sh...  6.54 us
  transfers between devices with their start and end apart: 2, of which 0 were waited for; matrix products, arithmetic and copies ran while one was open for 0% of the time, Pallas kernels for 0%

profile of v5, /device:TPU:1, one launch (start us, length us, event | category | flops | bytes accessed | tf_op | source)
XLA Modules:
  0.0 99.5 jit_solution(241813659648706680)
XLA Ops:
  0.6 0.9 shard_map.59
  1.6 11.3 %all-gather = f32[20,16,512]{2,1,0:T(8,128)S(1)} all-gather(f32[5,16,512]{2,1,0:T(8,128)S(1)} %shard_map.59), channel_id=2, replica_groups=mesh['band_0'=4,'band_1'=2,'part'=4,'gy_0'=8,'gy_1'=2] {'part'}, dimensions={0}, use_global_device_ids=true | all-gather | bytes 819200 | tf_op jit(solution)/shard_map/all_gather | solution.py:394
  12.9 0.7 collective-permute-start
  13.6 7.9 %all_gather.14.near_ref = f32[112,512]{1,0:T(8,128)S(1)} all-gather(f32[56,512]{1,0:T(8,128)S(1)} %get-tuple-element.20), channel_id=1, replica_groups=mesh['band_0'=4,'band_1'=2,'part'=4,'gy_0'=8,'gy_1'=2] {'band_1'}, dimensions={0}, use_global_device_ids=true | all-gather | bytes 344064 | tf_op jit(solution)/shard_map/all_gather | solution.py:368
  21.5 0.0 collective-permute-done.far_ref
  21.5 0.2 shard_map.61
  21.7 7.4 %collective-permute-start.1 = (f32[96,128]{1,0:T(8,128)S(1)}, f32[96,128]{1,0:T(8,128)S(1)}, u32[]{:S(2)}, u32[]{:S(2)}) collective-permute-start(f32[96,128]{1,0:T(8,128)S(1)} %get-tuple-element.22), channel_id=1, source_target_pairs={{1,2},{3,4},{5,6},{7,8},{9,10},{11,12},{13,14},{2,1},{4,3},{6,5},{... | collective-permute-start | bytes 147464 | tf_op jit(solution)/shard_map/ppermute | solution.py:367
  29.1 1.9 %all_gather.15.near_edge = f32[192,128]{1,0:T(8,128)S(1)} all-gather(f32[96,128]{1,0:T(8,128)S(1)} %get-tuple-element.23), channel_id=1, replica_groups=mesh['band_0'=4,'band_1'=2,'part'=4,'gy_0'=8,'gy_1'=2] {'gy_1'}, dimensions={0}, use_global_device_ids=true | all-gather | bytes 147456 | tf_op jit(solution)/shard_map/all_gather | solution.py:368
  31.0 0.0 collective-permute-done.1.far_edge
  31.0 1.0 %shard_map.62 = (f32[3,96,640]{2,1,0:T(8,128)S(1)}, f32[96,640]{1,0:T(8,128)S(1)}, f32[96,640]{1,0:T(8,128)S(1)}, f32[80,640]{1,0:T(8,128)S(1)}, f32[1,128]{1,0:T(1,128)S(1)}) custom-call(f32[5,96,512]{2,1,0:T(8,128)S(1)} %get-tuple-element.21.tall_ref, f32[96,128]{1,0:T(8,128)S(1)} %collective-permute-done.1.far_edge, f32[192,128]{1,0:T(8,128)S(1)} %all_gather.15.near_edge), custom_call_target="tpu_custom_call" | custom-call | tf_op jit(solution)/shard_map/pallas_call | solution.py:374
  32.1 28.6 %all_to_all.15 = f32[128,1,128]{2,1,0:T(1,128)S(1)} all-to-all(f32[128,1,128]{2,1,0:T(1,128)S(1)} %broadcast_in_dim.9), channel_id=1, replica_groups=mesh['band_0'=4,'band_1'=2,'part'=4,'gy_0'=8,'gy_1'=2] {'band_0','band_1..., dimensions={0} | all-to-all | bytes 131072 | tf_op jit(solution)/shard_map/all_to_all | solution.py:360
  60.6 1.1 %shard_map.63 = (f32[80,640]{1,0:T(8,128)S(1)}, f32[3,80,640]{2,1,0:T(8,128)S(1)}, f32[80,640]{1,0:T(8,128)S(1)}, f32[1,128]{1,0:T(1,128)S(1)}) custom-call(f32[128,128]{1,0:T(8,128)S(1)} %bitcast.10, f32[3,96,640]{2,1,0:T(8,128)S(1)} %get-tuple-element.25.last_ref, f32[96,640]{1,0:T(8,128)S(1)} %get-tuple-element.26.center_ref, ...), custom_call_target="tpu_custom_call" | custom-call | tf_op jit(solution)/shard_map/pallas_call | solution.py:374
  61.8 16.8 %all_to_all.16 = f32[128,1,128]{2,1,0:T(1,128)S(1)} all-to-all(f32[128,1,128]{2,1,0:T(1,128)S(1)} %broadcast_in_dim.10), channel_id=1, replica_groups=mesh['band_0'=4,'band_1'=2,'part'=4,'gy_0'=8,'gy_1'=2] {'band_0','band_1..., dimensions={0} | all-to-all | bytes 131072 | tf_op jit(solution)/shard_map/all_to_all | solution.py:360
  78.6 3.2 %shard_map.64 = (f32[64,512]{1,0:T(8,128)S(1)}, f32[9,64,512]{2,1,0:T(8,128)S(1)}, f32[1,128]{1,0:T(1,128)S(1)}) custom-call(f32[128,128]{1,0:T(8,128)S(1)} %bitcast.9, f32[3,80,640]{2,1,0:T(8,128)S(1)} %get-tuple-element.29.last_ref, f32[80,640]{1,0:T(8,128)S(1)} %get-tuple-element.30.center_ref, f32[80,640]{1,0:T(8,128)S(1)} %get-tuple-element.31.initial_ref, ...), custom_call_target="tpu_custom_call" | custom-call | tf_op jit(solution)/shard_map/pallas_call | solution.py:374
  81.8 16.8 %all_to_all.17 = f32[128,1,128]{2,1,0:T(1,128)S(1)} all-to-all(f32[128,1,128]{2,1,0:T(1,128)S(1)} %broadcast_in_dim.11), channel_id=1, replica_groups=mesh['band_0'=4,'band_1'=2,'part'=4,'gy_0'=8,'gy_1'=2] {'band_0','band_1..., dimensions={0} | all-to-all | bytes 131072 | tf_op jit(solution)/shard_map/all_to_all | solution.py:360
  98.6 0.9 shard_map.65
  (4 shorter events, 0.1 us)
Async XLA Ops:
  12.9 8.6 %collective-permute-start = (f32[56,512]{1,0:T(8,128)S(1)}, f32[56,512]{1,0:T(8,128)S(1)}, u32[]{:S(2)}, u32[]{:S(2)}) collective-permute-start(f32[56,512]{1,0:T(8,128)S(1)} %get-tuple-element.19), channel_id=1, source_target_pairs={{64,128},{192,256},{320,384},{128,64},{256,192},{384,320},{65,129}... | collective-permute-start | bytes 344072 | tf_op jit(solution)/shard_map/ppermute | solution.py:367
  21.7 9.2 %collective-permute-start.1 = (f32[96,128]{1,0:T(8,128)S(1)}, f32[96,128]{1,0:T(8,128)S(1)}, u32[]{:S(2)}, u32[]{:S(2)}) collective-permute-start(f32[96,128]{1,0:T(8,128)S(1)} %get-tuple-element.22), channel_id=1, source_target_pairs={{1,2},{3,4},{5,6},{7,8},{9,10},{11,12},{13,14},{2,1},{4,3},{6,5},{... | collective-permute-start | bytes 147464 | tf_op jit(solution)/shard_map/ppermute | solution.py:367

commit v6 on v5

--- a/solution.py
+++ b/solution.py
@@ -18,16 +18,17 @@
 
 LOW = 0.6
 HIGH = 10.5
-S1 = 2.0
-S2 = 6.0
+S1 = 3.5
+S2 = 5.5
 S3 = 4.0
-PAIRS = ((0, 0), (0, 1), (0, 2), (1, 1), (1, 2), (2, 2), (2, 3))
+PAIRS = ((0, 0), (0, 1), (1, 1), (1, 2), (2, 2), (2, 3))
 MIXED = ((0, 0), (1, 1), (2, 2), (0, 1), (0, 2), (1, 2))
 
 HALF = 64
 EDGE = 128
 TERMINAL, DIAGONAL, GUESS, INITIAL = 0, 1, 2, 4
 FIELDS = 5
+SENT = FIELDS + 3
 VMEM_LIMIT = 24 * 2**20
 STRIP = 16
 HALO = 16
@@ -94,7 +95,10 @@
 
 
 def dot(a, b):
-    return jnp.sum(jnp.sum(a * b, axis=0, keepdims=True), axis=1, keepdims=True)
+    rows, wide = a.shape
+    total = jnp.sum((a * b).reshape(rows // 8, 8, wide), axis=0)
+    total = sum(total[:, k : k + 128] for k in range(128, wide, 128)) + total[:, :128]
+    return jnp.sum(jnp.sum(total, axis=1, keepdims=True), axis=0, keepdims=True)
 
 
 def row_of(values):
@@ -130,6 +134,7 @@
 
 def coefficients(products):
     g = dict(zip(PAIRS, products))
+    g[0, 2] = g[1, 1] + (S1 - S2) * g[0, 1]
     gram = [[g[0, 0], g[0, 1], g[0, 2]], [None, g[1, 1], g[1, 2]], [None, None, g[2, 2]]]
     energy = [
         [g[0, 1] + S1 * g[0, 0], g[1, 1] + S1 * g[0, 1], g[1, 2] + S1 * g[0, 2]],
@@ -183,7 +188,7 @@
     return (lax.broadcasted_iota(jnp.int32, shape, 0) * 0 + place) == 1
 
 
-def stack_kernel(terminal, diagonal, guess, initial, fields_ref, sems):
+def stack_kernel(terminal, diagonal, guess, initial, fields_ref, far_edge, near_edge, sems):
     copies = [
         pltpu.make_async_copy(terminal, fields_ref.at[TERMINAL], sems.at[0]),
         pltpu.make_async_copy(diagonal, fields_ref.at[DIAGONAL], sems.at[1]),
@@ -194,21 +199,50 @@
         copy.start()
     for copy in copies:
         copy.wait()
+    _, x, own = fields_ref.shape
+    shape = (x, 128)
+    strip = lax.broadcasted_iota(jnp.int32, shape, 1) // STRIP
+    firsts = lasts = jnp.zeros(shape, jnp.float32)
+    for k in range(FIELDS):
+        first, last = fields_ref[k, :, :128], fields_ref[k, :, own - 128 :]
+        firsts = jnp.where(strip == k, pltpu.roll(first, STRIP * k, 1) if k else first, firsts)
+        lasts = jnp.where(strip == k, pltpu.roll(last, STRIP * (k + 1), 1), lasts)
+    odd = odd_index(GY, shape)
+    far_edge[...] = jnp.where(odd, lasts, firsts)
+    near_edge[...] = jnp.where(odd, firsts, lasts)
+
+
+def edge_kernel(fields_ref, far_edge, near_edge, block_ref):
+    _, x, own = fields_ref.shape
+    odd = odd_index(GY, (x, EDGE))
+    left = jnp.where(odd, near_edge[:x, :], far_edge[...])
+    right = jnp.where(odd, far_edge[...], near_edge[x:, :])
+    for k in range(FIELDS):
+        block_ref[x * k : x * (k + 1), :] = fields_ref[k]
+    edges = [right[:8], left[:8], right[8:], left[8:]]
+    block_ref[x * FIELDS :, :] = jnp.concatenate(edges, axis=1)
 
 
 def row_kernel(band_ref, far_ref, near_ref):
-    parts, _, _, own = band_ref.shape
+    parts, _, own = band_ref.shape
     shape = (8, own)
     row = lax.broadcasted_iota(jnp.int32, shape, 0)
-    first, second = ([band_ref[0, k, half] for k in range(FIELDS)] for half in (pl.ds(0, 8), pl.ds(8, 8)))
+
+    def halves(part):
+        tiles = [band_ref[part, 8 * k : 8 * k + 8, :] for k in range(2 * FIELDS + 1)]
+        return tiles[: 2 * FIELDS : 2], tiles[1 : 2 * FIELDS : 2], tiles[2 * FIELDS]
+
+    first, second, edge = halves(0)
     top = first + [
         jnp.where(row < 5, second[TERMINAL], pltpu.roll(second[DIAGONAL], 5, 0)),
         jnp.where(row < 4, second[GUESS + 1], pltpu.roll(second[GUESS], 4, 0)),
+        edge,
     ]
-    first, second = ([band_ref[parts - 1, k, half] for k in range(FIELDS)] for half in (pl.ds(0, 8), pl.ds(8, 8)))
+    first, second, edge = halves(parts - 1)
     bottom = second + [
         jnp.where(row >= 3, first[TERMINAL], pltpu.roll(first[DIAGONAL], 3, 0)),
         jnp.where(row >= 4, first[GUESS + 1], pltpu.roll(first[GUESS], 4, 0)),
+        edge,
     ]
     odd = odd_index(BAND, shape)
     for k, (t, b) in enumerate(zip(top, bottom)):
@@ -216,18 +250,20 @@
         near_ref[8 * k : 8 * k + 8, :] = jnp.where(odd, t, b)
 
 
-def column_kernel(band_ref, far_ref, near_ref, tall_ref, far_edge, near_edge):
-    parts, _, x, own = band_ref.shape
+def first_kernel(grid, band_ref, far_ref, near_ref, basis_ref, center_ref, guess_ref, initial_ref, sums_ref):
+    _, _, x, own = grid
+    wide = own + EDGE
+    rows = x + 2 * HALO
+    parts = band_ref.shape[0]
+    keep = inside(rows, wide, -HALO, own, grid)
     odd = odd_index(BAND, (8, own))
-
-    sent = FIELDS + 2
 
     def tile(k, odd_from, odd_start, even_from, even_start):
         odd_tile = odd_from[8 * (odd_start + k) : 8 * (odd_start + k) + 8, :]
         return jnp.where(odd, odd_tile, even_from[8 * (even_start + k) : 8 * (even_start + k) + 8, :])
 
-    above = [tile(k, near_ref, 0, far_ref, 0) for k in range(sent)]
-    below = [tile(k, far_ref, 0, near_ref, sent) for k in range(sent)]
+    above = [tile(k, near_ref, 0, far_ref, 0) for k in range(SENT)]
+    below = [tile(k, far_ref, 0, near_ref, SENT) for k in range(SENT)]
     rest_above = {
         TERMINAL: above[FIELDS],
         DIAGONAL: pltpu.roll(above[FIELDS], 5, 0),
@@ -241,37 +277,27 @@
         GUESS: pltpu.roll(below[FIELDS + 1], 4, 0),
     }
     nothing = jnp.zeros((8, own), jnp.float32)
-    shape = (parts * x + 2 * HALO, 128)
-    strip = lax.broadcasted_iota(jnp.int32, shape, 1) // STRIP
-    firsts = lasts = jnp.zeros(shape, jnp.float32)
-    for k in range(FIELDS):
-        blocks = [band_ref[part, k] for part in range(parts)]
+    blocks = [above[-1], *[band_ref[part, 2 * 8 * FIELDS :, :] for part in range(parts)], below[-1]]
+    right, left = (
+        jnp.concatenate([b[:, at : at + 128] for b in blocks for at in (start, start + 256)], axis=0)
+        for start in (0, 128)
+    )
+    half = lax.broadcasted_iota(jnp.int32, (rows, EDGE), 1) < HALF
+
+    def extended(k):
         whole = jnp.concatenate(
-            [rest_above.get(k, nothing), above[k], *blocks, below[k], rest_below.get(k, nothing)], axis=0
+            [
+                rest_above.get(k, nothing),
+                above[k],
+                *[band_ref[part, 16 * k : 16 * k + 16, :] for part in range(parts)],
+                below[k],
+                rest_below.get(k, nothing),
+            ],
+            axis=0,
         )
-        tall_ref[k] = whole
-        first, last = whole[:, :128], whole[:, own - 128 :]
-        firsts = jnp.where(strip == k, pltpu.roll(first, STRIP * k, 1) if k else first, firsts)
-        lasts = jnp.where(strip == k, pltpu.roll(last, STRIP * (k + 1), 1), lasts)
-    odd = odd_index(GY, shape)
-    far_edge[...] = jnp.where(odd, lasts, firsts)
-    near_edge[...] = jnp.where(odd, firsts, lasts)
-
-
-def first_kernel(grid, tall_ref, far_edge, near_edge, basis_ref, center_ref, guess_ref, initial_ref, sums_ref):
-    _, _, x, own = grid
-    wide = own + EDGE
-    rows = tall_ref.shape[1]
-    keep = inside(rows, wide, -HALO, own, grid)
-    odd = odd_index(GY, (rows, EDGE))
-    left = jnp.where(odd, near_edge[:rows, :], far_edge[...])
-    right = jnp.where(odd, far_edge[...], near_edge[rows:, :])
-    half = lax.broadcasted_iota(jnp.int32, (rows, EDGE), 1) < HALF
-
-    def extended(k):
         from_right = pltpu.roll(right, 128 - STRIP * k, 1) if k else right
         from_left = pltpu.roll(left, 128 - STRIP * (k + 1), 1)
-        return jnp.concatenate([tall_ref[k], jnp.where(half, from_right, from_left)], axis=1)
+        return jnp.concatenate([whole, jnp.where(half, from_right, from_left)], axis=1)
 
     later = extended(TERMINAL)
     center = extended(DIAGONAL) + (inv_step + 4.0)
@@ -384,28 +410,24 @@
     x, own = terminal.shape
     band = x * lax.axis_size(PART)
     grid = (x * lax.axis_size(GX), own * lax.axis_size(GY), band, own)
-    fields = pl.pallas_call(
+    fields, far, near = pl.pallas_call(
         stack_kernel,
-        out_shape=pltpu.VMEM((FIELDS, x, own), jnp.float32),
+        out_shape=[pltpu.VMEM(s, jnp.float32) for s in [(FIELDS, x, own), (x, EDGE), (x, EDGE)]],
         in_specs=[pl.BlockSpec(memory_space=pltpu.HBM)] * 4,
-        out_specs=pl.BlockSpec(memory_space=pltpu.VMEM),
+        out_specs=[pl.BlockSpec(memory_space=pltpu.VMEM)] * 3,
         scratch_shapes=[pltpu.SemaphoreType.DMA((4,))],
     )(terminal, diagonal, density_guess, initial_density)
-    whole = lax.all_gather(fields, PART)
-    packed = (8 * (FIELDS + 2), own)
+    (block,) = call(edge_kernel, [(x * FIELDS + 8, own)], fields, *swapped(far, near, GY))
+    whole = lax.all_gather(block, PART)
+    packed = (8 * SENT, own)
     far, near = call(row_kernel, [packed, packed], whole)
     rows = band + 2 * HALO
-    tall, far, near = call(
-        column_kernel,
-        [(FIELDS, rows, own), (rows, 128), (rows, 128)],
-        whole, *swapped(far, near, BAND),
-    )
     wide = own + EDGE
     full, fewer = (rows, wide), (band + 2 * INNER, wide)
     basis1, center, guess, initial, sums = call(
         functools.partial(first_kernel, grid),
         [(3, *full), full, full, fewer, (1, 128)],
-        tall, *swapped(far, near, GY),
+        whole, *swapped(far, near, BAND),
     )
     later, basis0, center, sums = call(
         functools.partial(second_kernel, grid),

time: 99.8 us -> 99.8 us (level)
  blocking collectives: 83.2 us -> 85.4 us
  starting transfers between devices: 8.03 us -> 6.05 us
    all_to_all x3, blocking collectives: 62.1 us -> 65 us  [everywhere(): lax.all_to_all(copies, axes, split_axis=0, concat_axis=0, tiled=True)]
    ppermute x2, starting transfers between devices: 8.03 us -> 6.05 us  [swapped(): lax.ppermute(far, axis, pairs + [(b, a) for a, b in pairs])]
where the time goes in v6:
time: 99.8 us; the launch traced here: 99.5 us
  blocking collectives  85.4 us (86%)
  Pallas kernels  7.27 us (7%)
  starting transfers between devices  6.05 us (6%)
    all_to_all x3, blocking collectives, everywhere(): lax.all_to_all(copies, axes, split_axis=0, concat_axis=0, tiled=True)  65 us
    all_gather x1, blocking collectives, shards(): whole = lax.all_gather(block, PART)  10.7 us
    all_gather x2, blocking collectives, swapped(): lax.all_gather(near, axis[-1], tiled=True)  9.63 us
    pallas_call x6, Pallas kernels, call(): pl.pallas_call(kernel, out_shape=[results(s, jnp.float32) for s in out_sh...  6.27 us
    ppermute x2, starting transfers between devices, swapped(): lax.ppermute(far, axis, pairs + [(b, a) for a, b in pairs])  6.05 us
  transfers between devices with their start and end apart: 2, of which 0 were waited for; matrix products, arithmetic and copies ran while one was open for 0% of the time, Pallas kernels for 0%

profile of v6, /device:TPU:1, one launch (start us, length us, event | category | flops | bytes accessed | tf_op | source)
XLA Modules:
  0.0 99.5 jit_solution(12255223057431771081)
XLA Ops:
  0.6 1.0 %shard_map.59 = (f32[5,16,512]{2,1,0:T(8,128)S(1)}, f32[16,128]{1,0:T(8,128)S(1)}, f32[16,128]{1,0:T(8,128)S(1)}) custom-call(f32[16,512]{1,0:T(8,128)} %terminal.1, f32[16,512]{1,0:T(8,128)} %diagonal.1, f32[2,16,512]{2,1,0:T(8,128)} %guess.1, f32[16,512]{1,0:T(8,128)} %initial.1), custom_call_target="tpu_custom_call" | custom-call | tf_op jit(solution)/shard_map/pallas_call | solution.py:413
  1.6 5.4 %collective-permute-start = (f32[16,128]{1,0:T(8,128)S(1)}, f32[16,128]{1,0:T(8,128)S(1)}, u32[]{:S(2)}, u32[]{:S(2)}) collective-permute-start(f32[16,128]{1,0:T(8,128)S(1)} %get-tuple-element.20), channel_id=1, source_target_pairs={{1,2},{3,4},{5,6},{7,8},{9,10},{11,12},{13,14},{2,1},{4,3},{6,5},{... | collective-permute-start | bytes 24584 | tf_op jit(solution)/shard_map/ppermute | solution.py:393
  7.0 3.6 %all_gather.12.near_edge = f32[32,128]{1,0:T(8,128)S(1)} all-gather(f32[16,128]{1,0:T(8,128)S(1)} %get-tuple-element.21), channel_id=1, replica_groups=mesh['band_0'=4,'band_1'=2,'part'=4,'gy_0'=8,'gy_1'=2] {'gy_1'}, dimensions={0}, use_global_device_ids=true | all-gather | bytes 24576 | tf_op jit(solution)/shard_map/all_gather | solution.py:394
  10.6 0.0 collective-permute-done.far_edge
  10.6 10.7 %all-gather = f32[352,512]{1,0:T(8,128)S(1)} all-gather(f32[88,512]{1,0:T(8,128)S(1)} %shard_map.60), channel_id=2, replica_groups=mesh['band_0'=4,'band_1'=2,'part'=4,'gy_0'=8,'gy_1'=2] {'part'}, dimensions={0}, use_global_device_ids=true | all-gather | bytes 901120 | tf_op jit(solution)/shard_map/all_gather | solution.py:421
  21.4 0.7 collective-permute-start.1
  22.1 6.0 %all_gather.15.near_ref = f32[128,512]{1,0:T(8,128)S(1)} all-gather(f32[64,512]{1,0:T(8,128)S(1)} %get-tuple-element.23), channel_id=1, replica_groups=mesh['band_0'=4,'band_1'=2,'part'=4,'gy_0'=8,'gy_1'=2] {'band_1'}, dimensions={0}, use_global_device_ids=true | all-gather | bytes 393216 | tf_op jit(solution)/shard_map/all_gather | solution.py:394
  28.1 0.0 collective-permute-done.1.far_ref
  28.1 1.1 %shard_map.62 = (f32[3,96,640]{2,1,0:T(8,128)S(1)}, f32[96,640]{1,0:T(8,128)S(1)}, f32[96,640]{1,0:T(8,128)S(1)}, f32[80,640]{1,0:T(8,128)S(1)}, f32[1,128]{1,0:T(1,128)S(1)}) custom-call(f32[4,88,512]{2,1,0:T(8,128)S(1)} %bitcast.8, f32[64,512]{1,0:T(8,128)S(1)} %collective-permute-done.1.far_ref, f32[128,512]{1,0:T(8,128)S(1)} %all_gather.15.near_ref), custom_call_target="tpu_custom_call" | custom-call | tf_op jit(solution)/shard_map/pallas_call | solution.py:400
  29.3 31.5 %all_to_all.15 = f32[128,1,128]{2,1,0:T(1,128)S(1)} all-to-all(f32[128,1,128]{2,1,0:T(1,128)S(1)} %broadcast_in_dim.9), channel_id=1, replica_groups=mesh['band_0'=4,'band_1'=2,'part'=4,'gy_0'=8,'gy_1'=2] {'band_0','band_1..., dimensions={0} | all-to-all | bytes 131072 | tf_op jit(solution)/shard_map/all_to_all | solution.py:386
  60.8 1.1 %shard_map.63 = (f32[80,640]{1,0:T(8,128)S(1)}, f32[3,80,640]{2,1,0:T(8,128)S(1)}, f32[80,640]{1,0:T(8,128)S(1)}, f32[1,128]{1,0:T(1,128)S(1)}) custom-call(f32[128,128]{1,0:T(8,128)S(1)} %bitcast.10, f32[3,96,640]{2,1,0:T(8,128)S(1)} %get-tuple-element.25.last_ref, f32[96,640]{1,0:T(8,128)S(1)} %get-tuple-element.26.center_ref, ...), custom_call_target="tpu_custom_call" | custom-call | tf_op jit(solution)/shard_map/pallas_call | solution.py:400
  61.9 16.8 %all_to_all.16 = f32[128,1,128]{2,1,0:T(1,128)S(1)} all-to-all(f32[128,1,128]{2,1,0:T(1,128)S(1)} %broadcast_in_dim.10), channel_id=1, replica_groups=mesh['band_0'=4,'band_1'=2,'part'=4,'gy_0'=8,'gy_1'=2] {'band_0','band_1..., dimensions={0} | all-to-all | bytes 131072 | tf_op jit(solution)/shard_map/all_to_all | solution.py:386
  78.7 3.1 %shard_map.64 = (f32[64,512]{1,0:T(8,128)S(1)}, f32[9,64,512]{2,1,0:T(8,128)S(1)}, f32[1,128]{1,0:T(1,128)S(1)}) custom-call(f32[128,128]{1,0:T(8,128)S(1)} %bitcast.9, f32[3,80,640]{2,1,0:T(8,128)S(1)} %get-tuple-element.29.last_ref, f32[80,640]{1,0:T(8,128)S(1)} %get-tuple-element.30.center_ref, f32[80,640]{1,0:T(8,128)S(1)} %get-tuple-element.31.initial_ref, ...), custom_call_target="tpu_custom_call" | custom-call | tf_op jit(solution)/shard_map/pallas_call | solution.py:400
  81.9 16.8 %all_to_all.17 = f32[128,1,128]{2,1,0:T(1,128)S(1)} all-to-all(f32[128,1,128]{2,1,0:T(1,128)S(1)} %broadcast_in_dim.11), channel_id=1, replica_groups=mesh['band_0'=4,'band_1'=2,'part'=4,'gy_0'=8,'gy_1'=2] {'band_0','band_1..., dimensions={0} | all-to-all | bytes 131072 | tf_op jit(solution)/shard_map/all_to_all | solution.py:386
  98.6 0.9 shard_map.65
  (5 shorter events, 0.2 us)
Async XLA Ops:
  1.6 9.0 %collective-permute-start = (f32[16,128]{1,0:T(8,128)S(1)}, f32[16,128]{1,0:T(8,128)S(1)}, u32[]{:S(2)}, u32[]{:S(2)}) collective-permute-start(f32[16,128]{1,0:T(8,128)S(1)} %get-tuple-element.20), channel_id=1, source_target_pairs={{1,2},{3,4},{5,6},{7,8},{9,10},{11,12},{13,14},{2,1},{4,3},{6,5},{... | collective-permute-start | bytes 24584 | tf_op jit(solution)/shard_map/ppermute | solution.py:393
  21.4 6.7 %collective-permute-start.1 = (f32[64,512]{1,0:T(8,128)S(1)}, f32[64,512]{1,0:T(8,128)S(1)}, u32[]{:S(2)}, u32[]{:S(2)}) collective-permute-start(f32[64,512]{1,0:T(8,128)S(1)} %get-tuple-element.22), channel_id=1, source_target_pairs={{64,128},{192,256},{320,384},{128,64},{256,192},{384,320},{65,129}... | collective-permute-start | bytes 393224 | tf_op jit(solution)/shard_map/ppermute | solution.py:393

commit v7 on v6

--- a/solution.py
+++ b/solution.py
@@ -43,17 +43,38 @@
     return pltpu.roll(v, v.shape[dim] - 1, dim)
 
 
-def inside(rows, wide, first_row, own, grid):
-    nx, ny, local_x, local_y = grid
-    row = lax.broadcasted_iota(jnp.int32, (rows, wide), 0) + (lax.axis_index(BAND) * local_x + first_row)
-    lane = lax.broadcasted_iota(jnp.int32, (rows, wide), 1)
-    column = jnp.where(lane < own + HALF, lane, lane - wide) + lax.axis_index(GY) * local_y
-    return (row >= 0) & (row < nx) & (column >= 0) & (column < ny)
+def keeper(halo, x, own):
+    band, column = lax.axis_index(BAND), lax.axis_index(GY)
+    bands, columns = lax.axis_size(BAND), lax.axis_size(GY)
+    top = jnp.where(band > 0, 1.0, 0.0)
+    bottom = jnp.where(band < bands - 1, 1.0, 0.0)
+    lane = lax.broadcasted_iota(jnp.int32, (8, EDGE), 1)
+    edge = jnp.where(
+        lane < HALF, jnp.where(column < columns - 1, 1.0, 0.0), jnp.where(column > 0, 1.0, 0.0)
+    )
+
+    def tiled(rows):
+        return jnp.concatenate([edge] * (rows // 8), axis=0)
+
+    ends = tiled(halo)
+
+    def keep(v):
+        first, last = v[:halo], v[halo + x :]
+        inner_rows = v[halo : halo + x]
+        main = [first[:, :own] * top, inner_rows[:, :own], last[:, :own] * bottom]
+        side = [
+            first[:, own:] * (ends * top),
+            inner_rows[:, own:] * tiled(x),
+            last[:, own:] * (ends * bottom),
+        ]
+        return jnp.concatenate([jnp.concatenate(p, axis=0) for p in (main, side)], axis=1)
+
+    return keep
 
 
 def shifted(v, center, shift, keep):
     beside = (before(v, 0) + after(v, 0)) + (before(v, 1) + after(v, 1))
-    return jnp.where(keep, (center - shift) * v - beside, 0.0)
+    return keep((center - shift) * v - beside)
 
 
 def basis(v0, center, keep):
@@ -91,7 +112,7 @@
     flux_x = out_x * m + in_x * after(m, 0)
     flux_y = out_y * m + in_y * after(m, 1)
     div = (flux_x - before(flux_x, 0)) + (flux_y - before(flux_y, 1))
-    return jnp.where(keep, inv_step * m - div, 0.0)
+    return keep(inv_step * m - div)
 
 
 def dot(a, b):
@@ -255,7 +276,7 @@
     wide = own + EDGE
     rows = x + 2 * HALO
     parts = band_ref.shape[0]
-    keep = inside(rows, wide, -HALO, own, grid)
+    keep = keeper(HALO, x, own)
     odd = odd_index(BAND, (8, own))
 
     def tile(k, odd_from, odd_start, even_from, even_start):
@@ -302,7 +323,7 @@
     later = extended(TERMINAL)
     center = extended(DIAGONAL) + (inv_step + 4.0)
     rhs = inv_step * later - hamiltonian(later) + coupling * extended(GUESS + 1)
-    vs = basis(jnp.where(keep, rhs, 0.0), center, keep)
+    vs = basis(keep(rhs), center, keep)
     for k in range(3):
         basis_ref[k] = vs[k]
     center_ref[...] = center
@@ -315,7 +336,7 @@
 def second_kernel(grid, parts_ref, last_ref, center_ref, guess_ref, later_ref, basis_ref, inner_center, sums_ref):
     _, _, x, own = grid
     rows, wide = last_ref.shape[1:]
-    keep = inside(rows, wide, -HALO, own, grid)
+    keep = keeper(HALO, x, own)
     row = gathered_products(parts_ref)
     coefs = coefficients([entry(row, k) for k in range(len(PAIRS))])
     later = combined(coefs, [last_ref[k] for k in range(3)])
@@ -323,7 +344,7 @@
     center = center_ref[...]
     inner_center[...] = inner(center)
     rhs = inv_step * later - hamiltonian(later) + coupling * guess_ref[...]
-    vs = basis(jnp.where(keep, rhs, 0.0), center, keep)
+    vs = basis(keep(rhs), center, keep)
     for k in range(3):
         basis_ref[k] = inner(vs[k])
     mine = [middle(v, x, own) for v in vs]
@@ -333,7 +354,7 @@
 def third_kernel(grid, parts_ref, last_ref, center_ref, initial_ref, later_ref, value_ref, images_ref, sums_ref):
     _, _, x, own = grid
     rows, wide = last_ref.shape[1:]
-    keep = inside(rows, wide, -INNER, own, grid)
+    keep = keeper(INNER, x, own)
     row = gathered_products(parts_ref)
     coefs = coefficients([entry(row, k) for k in range(len(PAIRS))])
     value = combined(coefs, [last_ref[k] for k in range(3)])

time: 99.8 us -> 99.3 us (level)
  no operation moved by 1% of the time
where the time goes in v7:
time: 99.3 us; the launch traced here: 99 us
  blocking collectives  85.4 us (86%)
  Pallas kernels  6.76 us (7%)
  starting transfers between devices  6.05 us (6%)
    all_to_all x3, blocking collectives, everywhere(): lax.all_to_all(copies, axes, split_axis=0, concat_axis=0, tiled=True)  65 us
    all_gather x1, blocking collectives, shards(): whole = lax.all_gather(block, PART)  10.7 us
    all_gather x2, blocking collectives, swapped(): lax.all_gather(near, axis[-1], tiled=True)  9.63 us
    ppermute x2, starting transfers between devices, swapped(): lax.ppermute(far, axis, pairs + [(b, a) for a, b in pairs])  6.05 us
    pallas_call x6, Pallas kernels, call(): pl.pallas_call(kernel, out_shape=[results(s, jnp.float32) for s in out_sh...  5.76 us
  transfers between devices with their start and end apart: 2, of which 0 were waited for; matrix products, arithmetic and copies ran while one was open for 0% of the time, Pallas kernels for 0%

profile of v7, /device:TPU:1, one launch (start us, length us, event | category | flops | bytes accessed | tf_op | source)
XLA Modules:
  0.0 99.0 jit_solution(2024848033234000992)
XLA Ops:
  0.6 1.0 %shard_map.59 = (f32[5,16,512]{2,1,0:T(8,128)S(1)}, f32[16,128]{1,0:T(8,128)S(1)}, f32[16,128]{1,0:T(8,128)S(1)}) custom-call(f32[16,512]{1,0:T(8,128)} %terminal.1, f32[16,512]{1,0:T(8,128)} %diagonal.1, f32[2,16,512]{2,1,0:T(8,128)} %guess.1, f32[16,512]{1,0:T(8,128)} %initial.1), custom_call_target="tpu_custom_call" | custom-call | tf_op jit(solution)/shard_map/pallas_call | solution.py:434
  1.6 5.4 %collective-permute-start = (f32[16,128]{1,0:T(8,128)S(1)}, f32[16,128]{1,0:T(8,128)S(1)}, u32[]{:S(2)}, u32[]{:S(2)}) collective-permute-start(f32[16,128]{1,0:T(8,128)S(1)} %get-tuple-element.20), channel_id=1, source_target_pairs={{1,2},{3,4},{5,6},{7,8},{9,10},{11,12},{13,14},{2,1},{4,3},{6,5},{... | collective-permute-start | bytes 24584 | tf_op jit(solution)/shard_map/ppermute | solution.py:414
  7.0 3.6 %all_gather.12.near_edge = f32[32,128]{1,0:T(8,128)S(1)} all-gather(f32[16,128]{1,0:T(8,128)S(1)} %get-tuple-element.21), channel_id=1, replica_groups=mesh['band_0'=4,'band_1'=2,'part'=4,'gy_0'=8,'gy_1'=2] {'gy_1'}, dimensions={0}, use_global_device_ids=true | all-gather | bytes 24576 | tf_op jit(solution)/shard_map/all_gather | solution.py:415
  10.6 0.0 collective-permute-done.far_edge
  10.6 10.7 %all-gather = f32[352,512]{1,0:T(8,128)S(1)} all-gather(f32[88,512]{1,0:T(8,128)S(1)} %shard_map.60), channel_id=2, replica_groups=mesh['band_0'=4,'band_1'=2,'part'=4,'gy_0'=8,'gy_1'=2] {'part'}, dimensions={0}, use_global_device_ids=true | all-gather | bytes 901120 | tf_op jit(solution)/shard_map/all_gather | solution.py:442
  21.4 0.7 collective-permute-start.1
  22.1 6.0 %all_gather.15.near_ref = f32[128,512]{1,0:T(8,128)S(1)} all-gather(f32[64,512]{1,0:T(8,128)S(1)} %get-tuple-element.23), channel_id=1, replica_groups=mesh['band_0'=4,'band_1'=2,'part'=4,'gy_0'=8,'gy_1'=2] {'band_1'}, dimensions={0}, use_global_device_ids=true | all-gather | bytes 393216 | tf_op jit(solution)/shard_map/all_gather | solution.py:415
  28.1 0.0 collective-permute-done.1.far_ref
  28.1 1.0 shard_map.62
  29.2 31.5 %all_to_all.15 = f32[128,1,128]{2,1,0:T(1,128)S(1)} all-to-all(f32[128,1,128]{2,1,0:T(1,128)S(1)} %broadcast_in_dim.9), channel_id=1, replica_groups=mesh['band_0'=4,'band_1'=2,'part'=4,'gy_0'=8,'gy_1'=2] {'band_0','band_1..., dimensions={0} | all-to-all | bytes 131072 | tf_op jit(solution)/shard_map/all_to_all | solution.py:407
  60.6 1.0 %shard_map.63 = (f32[80,640]{1,0:T(8,128)S(1)}, f32[3,80,640]{2,1,0:T(8,128)S(1)}, f32[80,640]{1,0:T(8,128)S(1)}, f32[1,128]{1,0:T(1,128)S(1)}) custom-call(f32[128,128]{1,0:T(8,128)S(1)} %bitcast.10, f32[3,96,640]{2,1,0:T(8,128)S(1)} %get-tuple-element.25.last_ref, f32[96,640]{1,0:T(8,128)S(1)} %get-tuple-element.26.center_ref, ...), custom_call_target="tpu_custom_call" | custom-call | tf_op jit(solution)/shard_map/pallas_call | solution.py:421
  61.7 16.8 %all_to_all.16 = f32[128,1,128]{2,1,0:T(1,128)S(1)} all-to-all(f32[128,1,128]{2,1,0:T(1,128)S(1)} %broadcast_in_dim.10), channel_id=1, replica_groups=mesh['band_0'=4,'band_1'=2,'part'=4,'gy_0'=8,'gy_1'=2] {'band_0','band_1..., dimensions={0} | all-to-all | bytes 131072 | tf_op jit(solution)/shard_map/all_to_all | solution.py:407
  78.5 2.8 %shard_map.64 = (f32[64,512]{1,0:T(8,128)S(1)}, f32[9,64,512]{2,1,0:T(8,128)S(1)}, f32[1,128]{1,0:T(1,128)S(1)}) custom-call(f32[128,128]{1,0:T(8,128)S(1)} %bitcast.9, f32[3,80,640]{2,1,0:T(8,128)S(1)} %get-tuple-element.29.last_ref, f32[80,640]{1,0:T(8,128)S(1)} %get-tuple-element.30.center_ref, f32[80,640]{1,0:T(8,128)S(1)} %get-tuple-element.31.initial_ref, ...), custom_call_target="tpu_custom_call" | custom-call | tf_op jit(solution)/shard_map/pallas_call | solution.py:421
  81.3 16.8 %all_to_all.17 = f32[128,1,128]{2,1,0:T(1,128)S(1)} all-to-all(f32[128,1,128]{2,1,0:T(1,128)S(1)} %broadcast_in_dim.11), channel_id=1, replica_groups=mesh['band_0'=4,'band_1'=2,'part'=4,'gy_0'=8,'gy_1'=2] {'band_0','band_1..., dimensions={0} | all-to-all | bytes 131072 | tf_op jit(solution)/shard_map/all_to_all | solution.py:407
  98.1 0.9 shard_map.65
  (5 shorter events, 0.2 us)
Async XLA Ops:
  1.6 9.0 %collective-permute-start = (f32[16,128]{1,0:T(8,128)S(1)}, f32[16,128]{1,0:T(8,128)S(1)}, u32[]{:S(2)}, u32[]{:S(2)}) collective-permute-start(f32[16,128]{1,0:T(8,128)S(1)} %get-tuple-element.20), channel_id=1, source_target_pairs={{1,2},{3,4},{5,6},{7,8},{9,10},{11,12},{13,14},{2,1},{4,3},{6,5},{... | collective-permute-start | bytes 24584 | tf_op jit(solution)/shard_map/ppermute | solution.py:414
  21.4 6.7 %collective-permute-start.1 = (f32[64,512]{1,0:T(8,128)S(1)}, f32[64,512]{1,0:T(8,128)S(1)}, u32[]{:S(2)}, u32[]{:S(2)}) collective-permute-start(f32[64,512]{1,0:T(8,128)S(1)} %get-tuple-element.22), channel_id=1, source_target_pairs={{64,128},{192,256},{320,384},{128,64},{256,192},{384,320},{65,129}... | collective-permute-start | bytes 393224 | tf_op jit(solution)/shard_map/ppermute | solution.py:414

commit v8 on v7

--- a/solution.py
+++ b/solution.py
@@ -238,10 +238,11 @@
     odd = odd_index(GY, (x, EDGE))
     left = jnp.where(odd, near_edge[:x, :], far_edge[...])
     right = jnp.where(odd, far_edge[...], near_edge[x:, :])
-    for k in range(FIELDS):
-        block_ref[x * k : x * (k + 1), :] = fields_ref[k]
-    edges = [right[:8], left[:8], right[8:], left[8:]]
-    block_ref[x * FIELDS :, :] = jnp.concatenate(edges, axis=1)
+    edges = jnp.concatenate([right[:8], left[:8], right[8:], left[8:]], axis=1)
+    for part in range(block_ref.shape[0]):
+        for k in range(FIELDS):
+            block_ref[part, x * k : x * (k + 1), :] = fields_ref[k]
+        block_ref[part, x * FIELDS :, :] = edges
 
 
 def row_kernel(band_ref, far_ref, near_ref):
@@ -438,8 +439,9 @@
         out_specs=[pl.BlockSpec(memory_space=pltpu.VMEM)] * 3,
         scratch_shapes=[pltpu.SemaphoreType.DMA((4,))],
     )(terminal, diagonal, density_guess, initial_density)
-    (block,) = call(edge_kernel, [(x * FIELDS + 8, own)], fields, *swapped(far, near, GY))
-    whole = lax.all_gather(block, PART)
+    copies = (lax.axis_size(PART), x * FIELDS + 8, own)
+    (blocks,) = call(edge_kernel, [copies], fields, *swapped(far, near, GY))
+    whole = lax.all_to_all(blocks, PART, split_axis=0, concat_axis=0, tiled=True)
     packed = (8 * SENT, own)
     far, near = call(row_kernel, [packed, packed], whole)
     rows = band + 2 * HALO

time: 99.3 us -> 101 us (1.017)
  blocking collectives: 85.4 us -> 86.5 us
    all_to_all x0 -> x1, blocking collectives: none -> 13.4 us  [shards(): lax.all_to_all(blocks, PART, split_axis=0, concat_axis=0, tiled=True)]
    all_gather x1 -> x0, blocking collectives: 10.7 us -> none  [shards(): whole = lax.all_gather(block, PART)]
    all_to_all x3, blocking collectives: 65 us -> 63.1 us  [everywhere(): lax.all_to_all(copies, axes, split_axis=0, concat_axis=0, tiled=True)]
where the time goes in v8:
time: 101 us; the launch traced here: 100 us
  blocking collectives  86.5 us (86%)
  Pallas kernels  6.79 us (7%)
  starting transfers between devices  6.05 us (6%)
    all_to_all x3, blocking collectives, everywhere(): lax.all_to_all(copies, axes, split_axis=0, concat_axis=0, tiled=True)  63.1 us
    all_to_all x1, blocking collectives, shards(): lax.all_to_all(blocks, PART, split_axis=0, concat_axis=0, tiled=True)  13.4 us
    all_gather x2, blocking collectives, swapped(): lax.all_gather(near, axis[-1], tiled=True)  10 us
    ppermute x2, starting transfers between devices, swapped(): lax.ppermute(far, axis, pairs + [(b, a) for a, b in pairs])  6.05 us
    pallas_call x6, Pallas kernels, call(): pl.pallas_call(kernel, out_shape=[results(s, jnp.float32) for s in out_sh...  5.79 us
  transfers between devices with their start and end apart: 2, of which 0 were waited for; matrix products, arithmetic and copies ran while one was open for 0% of the time, Pallas kernels for 0%

profile of v8, /device:TPU:1, one launch (start us, length us, event | category | flops | bytes accessed | tf_op | source)
XLA Modules:
  0.0 100.2 jit_solution(9023303933842002249)
XLA Ops:
  0.6 1.0 %shard_map.59 = (f32[5,16,512]{2,1,0:T(8,128)S(1)}, f32[16,128]{1,0:T(8,128)S(1)}, f32[16,128]{1,0:T(8,128)S(1)}) custom-call(f32[16,512]{1,0:T(8,128)} %terminal.1, f32[16,512]{1,0:T(8,128)} %diagonal.1, f32[2,16,512]{2,1,0:T(8,128)} %guess.1, f32[16,512]{1,0:T(8,128)} %initial.1), custom_call_target="tpu_custom_call" | custom-call | tf_op jit(solution)/shard_map/pallas_call | solution.py:435
  1.6 5.4 %collective-permute-start = (f32[16,128]{1,0:T(8,128)S(1)}, f32[16,128]{1,0:T(8,128)S(1)}, u32[]{:S(2)}, u32[]{:S(2)}) collective-permute-start(f32[16,128]{1,0:T(8,128)S(1)} %get-tuple-element.20), channel_id=1, source_target_pairs={{1,2},{3,4},{5,6},{7,8},{9,10},{11,12},{13,14},{2,1},{4,3},{6,5},{... | collective-permute-start | bytes 24584 | tf_op jit(solution)/shard_map/ppermute | solution.py:415
  7.0 3.6 %all_gather.6.near_edge = f32[32,128]{1,0:T(8,128)S(1)} all-gather(f32[16,128]{1,0:T(8,128)S(1)} %get-tuple-element.21), channel_id=1, replica_groups=mesh['band_0'=4,'band_1'=2,'part'=4,'gy_0'=8,'gy_1'=2] {'gy_1'}, dimensions={0}, use_global_device_ids=true | all-gather | bytes 24576 | tf_op jit(solution)/shard_map/all_gather | solution.py:416
  10.6 0.0 collective-permute-done.far_edge
  10.7 13.4 %all_to_all.20.band_ref = f32[4,88,512]{2,1,0:T(8,128)S(1)} all-to-all(f32[4,88,512]{2,1,0:T(8,128)S(1)} %shard_map.60), channel_id=1, replica_groups=mesh['band_0'=4,'band_1'=2,'part'=4,'gy_0'=8,'gy_1'=2] {'part'}, dimensions={0} | all-to-all | bytes 1441792 | tf_op jit(solution)/shard_map/all_to_all | solution.py:444
  24.1 0.7 collective-permute-start.1
  24.8 6.4 %all_gather.7.near_ref = f32[128,512]{1,0:T(8,128)S(1)} all-gather(f32[64,512]{1,0:T(8,128)S(1)} %get-tuple-element.23), channel_id=1, replica_groups=mesh['band_0'=4,'band_1'=2,'part'=4,'gy_0'=8,'gy_1'=2] {'band_1'}, dimensions={0}, use_global_device_ids=true | all-gather | bytes 393216 | tf_op jit(solution)/shard_map/all_gather | solution.py:416
  31.2 0.0 collective-permute-done.1.far_ref
  31.2 1.0 shard_map.62
  32.3 29.6 %all_to_all.21 = f32[128,1,128]{2,1,0:T(1,128)S(1)} all-to-all(f32[128,1,128]{2,1,0:T(1,128)S(1)} %broadcast_in_dim.9), channel_id=1, replica_groups=mesh['band_0'=4,'band_1'=2,'part'=4,'gy_0'=8,'gy_1'=2] {'band_0','band_1..., dimensions={0} | all-to-all | bytes 131072 | tf_op jit(solution)/shard_map/all_to_all | solution.py:408
  61.8 1.0 %shard_map.63 = (f32[80,640]{1,0:T(8,128)S(1)}, f32[3,80,640]{2,1,0:T(8,128)S(1)}, f32[80,640]{1,0:T(8,128)S(1)}, f32[1,128]{1,0:T(1,128)S(1)}) custom-call(f32[128,128]{1,0:T(8,128)S(1)} %bitcast.7, f32[3,96,640]{2,1,0:T(8,128)S(1)} %get-tuple-element.25.last_ref, f32[96,640]{1,0:T(8,128)S(1)} %get-tuple-element.26.center_ref, ...), custom_call_target="tpu_custom_call" | custom-call | tf_op jit(solution)/shard_map/pallas_call | solution.py:422
  62.9 16.8 %all_to_all.22 = f32[128,1,128]{2,1,0:T(1,128)S(1)} all-to-all(f32[128,1,128]{2,1,0:T(1,128)S(1)} %broadcast_in_dim.10), channel_id=1, replica_groups=mesh['band_0'=4,'band_1'=2,'part'=4,'gy_0'=8,'gy_1'=2] {'band_0','band_1..., dimensions={0} | all-to-all | bytes 131072 | tf_op jit(solution)/shard_map/all_to_all | solution.py:408
  79.7 2.8 %shard_map.64 = (f32[64,512]{1,0:T(8,128)S(1)}, f32[9,64,512]{2,1,0:T(8,128)S(1)}, f32[1,128]{1,0:T(1,128)S(1)}) custom-call(f32[128,128]{1,0:T(8,128)S(1)} %bitcast.6, f32[3,80,640]{2,1,0:T(8,128)S(1)} %get-tuple-element.29.last_ref, f32[80,640]{1,0:T(8,128)S(1)} %get-tuple-element.30.center_ref, f32[80,640]{1,0:T(8,128)S(1)} %get-tuple-element.31.initial_ref, ...), custom_call_target="tpu_custom_call" | custom-call | tf_op jit(solution)/shard_map/pallas_call | solution.py:422
  82.5 16.8 %all_to_all.23 = f32[128,1,128]{2,1,0:T(1,128)S(1)} all-to-all(f32[128,1,128]{2,1,0:T(1,128)S(1)} %broadcast_in_dim.11), channel_id=1, replica_groups=mesh['band_0'=4,'band_1'=2,'part'=4,'gy_0'=8,'gy_1'=2] {'band_0','band_1..., dimensions={0} | all-to-all | bytes 131072 | tf_op jit(solution)/shard_map/all_to_all | solution.py:408
  99.3 0.9 shard_map.65
  (5 shorter events, 0.2 us)
Async XLA Ops:
  1.6 9.0 %collective-permute-start = (f32[16,128]{1,0:T(8,128)S(1)}, f32[16,128]{1,0:T(8,128)S(1)}, u32[]{:S(2)}, u32[]{:S(2)}) collective-permute-start(f32[16,128]{1,0:T(8,128)S(1)} %get-tuple-element.20), channel_id=1, source_target_pairs={{1,2},{3,4},{5,6},{7,8},{9,10},{11,12},{13,14},{2,1},{4,3},{6,5},{... | collective-permute-start | bytes 24584 | tf_op jit(solution)/shard_map/ppermute | solution.py:415
  24.1 7.1 %collective-permute-start.1 = (f32[64,512]{1,0:T(8,128)S(1)}, f32[64,512]{1,0:T(8,128)S(1)}, u32[]{:S(2)}, u32[]{:S(2)}) collective-permute-start(f32[64,512]{1,0:T(8,128)S(1)} %get-tuple-element.22), channel_id=1, source_target_pairs={{64,128},{192,256},{320,384},{128,64},{256,192},{384,320},{65,129}... | collective-permute-start | bytes 393224 | tf_op jit(solution)/shard_map/ppermute | solution.py:415

commit v9 on v7

--- a/solution.py
+++ b/solution.py
@@ -239,9 +239,10 @@
     left = jnp.where(odd, near_edge[:x, :], far_edge[...])
     right = jnp.where(odd, far_edge[...], near_edge[x:, :])
     for k in range(FIELDS):
-        block_ref[x * k : x * (k + 1), :] = fields_ref[k]
+        block_ref[2 * k] = fields_ref[k, :8, :]
+        block_ref[2 * k + 1] = fields_ref[k, 8:, :]
     edges = [right[:8], left[:8], right[8:], left[8:]]
-    block_ref[x * FIELDS :, :] = jnp.concatenate(edges, axis=1)
+    block_ref[2 * FIELDS] = jnp.concatenate(edges, axis=1)
 
 
 def row_kernel(band_ref, far_ref, near_ref):
@@ -438,8 +439,8 @@
         out_specs=[pl.BlockSpec(memory_space=pltpu.VMEM)] * 3,
         scratch_shapes=[pltpu.SemaphoreType.DMA((4,))],
     )(terminal, diagonal, density_guess, initial_density)
-    (block,) = call(edge_kernel, [(x * FIELDS + 8, own)], fields, *swapped(far, near, GY))
-    whole = lax.all_gather(block, PART)
+    (block,) = call(edge_kernel, [(2 * FIELDS + 1, 8, own)], fields, *swapped(far, near, GY))
+    whole = lax.all_gather(block, PART).reshape(-1, x * FIELDS + 8, own)
     packed = (8 * SENT, own)
     far, near = call(row_kernel, [packed, packed], whole)
     rows = band + 2 * HALO

time: 99.3 us -> 99.3 us (level)
  no operation moved by 1% of the time
where the time goes in v9:
time: 99.3 us; the launch traced here: 99 us
  blocking collectives  85.4 us (86%)
  Pallas kernels  6.76 us (7%)
  starting transfers between devices  6.05 us (6%)
    all_to_all x3, blocking collectives, everywhere(): lax.all_to_all(copies, axes, split_axis=0, concat_axis=0, tiled=True)  65 us
    all_gather x1, blocking collectives, shards(): whole = lax.all_gather(block, PART).reshape(-1, x * FIELDS + 8, own)  10.7 us
    all_gather x2, blocking collectives, swapped(): lax.all_gather(near, axis[-1], tiled=True)  9.63 us
    ppermute x2, starting transfers between devices, swapped(): lax.ppermute(far, axis, pairs + [(b, a) for a, b in pairs])  6.05 us
    pallas_call x6, Pallas kernels, call(): pl.pallas_call(kernel, out_shape=[results(s, jnp.float32) for s in out_sh...  5.76 us
  transfers between devices with their start and end apart: 2, of which 0 were waited for; matrix products, arithmetic and copies ran while one was open for 0% of the time, Pallas kernels for 0%

profile of v9, /device:TPU:1, one launch (start us, length us, event | category | flops | bytes accessed | tf_op | source)
XLA Modules:
  0.0 99.0 jit_solution(16184932862459124092)
XLA Ops:
  0.6 1.0 %shard_map.59 = (f32[5,16,512]{2,1,0:T(8,128)S(1)}, f32[16,128]{1,0:T(8,128)S(1)}, f32[16,128]{1,0:T(8,128)S(1)}) custom-call(f32[16,512]{1,0:T(8,128)} %terminal.1, f32[16,512]{1,0:T(8,128)} %diagonal.1, f32[2,16,512]{2,1,0:T(8,128)} %guess.1, f32[16,512]{1,0:T(8,128)} %initial.1), custom_call_target="tpu_custom_call" | custom-call | tf_op jit(solution)/shard_map/pallas_call | solution.py:435
  1.6 5.4 %collective-permute-start = (f32[16,128]{1,0:T(8,128)S(1)}, f32[16,128]{1,0:T(8,128)S(1)}, u32[]{:S(2)}, u32[]{:S(2)}) collective-permute-start(f32[16,128]{1,0:T(8,128)S(1)} %get-tuple-element.20), channel_id=1, source_target_pairs={{1,2},{3,4},{5,6},{7,8},{9,10},{11,12},{13,14},{2,1},{4,3},{6,5},{... | collective-permute-start | bytes 24584 | tf_op jit(solution)/shard_map/ppermute | solution.py:415
  7.0 3.6 %all_gather.12.near_edge = f32[32,128]{1,0:T(8,128)S(1)} all-gather(f32[16,128]{1,0:T(8,128)S(1)} %get-tuple-element.21), channel_id=1, replica_groups=mesh['band_0'=4,'band_1'=2,'part'=4,'gy_0'=8,'gy_1'=2] {'gy_1'}, dimensions={0}, use_global_device_ids=true | all-gather | bytes 24576 | tf_op jit(solution)/shard_map/all_gather | solution.py:416
  10.6 0.0 collective-permute-done.far_edge
  10.6 10.7 %all-gather = f32[44,8,512]{2,1,0:T(8,128)S(1)} all-gather(f32[11,8,512]{2,1,0:T(8,128)S(1)} %shard_map.60), channel_id=2, replica_groups=mesh['band_0'=4,'band_1'=2,'part'=4,'gy_0'=8,'gy_1'=2] {'part'}, dimensions={0}, use_global_device_ids=true | all-gather | bytes 901120 | tf_op jit(solution)/shard_map/all_gather | solution.py:443
  21.4 0.7 collective-permute-start.1
  22.1 6.0 %all_gather.15.near_ref = f32[128,512]{1,0:T(8,128)S(1)} all-gather(f32[64,512]{1,0:T(8,128)S(1)} %get-tuple-element.23), channel_id=1, replica_groups=mesh['band_0'=4,'band_1'=2,'part'=4,'gy_0'=8,'gy_1'=2] {'band_1'}, dimensions={0}, use_global_device_ids=true | all-gather | bytes 393216 | tf_op jit(solution)/shard_map/all_gather | solution.py:416
  28.1 0.0 collective-permute-done.1.far_ref
  28.1 1.0 shard_map.62
  29.2 31.5 %all_to_all.15 = f32[128,1,128]{2,1,0:T(1,128)S(1)} all-to-all(f32[128,1,128]{2,1,0:T(1,128)S(1)} %broadcast_in_dim.9), channel_id=1, replica_groups=mesh['band_0'=4,'band_1'=2,'part'=4,'gy_0'=8,'gy_1'=2] {'band_0','band_1..., dimensions={0} | all-to-all | bytes 131072 | tf_op jit(solution)/shard_map/all_to_all | solution.py:408
  60.6 1.0 %shard_map.63 = (f32[80,640]{1,0:T(8,128)S(1)}, f32[3,80,640]{2,1,0:T(8,128)S(1)}, f32[80,640]{1,0:T(8,128)S(1)}, f32[1,128]{1,0:T(1,128)S(1)}) custom-call(f32[128,128]{1,0:T(8,128)S(1)} %bitcast.10, f32[3,96,640]{2,1,0:T(8,128)S(1)} %get-tuple-element.25.last_ref, f32[96,640]{1,0:T(8,128)S(1)} %get-tuple-element.26.center_ref, ...), custom_call_target="tpu_custom_call" | custom-call | tf_op jit(solution)/shard_map/pallas_call | solution.py:422
  61.7 16.8 %all_to_all.16 = f32[128,1,128]{2,1,0:T(1,128)S(1)} all-to-all(f32[128,1,128]{2,1,0:T(1,128)S(1)} %broadcast_in_dim.10), channel_id=1, replica_groups=mesh['band_0'=4,'band_1'=2,'part'=4,'gy_0'=8,'gy_1'=2] {'band_0','band_1..., dimensions={0} | all-to-all | bytes 131072 | tf_op jit(solution)/shard_map/all_to_all | solution.py:408
  78.5 2.8 %shard_map.64 = (f32[64,512]{1,0:T(8,128)S(1)}, f32[9,64,512]{2,1,0:T(8,128)S(1)}, f32[1,128]{1,0:T(1,128)S(1)}) custom-call(f32[128,128]{1,0:T(8,128)S(1)} %bitcast.9, f32[3,80,640]{2,1,0:T(8,128)S(1)} %get-tuple-element.29.last_ref, f32[80,640]{1,0:T(8,128)S(1)} %get-tuple-element.30.center_ref, f32[80,640]{1,0:T(8,128)S(1)} %get-tuple-element.31.initial_ref, ...), custom_call_target="tpu_custom_call" | custom-call | tf_op jit(solution)/shard_map/pallas_call | solution.py:422
  81.3 16.8 %all_to_all.17 = f32[128,1,128]{2,1,0:T(1,128)S(1)} all-to-all(f32[128,1,128]{2,1,0:T(1,128)S(1)} %broadcast_in_dim.11), channel_id=1, replica_groups=mesh['band_0'=4,'band_1'=2,'part'=4,'gy_0'=8,'gy_1'=2] {'band_0','band_1..., dimensions={0} | all-to-all | bytes 131072 | tf_op jit(solution)/shard_map/all_to_all | solution.py:408
  98.1 0.9 shard_map.65
  (5 shorter events, 0.2 us)
Async XLA Ops:
  1.6 9.0 %collective-permute-start = (f32[16,128]{1,0:T(8,128)S(1)}, f32[16,128]{1,0:T(8,128)S(1)}, u32[]{:S(2)}, u32[]{:S(2)}) collective-permute-start(f32[16,128]{1,0:T(8,128)S(1)} %get-tuple-element.20), channel_id=1, source_target_pairs={{1,2},{3,4},{5,6},{7,8},{9,10},{11,12},{13,14},{2,1},{4,3},{6,5},{... | collective-permute-start | bytes 24584 | tf_op jit(solution)/shard_map/ppermute | solution.py:415
  21.4 6.7 %collective-permute-start.1 = (f32[64,512]{1,0:T(8,128)S(1)}, f32[64,512]{1,0:T(8,128)S(1)}, u32[]{:S(2)}, u32[]{:S(2)}) collective-permute-start(f32[64,512]{1,0:T(8,128)S(1)} %get-tuple-element.22), channel_id=1, source_target_pairs={{64,128},{192,256},{320,384},{128,64},{256,192},{384,320},{65,129}... | collective-permute-start | bytes 393224 | tf_op jit(solution)/shard_map/ppermute | solution.py:415

commit v10 on v7

--- a/solution.py
+++ b/solution.py
@@ -84,16 +84,12 @@
 
 
 def hamiltonian(u):
-    ahead_x = after(u, 0) - u
-    back_x = u - before(u, 0)
-    ahead_y = after(u, 1) - u
-    back_y = u - before(u, 1)
-    return 0.5 * (
-        jnp.maximum(back_x, 0.0) ** 2
-        + jnp.minimum(ahead_x, 0.0) ** 2
-        + jnp.maximum(back_y, 0.0) ** 2
-        + jnp.minimum(ahead_y, 0.0) ** 2
-    )
+    total = None
+    for dim in (0, 1):
+        ahead = after(u, dim) - u
+        term = before(jnp.maximum(ahead, 0.0) ** 2, dim) + jnp.minimum(ahead, 0.0) ** 2
+        total = term if total is None else total + term
+    return 0.5 * total
 
 
 def drift(u):
@@ -119,15 +115,15 @@
     rows, wide = a.shape
     total = jnp.sum((a * b).reshape(rows // 8, 8, wide), axis=0)
     total = sum(total[:, k : k + 128] for k in range(128, wide, 128)) + total[:, :128]
-    return jnp.sum(jnp.sum(total, axis=1, keepdims=True), axis=0, keepdims=True)
+    return jnp.sum(total, axis=1, keepdims=True)
 
 
 def row_of(values):
-    lane = lax.broadcasted_iota(jnp.int32, (1, 128), 1)
-    row = jnp.zeros((1, 128), jnp.float32)
+    lane = lax.broadcasted_iota(jnp.int32, (8, 128), 1)
+    rows = jnp.zeros((8, 128), jnp.float32)
     for place, value in values:
-        row = jnp.where(lane == place, value, row)
-    return row
+        rows = jnp.where(lane == place, value, rows)
+    return jnp.sum(rows, axis=0, keepdims=True)
 
 
 def entry(row, place):

time: 99.3 us -> 99.3 us (level)
  no operation moved by 1% of the time
where the time goes in v10:
time: 99.3 us; the launch traced here: 99 us
  blocking collectives  85.4 us (86%)
  Pallas kernels  6.72 us (7%)
  starting transfers between devices  6.05 us (6%)
    all_to_all x3, blocking collectives, everywhere(): lax.all_to_all(copies, axes, split_axis=0, concat_axis=0, tiled=True)  65 us
    all_gather x1, blocking collectives, shards(): whole = lax.all_gather(block, PART)  10.7 us
    all_gather x2, blocking collectives, swapped(): lax.all_gather(near, axis[-1], tiled=True)  9.63 us
    ppermute x2, starting transfers between devices, swapped(): lax.ppermute(far, axis, pairs + [(b, a) for a, b in pairs])  6.05 us
    pallas_call x6, Pallas kernels, call(): pl.pallas_call(kernel, out_shape=[results(s, jnp.float32) for s in out_sh...  5.72 us
  transfers between devices with their start and end apart: 2, of which 0 were waited for; matrix products, arithmetic and copies ran while one was open for 0% of the time, Pallas kernels for 0%

profile of v10, /device:TPU:1, one launch (start us, length us, event | category | flops | bytes accessed | tf_op | source)
XLA Modules:
  0.0 99.0 jit_solution(796804946617633828)
XLA Ops:
  0.6 1.0 %shard_map.59 = (f32[5,16,512]{2,1,0:T(8,128)S(1)}, f32[16,128]{1,0:T(8,128)S(1)}, f32[16,128]{1,0:T(8,128)S(1)}) custom-call(f32[16,512]{1,0:T(8,128)} %terminal.1, f32[16,512]{1,0:T(8,128)} %diagonal.1, f32[2,16,512]{2,1,0:T(8,128)} %guess.1, f32[16,512]{1,0:T(8,128)} %initial.1), custom_call_target="tpu_custom_call" | custom-call | tf_op jit(solution)/shard_map/pallas_call | solution.py:430
  1.6 5.4 %collective-permute-start = (f32[16,128]{1,0:T(8,128)S(1)}, f32[16,128]{1,0:T(8,128)S(1)}, u32[]{:S(2)}, u32[]{:S(2)}) collective-permute-start(f32[16,128]{1,0:T(8,128)S(1)} %get-tuple-element.20), channel_id=1, source_target_pairs={{1,2},{3,4},{5,6},{7,8},{9,10},{11,12},{13,14},{2,1},{4,3},{6,5},{... | collective-permute-start | bytes 24584 | tf_op jit(solution)/shard_map/ppermute | solution.py:410
  7.0 3.6 %all_gather.12.near_edge = f32[32,128]{1,0:T(8,128)S(1)} all-gather(f32[16,128]{1,0:T(8,128)S(1)} %get-tuple-element.21), channel_id=1, replica_groups=mesh['band_0'=4,'band_1'=2,'part'=4,'gy_0'=8,'gy_1'=2] {'gy_1'}, dimensions={0}, use_global_device_ids=true | all-gather | bytes 24576 | tf_op jit(solution)/shard_map/all_gather | solution.py:411
  10.6 0.0 collective-permute-done.far_edge
  10.6 10.7 %all-gather = f32[352,512]{1,0:T(8,128)S(1)} all-gather(f32[88,512]{1,0:T(8,128)S(1)} %shard_map.60), channel_id=2, replica_groups=mesh['band_0'=4,'band_1'=2,'part'=4,'gy_0'=8,'gy_1'=2] {'part'}, dimensions={0}, use_global_device_ids=true | all-gather | bytes 901120 | tf_op jit(solution)/shard_map/all_gather | solution.py:438
  21.4 0.7 collective-permute-start.1
  22.1 6.0 %all_gather.15.near_ref = f32[128,512]{1,0:T(8,128)S(1)} all-gather(f32[64,512]{1,0:T(8,128)S(1)} %get-tuple-element.23), channel_id=1, replica_groups=mesh['band_0'=4,'band_1'=2,'part'=4,'gy_0'=8,'gy_1'=2] {'band_1'}, dimensions={0}, use_global_device_ids=true | all-gather | bytes 393216 | tf_op jit(solution)/shard_map/all_gather | solution.py:411
  28.1 0.0 collective-permute-done.1.far_ref
  28.1 1.0 shard_map.62
  29.2 31.5 %all_to_all.15 = f32[128,1,128]{2,1,0:T(1,128)S(1)} all-to-all(f32[128,1,128]{2,1,0:T(1,128)S(1)} %broadcast_in_dim.9), channel_id=1, replica_groups=mesh['band_0'=4,'band_1'=2,'part'=4,'gy_0'=8,'gy_1'=2] {'band_0','band_1..., dimensions={0} | all-to-all | bytes 131072 | tf_op jit(solution)/shard_map/all_to_all | solution.py:403
  60.6 1.0 shard_map.63
  61.7 16.8 %all_to_all.16 = f32[128,1,128]{2,1,0:T(1,128)S(1)} all-to-all(f32[128,1,128]{2,1,0:T(1,128)S(1)} %broadcast_in_dim.10), channel_id=1, replica_groups=mesh['band_0'=4,'band_1'=2,'part'=4,'gy_0'=8,'gy_1'=2] {'band_0','band_1..., dimensions={0} | all-to-all | bytes 131072 | tf_op jit(solution)/shard_map/all_to_all | solution.py:403
  78.4 2.8 %shard_map.64 = (f32[64,512]{1,0:T(8,128)S(1)}, f32[9,64,512]{2,1,0:T(8,128)S(1)}, f32[1,128]{1,0:T(1,128)S(1)}) custom-call(f32[128,128]{1,0:T(8,128)S(1)} %bitcast.9, f32[3,80,640]{2,1,0:T(8,128)S(1)} %get-tuple-element.29.last_ref, f32[80,640]{1,0:T(8,128)S(1)} %get-tuple-element.30.center_ref, f32[80,640]{1,0:T(8,128)S(1)} %get-tuple-element.31.initial_ref, ...), custom_call_target="tpu_custom_call" | custom-call | tf_op jit(solution)/shard_map/pallas_call | solution.py:417
  81.3 16.8 %all_to_all.17 = f32[128,1,128]{2,1,0:T(1,128)S(1)} all-to-all(f32[128,1,128]{2,1,0:T(1,128)S(1)} %broadcast_in_dim.11), channel_id=1, replica_groups=mesh['band_0'=4,'band_1'=2,'part'=4,'gy_0'=8,'gy_1'=2] {'band_0','band_1..., dimensions={0} | all-to-all | bytes 131072 | tf_op jit(solution)/shard_map/all_to_all | solution.py:403
  98.1 0.9 shard_map.65
  (5 shorter events, 0.2 us)
Async XLA Ops:
  1.6 9.0 %collective-permute-start = (f32[16,128]{1,0:T(8,128)S(1)}, f32[16,128]{1,0:T(8,128)S(1)}, u32[]{:S(2)}, u32[]{:S(2)}) collective-permute-start(f32[16,128]{1,0:T(8,128)S(1)} %get-tuple-element.20), channel_id=1, source_target_pairs={{1,2},{3,4},{5,6},{7,8},{9,10},{11,12},{13,14},{2,1},{4,3},{6,5},{... | collective-permute-start | bytes 24584 | tf_op jit(solution)/shard_map/ppermute | solution.py:410
  21.4 6.7 %collective-permute-start.1 = (f32[64,512]{1,0:T(8,128)S(1)}, f32[64,512]{1,0:T(8,128)S(1)}, u32[]{:S(2)}, u32[]{:S(2)}) collective-permute-start(f32[64,512]{1,0:T(8,128)S(1)} %get-tuple-element.22), channel_id=1, source_target_pairs={{64,128},{192,256},{320,384},{128,64},{256,192},{384,320},{65,129}... | collective-permute-start | bytes 393224 | tf_op jit(solution)/shard_map/ppermute | solution.py:410

commit v11 on v5

--- a/solution.py
+++ b/solution.py
@@ -18,10 +18,10 @@
 
 LOW = 0.6
 HIGH = 10.5
-S1 = 2.0
-S2 = 6.0
+S1 = 3.5
+S2 = 5.5
 S3 = 4.0
-PAIRS = ((0, 0), (0, 1), (0, 2), (1, 1), (1, 2), (2, 2), (2, 3))
+PAIRS = ((0, 0), (0, 1), (1, 1), (1, 2), (2, 2), (2, 3))
 MIXED = ((0, 0), (1, 1), (2, 2), (0, 1), (0, 2), (1, 2))
 
 HALF = 64
@@ -42,17 +42,38 @@
     return pltpu.roll(v, v.shape[dim] - 1, dim)
 
 
-def inside(rows, wide, first_row, own, grid):
-    nx, ny, local_x, local_y = grid
-    row = lax.broadcasted_iota(jnp.int32, (rows, wide), 0) + (lax.axis_index(BAND) * local_x + first_row)
-    lane = lax.broadcasted_iota(jnp.int32, (rows, wide), 1)
-    column = jnp.where(lane < own + HALF, lane, lane - wide) + lax.axis_index(GY) * local_y
-    return (row >= 0) & (row < nx) & (column >= 0) & (column < ny)
+def keeper(halo, x, own):
+    band, column = lax.axis_index(BAND), lax.axis_index(GY)
+    bands, columns = lax.axis_size(BAND), lax.axis_size(GY)
+    top = jnp.where(band > 0, 1.0, 0.0)
+    bottom = jnp.where(band < bands - 1, 1.0, 0.0)
+    lane = lax.broadcasted_iota(jnp.int32, (8, EDGE), 1)
+    edge = jnp.where(
+        lane < HALF, jnp.where(column < columns - 1, 1.0, 0.0), jnp.where(column > 0, 1.0, 0.0)
+    )
+
+    def tiled(rows):
+        return jnp.concatenate([edge] * (rows // 8), axis=0)
+
+    ends = tiled(halo)
+
+    def keep(v):
+        first, last = v[:halo], v[halo + x :]
+        inner_rows = v[halo : halo + x]
+        main = [first[:, :own] * top, inner_rows[:, :own], last[:, :own] * bottom]
+        side = [
+            first[:, own:] * (ends * top),
+            inner_rows[:, own:] * tiled(x),
+            last[:, own:] * (ends * bottom),
+        ]
+        return jnp.concatenate([jnp.concatenate(p, axis=0) for p in (main, side)], axis=1)
+
+    return keep
 
 
 def shifted(v, center, shift, keep):
     beside = (before(v, 0) + after(v, 0)) + (before(v, 1) + after(v, 1))
-    return jnp.where(keep, (center - shift) * v - beside, 0.0)
+    return keep((center - shift) * v - beside)
 
 
 def basis(v0, center, keep):
@@ -62,16 +83,12 @@
 
 
 def hamiltonian(u):
-    ahead_x = after(u, 0) - u
-    back_x = u - before(u, 0)
-    ahead_y = after(u, 1) - u
-    back_y = u - before(u, 1)
-    return 0.5 * (
-        jnp.maximum(back_x, 0.0) ** 2
-        + jnp.minimum(ahead_x, 0.0) ** 2
-        + jnp.maximum(back_y, 0.0) ** 2
-        + jnp.minimum(ahead_y, 0.0) ** 2
-    )
+    total = None
+    for dim in (0, 1):
+        ahead = after(u, dim) - u
+        term = before(jnp.maximum(ahead, 0.0) ** 2, dim) + jnp.minimum(ahead, 0.0) ** 2
+        total = term if total is None else total + term
+    return 0.5 * total
 
 
 def drift(u):
@@ -90,19 +107,22 @@
     flux_x = out_x * m + in_x * after(m, 0)
     flux_y = out_y * m + in_y * after(m, 1)
     div = (flux_x - before(flux_x, 0)) + (flux_y - before(flux_y, 1))
-    return jnp.where(keep, inv_step * m - div, 0.0)
+    return keep(inv_step * m - div)
 
 
 def dot(a, b):
-    return jnp.sum(jnp.sum(a * b, axis=0, keepdims=True), axis=1, keepdims=True)
+    rows, wide = a.shape
+    total = jnp.sum((a * b).reshape(rows // 8, 8, wide), axis=0)
+    total = sum(total[:, k : k + 128] for k in range(128, wide, 128)) + total[:, :128]
+    return jnp.sum(total, axis=1, keepdims=True)
 
 
 def row_of(values):
-    lane = lax.broadcasted_iota(jnp.int32, (1, 128), 1)
-    row = jnp.zeros((1, 128), jnp.float32)
+    lane = lax.broadcasted_iota(jnp.int32, (8, 128), 1)
+    rows = jnp.zeros((8, 128), jnp.float32)
     for place, value in values:
-        row = jnp.where(lane == place, value, row)
-    return row
+        rows = jnp.where(lane == place, value, rows)
+    return jnp.sum(rows, axis=0, keepdims=True)
 
 
 def entry(row, place):
@@ -130,6 +150,7 @@
 
 def coefficients(products):
     g = dict(zip(PAIRS, products))
+    g[0, 2] = g[1, 1] + (S1 - S2) * g[0, 1]
     gram = [[g[0, 0], g[0, 1], g[0, 2]], [None, g[1, 1], g[1, 2]], [None, None, g[2, 2]]]
     energy = [
         [g[0, 1] + S1 * g[0, 0], g[1, 1] + S1 * g[0, 1], g[1, 2] + S1 * g[0, 2]],
@@ -262,7 +283,7 @@
     _, _, x, own = grid
     wide = own + EDGE
     rows = tall_ref.shape[1]
-    keep = inside(rows, wide, -HALO, own, grid)
+    keep = keeper(HALO, x, own)
     odd = odd_index(GY, (rows, EDGE))
     left = jnp.where(odd, near_edge[:rows, :], far_edge[...])
     right = jnp.where(odd, far_edge[...], near_edge[rows:, :])
@@ -276,7 +297,7 @@
     later = extended(TERMINAL)
     center = extended(DIAGONAL) + (inv_step + 4.0)
     rhs = inv_step * later - hamiltonian(later) + coupling * extended(GUESS + 1)
-    vs = basis(jnp.where(keep, rhs, 0.0), center, keep)
+    vs = basis(keep(rhs), center, keep)
     for k in range(3):
         basis_ref[k] = vs[k]
     center_ref[...] = center
@@ -289,7 +310,7 @@
 def second_kernel(grid, parts_ref, last_ref, center_ref, guess_ref, later_ref, basis_ref, inner_center, sums_ref):
     _, _, x, own = grid
     rows, wide = last_ref.shape[1:]
-    keep = inside(rows, wide, -HALO, own, grid)
+    keep = keeper(HALO, x, own)
     row = gathered_products(parts_ref)
     coefs = coefficients([entry(row, k) for k in range(len(PAIRS))])
     later = combined(coefs, [last_ref[k] for k in range(3)])
@@ -297,7 +318,7 @@
     center = center_ref[...]
     inner_center[...] = inner(center)
     rhs = inv_step * later - hamiltonian(later) + coupling * guess_ref[...]
-    vs = basis(jnp.where(keep, rhs, 0.0), center, keep)
+    vs = basis(keep(rhs), center, keep)
     for k in range(3):
         basis_ref[k] = inner(vs[k])
     mine = [middle(v, x, own) for v in vs]
@@ -307,7 +328,7 @@
 def third_kernel(grid, parts_ref, last_ref, center_ref, initial_ref, later_ref, value_ref, images_ref, sums_ref):
     _, _, x, own = grid
     rows, wide = last_ref.shape[1:]
-    keep = inside(rows, wide, -INNER, own, grid)
+    keep = keeper(INNER, x, own)
     row = gathered_products(parts_ref)
     coefs = coefficients([entry(row, k) for k in range(len(PAIRS))])
     value = combined(coefs, [last_ref[k] for k in range(3)])

time: 99.8 us -> 99.1 us (level)
  no operation moved by 1% of the time
where the time goes in v11:
time: 99.1 us; the launch traced here: 98.8 us
  blocking collectives  83.2 us (84%)
  starting transfers between devices  8.03 us (8%)
  Pallas kernels  6.74 us (7%)
    all_to_all x3, blocking collectives, everywhere(): lax.all_to_all(copies, axes, split_axis=0, concat_axis=0, tiled=True)  62.1 us
    all_gather x1, blocking collectives, shards(): whole = lax.all_gather(fields, PART)  11.3 us
    all_gather x2, blocking collectives, swapped(): lax.all_gather(near, axis[-1], tiled=True)  9.79 us
    ppermute x2, starting transfers between devices, swapped(): lax.ppermute(far, axis, pairs + [(b, a) for a, b in pairs])  8.03 us
    pallas_call x6, Pallas kernels, call(): pl.pallas_call(kernel, out_shape=[results(s, jnp.float32) for s in out_sh...  5.82 us
  transfers between devices with their start and end apart: 2, of which 0 were waited for; matrix products, arithmetic and copies ran while one was open for 0% of the time, Pallas kernels for 0%

profile of v11, /device:TPU:1, one launch (start us, length us, event | category | flops | bytes accessed | tf_op | source)
XLA Modules:
  0.0 98.8 jit_solution(5582516442380316634)
XLA Ops:
  0.6 0.9 shard_map.59
  1.6 11.3 %all-gather = f32[20,16,512]{2,1,0:T(8,128)S(1)} all-gather(f32[5,16,512]{2,1,0:T(8,128)S(1)} %shard_map.59), channel_id=2, replica_groups=mesh['band_0'=4,'band_1'=2,'part'=4,'gy_0'=8,'gy_1'=2] {'part'}, dimensions={0}, use_global_device_ids=true | all-gather | bytes 819200 | tf_op jit(solution)/shard_map/all_gather | solution.py:415
  12.9 0.7 collective-permute-start
  13.6 7.9 %all_gather.14.near_ref = f32[112,512]{1,0:T(8,128)S(1)} all-gather(f32[56,512]{1,0:T(8,128)S(1)} %get-tuple-element.20), channel_id=1, replica_groups=mesh['band_0'=4,'band_1'=2,'part'=4,'gy_0'=8,'gy_1'=2] {'band_1'}, dimensions={0}, use_global_device_ids=true | all-gather | bytes 344064 | tf_op jit(solution)/shard_map/all_gather | solution.py:389
  21.5 0.0 collective-permute-done.far_ref
  21.5 0.2 shard_map.61
  21.7 7.4 %collective-permute-start.1 = (f32[96,128]{1,0:T(8,128)S(1)}, f32[96,128]{1,0:T(8,128)S(1)}, u32[]{:S(2)}, u32[]{:S(2)}) collective-permute-start(f32[96,128]{1,0:T(8,128)S(1)} %get-tuple-element.22), channel_id=1, source_target_pairs={{1,2},{3,4},{5,6},{7,8},{9,10},{11,12},{13,14},{2,1},{4,3},{6,5},{... | collective-permute-start | bytes 147464 | tf_op jit(solution)/shard_map/ppermute | solution.py:388
  29.1 1.9 %all_gather.15.near_edge = f32[192,128]{1,0:T(8,128)S(1)} all-gather(f32[96,128]{1,0:T(8,128)S(1)} %get-tuple-element.23), channel_id=1, replica_groups=mesh['band_0'=4,'band_1'=2,'part'=4,'gy_0'=8,'gy_1'=2] {'gy_1'}, dimensions={0}, use_global_device_ids=true | all-gather | bytes 147456 | tf_op jit(solution)/shard_map/all_gather | solution.py:389
  31.0 0.0 collective-permute-done.1.far_edge
  31.0 0.9 shard_map.62
  31.9 28.6 %all_to_all.15 = f32[128,1,128]{2,1,0:T(1,128)S(1)} all-to-all(f32[128,1,128]{2,1,0:T(1,128)S(1)} %broadcast_in_dim.9), channel_id=1, replica_groups=mesh['band_0'=4,'band_1'=2,'part'=4,'gy_0'=8,'gy_1'=2] {'band_0','band_1..., dimensions={0} | all-to-all | bytes 131072 | tf_op jit(solution)/shard_map/all_to_all | solution.py:381
  60.5 1.0 shard_map.63
  61.5 16.8 %all_to_all.16 = f32[128,1,128]{2,1,0:T(1,128)S(1)} all-to-all(f32[128,1,128]{2,1,0:T(1,128)S(1)} %broadcast_in_dim.10), channel_id=1, replica_groups=mesh['band_0'=4,'band_1'=2,'part'=4,'gy_0'=8,'gy_1'=2] {'band_0','band_1..., dimensions={0} | all-to-all | bytes 131072 | tf_op jit(solution)/shard_map/all_to_all | solution.py:381
  78.3 2.8 %shard_map.64 = (f32[64,512]{1,0:T(8,128)S(1)}, f32[9,64,512]{2,1,0:T(8,128)S(1)}, f32[1,128]{1,0:T(1,128)S(1)}) custom-call(f32[128,128]{1,0:T(8,128)S(1)} %bitcast.9, f32[3,80,640]{2,1,0:T(8,128)S(1)} %get-tuple-element.29.last_ref, f32[80,640]{1,0:T(8,128)S(1)} %get-tuple-element.30.center_ref, f32[80,640]{1,0:T(8,128)S(1)} %get-tuple-element.31.initial_ref, ...), custom_call_target="tpu_custom_call" | custom-call | tf_op jit(solution)/shard_map/pallas_call | solution.py:395
  81.1 16.8 %all_to_all.17 = f32[128,1,128]{2,1,0:T(1,128)S(1)} all-to-all(f32[128,1,128]{2,1,0:T(1,128)S(1)} %broadcast_in_dim.11), channel_id=1, replica_groups=mesh['band_0'=4,'band_1'=2,'part'=4,'gy_0'=8,'gy_1'=2] {'band_0','band_1..., dimensions={0} | all-to-all | bytes 131072 | tf_op jit(solution)/shard_map/all_to_all | solution.py:381
  97.9 0.9 shard_map.65
  (4 shorter events, 0.2 us)
Async XLA Ops:
  12.9 8.6 %collective-permute-start = (f32[56,512]{1,0:T(8,128)S(1)}, f32[56,512]{1,0:T(8,128)S(1)}, u32[]{:S(2)}, u32[]{:S(2)}) collective-permute-start(f32[56,512]{1,0:T(8,128)S(1)} %get-tuple-element.19), channel_id=1, source_target_pairs={{64,128},{192,256},{320,384},{128,64},{256,192},{384,320},{65,129}... | collective-permute-start | bytes 344072 | tf_op jit(solution)/shard_map/ppermute | solution.py:388
  21.7 9.2 %collective-permute-start.1 = (f32[96,128]{1,0:T(8,128)S(1)}, f32[96,128]{1,0:T(8,128)S(1)}, u32[]{:S(2)}, u32[]{:S(2)}) collective-permute-start(f32[96,128]{1,0:T(8,128)S(1)} %get-tuple-element.22), channel_id=1, source_target_pairs={{1,2},{3,4},{5,6},{7,8},{9,10},{11,12},{13,14},{2,1},{4,3},{6,5},{... | collective-permute-start | bytes 147464 | tf_op jit(solution)/shard_map/ppermute | solution.py:388

commit v12 on v10

--- a/solution.py
+++ b/solution.py
@@ -406,10 +406,10 @@
 def swapped(far, near, axis):
     peers = lax.axis_size(axis)
     pairs = [(i, i + 1) for i in range(1, peers - 1, 2)]
-    return (
-        lax.ppermute(far, axis, pairs + [(b, a) for a, b in pairs]),
-        lax.all_gather(near, axis[-1], tiled=True),
-    )
+    gathered = lax.all_gather(near, axis[-1], tiled=True)
+    if axis == GY:
+        far, gathered = lax.optimization_barrier((far, gathered))
+    return lax.ppermute(far, axis, pairs + [(b, a) for a, b in pairs]), gathered
 
 
 def call(kernel, out_shape, *args, results=pltpu.VMEM):

time: 99.3 us -> 101 us (1.017)
  starting transfers between devices: 6.05 us -> 2.58 us
  waiting for transfers between devices: 0.01 us -> 3.34 us
  blocking collectives: 85.4 us -> 87.5 us
    all_gather x2, blocking collectives: 9.63 us -> 13.3 us  [swapped(): gathered = lax.all_gather(near, axis[-1], tiled=True)]
    ppermute x2, starting transfers between devices: 6.05 us -> 2.58 us  [swapped(): lax.ppermute(far, axis, pairs + [(b, a) for a, b in pairs])]
    ppermute x2, waiting for transfers between devices: 0.01 us -> 3.34 us  [swapped(): lax.ppermute(far, axis, pairs + [(b, a) for a, b in pairs])]
    all_to_all x3, blocking collectives: 65 us -> 63.9 us  [everywhere(): lax.all_to_all(copies, axes, split_axis=0, concat_axis=0, tiled=True)]
  transfers between devices with their start and end apart: 2 -> 2, of which waited for: 0 -> 1; matrix products, arithmetic and copies ran while one was open for 0% -> 0% of each run, Pallas kernels for 0% -> 0%
where the time goes in v12:
time: 101 us
  blocking collectives  87.5 us (87%)
  Pallas kernels  6.72 us (7%)
  waiting for transfers between devices  3.34 us (3%)
  starting transfers between devices  2.58 us (3%)
    all_to_all x3, blocking collectives, everywhere(): lax.all_to_all(copies, axes, split_axis=0, concat_axis=0, tiled=True)  63.9 us
    all_gather x2, blocking collectives, swapped(): gathered = lax.all_gather(near, axis[-1], tiled=True)  13.3 us
    all_gather x1, blocking collectives, shards(): whole = lax.all_gather(block, PART)  10.3 us
    pallas_call x6, Pallas kernels, call(): pl.pallas_call(kernel, out_shape=[results(s, jnp.float32) for s in out_sh...  5.72 us
    ppermute x2, waiting for transfers between devices, swapped(): lax.ppermute(far, axis, pairs + [(b, a) for a, b in pairs])  3.34 us
    ppermute x2, starting transfers between devices, swapped(): lax.ppermute(far, axis, pairs + [(b, a) for a, b in pairs])  2.58 us
  transfers between devices with their start and end apart: 2, of which 1 were waited for; matrix products, arithmetic and copies ran while one was open for 0% of the time, Pallas kernels for 0%

profile of v12, /device:TPU:1, one launch (start us, length us, event | category | flops | bytes accessed | tf_op | source)
XLA Modules:
  0.0 101.0 jit_solution(17914440201080112812)
XLA Ops:
  0.6 1.0 shard_map.59
  1.6 8.3 %all_gather.12.near_edge = f32[32,128]{1,0:T(8,128)S(1)} all-gather(f32[16,128]{1,0:T(8,128)S(1)} %get-tuple-element.23), channel_id=1, replica_groups=mesh['band_0'=4,'band_1'=2,'part'=4,'gy_0'=8,'gy_1'=2] {'gy_1'}, dimensions={0}, use_global_device_ids=true | all-gather | bytes 24576 | tf_op jit(solution)/shard_map/all_gather | solution.py:409
  10.0 1.9 %collective-permute-start = (f32[16,128]{1,0:T(8,128)S(1)}, f32[16,128]{1,0:T(8,128)S(1)}, u32[]{:S(2)}, u32[]{:S(2)}) collective-permute-start(f32[16,128]{1,0:T(8,128)S(1)} %get-tuple-element.24), channel_id=1, source_target_pairs={{1,2},{3,4},{5,6},{7,8},{9,10},{11,12},{13,14},{2,1},{4,3},{6,5},{... | collective-permute-start | bytes 24584 | tf_op jit(solution)/shard_map/ppermute | solution.py:412
  11.9 3.3 %collective-permute-done.far_edge = f32[16,128]{1,0:T(8,128)S(1)} collective-permute-done((f32[16,128]{1,0:T(8,128)S(1)}, f32[16,128]{1,0:T(8,128)S(1)}, u32[]{:S(2)}, u32[]{:S(2)}) %collective-permute-start) | collective-permute-done | bytes 8224 | tf_op jit(solution)/shard_map/ppermute | solution.py:412
  15.2 10.3 %all-gather = f32[352,512]{1,0:T(8,128)S(1)} all-gather(f32[88,512]{1,0:T(8,128)S(1)} %shard_map.60), channel_id=2, replica_groups=mesh['band_0'=4,'band_1'=2,'part'=4,'gy_0'=8,'gy_1'=2] {'part'}, dimensions={0}, use_global_device_ids=true | all-gather | bytes 901120 | tf_op jit(solution)/shard_map/all_gather | solution.py:438
  25.6 0.7 collective-permute-start.1
  26.2 5.0 %all_gather.15.near_ref = f32[128,512]{1,0:T(8,128)S(1)} all-gather(f32[64,512]{1,0:T(8,128)S(1)} %get-tuple-element.27), channel_id=1, replica_groups=mesh['band_0'=4,'band_1'=2,'part'=4,'gy_0'=8,'gy_1'=2] {'band_1'}, dimensions={0}, use_global_device_ids=true | all-gather | bytes 393216 | tf_op jit(solution)/shard_map/all_gather | solution.py:409
  31.3 0.0 collective-permute-done.1.far_ref
  31.3 1.0 shard_map.62
  32.3 30.4 %all_to_all.15 = f32[128,1,128]{2,1,0:T(1,128)S(1)} all-to-all(f32[128,1,128]{2,1,0:T(1,128)S(1)} %broadcast_in_dim.9), channel_id=1, replica_groups=mesh['band_0'=4,'band_1'=2,'part'=4,'gy_0'=8,'gy_1'=2] {'band_0','band_1..., dimensions={0} | all-to-all | bytes 131072 | tf_op jit(solution)/shard_map/all_to_all | solution.py:403
  62.7 1.0 shard_map.63
  63.7 16.8 %all_to_all.16 = f32[128,1,128]{2,1,0:T(1,128)S(1)} all-to-all(f32[128,1,128]{2,1,0:T(1,128)S(1)} %broadcast_in_dim.10), channel_id=1, replica_groups=mesh['band_0'=4,'band_1'=2,'part'=4,'gy_0'=8,'gy_1'=2] {'band_0','band_1..., dimensions={0} | all-to-all | bytes 131072 | tf_op jit(solution)/shard_map/all_to_all | solution.py:403
  80.4 2.8 %shard_map.64 = (f32[64,512]{1,0:T(8,128)S(1)}, f32[9,64,512]{2,1,0:T(8,128)S(1)}, f32[1,128]{1,0:T(1,128)S(1)}) custom-call(f32[128,128]{1,0:T(8,128)S(1)} %bitcast.9, f32[3,80,640]{2,1,0:T(8,128)S(1)} %get-tuple-element.33.last_ref, f32[80,640]{1,0:T(8,128)S(1)} %get-tuple-element.34.center_ref, f32[80,640]{1,0:T(8,128)S(1)} %get-tuple-element.35.initial_ref, ...), custom_call_target="tpu_custom_call" | custom-call | tf_op jit(solution)/shard_map/pallas_call | solution.py:417
  83.3 16.8 %all_to_all.17 = f32[128,1,128]{2,1,0:T(1,128)S(1)} all-to-all(f32[128,1,128]{2,1,0:T(1,128)S(1)} %broadcast_in_dim.11), channel_id=1, replica_groups=mesh['band_0'=4,'band_1'=2,'part'=4,'gy_0'=8,'gy_1'=2] {'band_0','band_1..., dimensions={0} | all-to-all | bytes 131072 | tf_op jit(solution)/shard_map/all_to_all | solution.py:403
  100.1 0.9 shard_map.65
  (5 shorter events, 0.2 us)
Async XLA Ops:
  10.0 5.3 %collective-permute-start = (f32[16,128]{1,0:T(8,128)S(1)}, f32[16,128]{1,0:T(8,128)S(1)}, u32[]{:S(2)}, u32[]{:S(2)}) collective-permute-start(f32[16,128]{1,0:T(8,128)S(1)} %get-tuple-element.24), channel_id=1, source_target_pairs={{1,2},{3,4},{5,6},{7,8},{9,10},{11,12},{13,14},{2,1},{4,3},{6,5},{... | collective-permute-start | bytes 24584 | tf_op jit(solution)/shard_map/ppermute | solution.py:412
  25.6 5.7 %collective-permute-start.1 = (f32[64,512]{1,0:T(8,128)S(1)}, f32[64,512]{1,0:T(8,128)S(1)}, u32[]{:S(2)}, u32[]{:S(2)}) collective-permute-start(f32[64,512]{1,0:T(8,128)S(1)} %get-tuple-element.26), channel_id=1, source_target_pairs={{64,128},{192,256},{320,384},{128,64},{256,192},{384,320},{65,129}... | collective-permute-start | bytes 393224 | tf_op jit(solution)/shard_map/ppermute | solution.py:412

commit v13 on v10

--- a/solution.py
+++ b/solution.py
@@ -18,8 +18,8 @@
 
 LOW = 0.6
 HIGH = 10.5
-S1 = 3.5
-S2 = 5.5
+S1 = 2.0
+S2 = 6.0
 S3 = 4.0
 PAIRS = ((0, 0), (0, 1), (1, 1), (1, 2), (2, 2), (2, 3))
 MIXED = ((0, 0), (1, 1), (2, 2), (0, 1), (0, 2), (1, 2))

time: 99.3 us -> 99.3 us (level)
  no operation moved by 1% of the time
where the time goes in v13:
time: 99.3 us; the launch traced here: 99 us
  blocking collectives  85.4 us (86%)
  Pallas kernels  6.72 us (7%)
  starting transfers between devices  6.05 us (6%)
    all_to_all x3, blocking collectives, everywhere(): lax.all_to_all(copies, axes, split_axis=0, concat_axis=0, tiled=True)  65 us
    all_gather x1, blocking collectives, shards(): whole = lax.all_gather(block, PART)  10.7 us
    all_gather x2, blocking collectives, swapped(): lax.all_gather(near, axis[-1], tiled=True)  9.63 us
    ppermute x2, starting transfers between devices, swapped(): lax.ppermute(far, axis, pairs + [(b, a) for a, b in pairs])  6.05 us
    pallas_call x6, Pallas kernels, call(): pl.pallas_call(kernel, out_shape=[results(s, jnp.float32) for s in out_sh...  5.72 us
  transfers between devices with their start and end apart: 2, of which 0 were waited for; matrix products, arithmetic and copies ran while one was open for 0% of the time, Pallas kernels for 0%

profile of v13, /device:TPU:1, one launch (start us, length us, event | category | flops | bytes accessed | tf_op | source)
XLA Modules:
  0.0 99.0 jit_solution(10513575786598153333)
XLA Ops:
  0.6 1.0 %shard_map.59 = (f32[5,16,512]{2,1,0:T(8,128)S(1)}, f32[16,128]{1,0:T(8,128)S(1)}, f32[16,128]{1,0:T(8,128)S(1)}) custom-call(f32[16,512]{1,0:T(8,128)} %terminal.1, f32[16,512]{1,0:T(8,128)} %diagonal.1, f32[2,16,512]{2,1,0:T(8,128)} %guess.1, f32[16,512]{1,0:T(8,128)} %initial.1), custom_call_target="tpu_custom_call" | custom-call | tf_op jit(solution)/shard_map/pallas_call | solution.py:430
  1.6 5.4 %collective-permute-start = (f32[16,128]{1,0:T(8,128)S(1)}, f32[16,128]{1,0:T(8,128)S(1)}, u32[]{:S(2)}, u32[]{:S(2)}) collective-permute-start(f32[16,128]{1,0:T(8,128)S(1)} %get-tuple-element.20), channel_id=1, source_target_pairs={{1,2},{3,4},{5,6},{7,8},{9,10},{11,12},{13,14},{2,1},{4,3},{6,5},{... | collective-permute-start | bytes 24584 | tf_op jit(solution)/shard_map/ppermute | solution.py:410
  7.0 3.6 %all_gather.12.near_edge = f32[32,128]{1,0:T(8,128)S(1)} all-gather(f32[16,128]{1,0:T(8,128)S(1)} %get-tuple-element.21), channel_id=1, replica_groups=mesh['band_0'=4,'band_1'=2,'part'=4,'gy_0'=8,'gy_1'=2] {'gy_1'}, dimensions={0}, use_global_device_ids=true | all-gather | bytes 24576 | tf_op jit(solution)/shard_map/all_gather | solution.py:411
  10.6 0.0 collective-permute-done.far_edge
  10.6 10.7 %all-gather = f32[352,512]{1,0:T(8,128)S(1)} all-gather(f32[88,512]{1,0:T(8,128)S(1)} %shard_map.60), channel_id=2, replica_groups=mesh['band_0'=4,'band_1'=2,'part'=4,'gy_0'=8,'gy_1'=2] {'part'}, dimensions={0}, use_global_device_ids=true | all-gather | bytes 901120 | tf_op jit(solution)/shard_map/all_gather | solution.py:438
  21.4 0.7 collective-permute-start.1
  22.1 6.0 %all_gather.15.near_ref = f32[128,512]{1,0:T(8,128)S(1)} all-gather(f32[64,512]{1,0:T(8,128)S(1)} %get-tuple-element.23), channel_id=1, replica_groups=mesh['band_0'=4,'band_1'=2,'part'=4,'gy_0'=8,'gy_1'=2] {'band_1'}, dimensions={0}, use_global_device_ids=true | all-gather | bytes 393216 | tf_op jit(solution)/shard_map/all_gather | solution.py:411
  28.1 0.0 collective-permute-done.1.far_ref
  28.1 1.0 shard_map.62
  29.2 31.5 %all_to_all.15 = f32[128,1,128]{2,1,0:T(1,128)S(1)} all-to-all(f32[128,1,128]{2,1,0:T(1,128)S(1)} %broadcast_in_dim.9), channel_id=1, replica_groups=mesh['band_0'=4,'band_1'=2,'part'=4,'gy_0'=8,'gy_1'=2] {'band_0','band_1..., dimensions={0} | all-to-all | bytes 131072 | tf_op jit(solution)/shard_map/all_to_all | solution.py:403
  60.6 1.0 shard_map.63
  61.7 16.8 %all_to_all.16 = f32[128,1,128]{2,1,0:T(1,128)S(1)} all-to-all(f32[128,1,128]{2,1,0:T(1,128)S(1)} %broadcast_in_dim.10), channel_id=1, replica_groups=mesh['band_0'=4,'band_1'=2,'part'=4,'gy_0'=8,'gy_1'=2] {'band_0','band_1..., dimensions={0} | all-to-all | bytes 131072 | tf_op jit(solution)/shard_map/all_to_all | solution.py:403
  78.4 2.8 %shard_map.64 = (f32[64,512]{1,0:T(8,128)S(1)}, f32[9,64,512]{2,1,0:T(8,128)S(1)}, f32[1,128]{1,0:T(1,128)S(1)}) custom-call(f32[128,128]{1,0:T(8,128)S(1)} %bitcast.9, f32[3,80,640]{2,1,0:T(8,128)S(1)} %get-tuple-element.29.last_ref, f32[80,640]{1,0:T(8,128)S(1)} %get-tuple-element.30.center_ref, f32[80,640]{1,0:T(8,128)S(1)} %get-tuple-element.31.initial_ref, ...), custom_call_target="tpu_custom_call" | custom-call | tf_op jit(solution)/shard_map/pallas_call | solution.py:417
  81.3 16.8 %all_to_all.17 = f32[128,1,128]{2,1,0:T(1,128)S(1)} all-to-all(f32[128,1,128]{2,1,0:T(1,128)S(1)} %broadcast_in_dim.11), channel_id=1, replica_groups=mesh['band_0'=4,'band_1'=2,'part'=4,'gy_0'=8,'gy_1'=2] {'band_0','band_1..., dimensions={0} | all-to-all | bytes 131072 | tf_op jit(solution)/shard_map/all_to_all | solution.py:403
  98.1 0.9 shard_map.65
  (5 shorter events, 0.2 us)
Async XLA Ops:
  1.6 9.0 %collective-permute-start = (f32[16,128]{1,0:T(8,128)S(1)}, f32[16,128]{1,0:T(8,128)S(1)}, u32[]{:S(2)}, u32[]{:S(2)}) collective-permute-start(f32[16,128]{1,0:T(8,128)S(1)} %get-tuple-element.20), channel_id=1, source_target_pairs={{1,2},{3,4},{5,6},{7,8},{9,10},{11,12},{13,14},{2,1},{4,3},{6,5},{... | collective-permute-start | bytes 24584 | tf_op jit(solution)/shard_map/ppermute | solution.py:410
  21.4 6.7 %collective-permute-start.1 = (f32[64,512]{1,0:T(8,128)S(1)}, f32[64,512]{1,0:T(8,128)S(1)}, u32[]{:S(2)}, u32[]{:S(2)}) collective-permute-start(f32[64,512]{1,0:T(8,128)S(1)} %get-tuple-element.22), channel_id=1, source_target_pairs={{64,128},{192,256},{320,384},{128,64},{256,192},{384,320},{65,129}... | collective-permute-start | bytes 393224 | tf_op jit(solution)/shard_map/ppermute | solution.py:410
